TPU v7x, 128 devices: a whole 4x4x4 slice. The times are simulated.
128 devices in a mesh: ty: 16 (over z, x), tx: 8 (over y, core).
Axes of the slice: x: 4, y: 4, z: 4, core: 2. Of those that a mesh axis runs over, the one named last changes fastest.
Arguments:
- fields: bfloat16 [2, 48, 128, 8192], P(None, None, 'ty', 'tx'), may hold values from -6 to 6
- kernel_one: bfloat16 [3, 3, 48, 32], replicated, may hold values from -0.3125 to 0.3125
- bias_one: float32 [32], replicated, may hold values from -1.5 to 1.5
- kernel_two: bfloat16 [3, 3, 32, 64], replicated, may hold values from -0.75 to 0.75
- bias_two: float32 [64], replicated, may hold values from -1.5 to 1.5
- kernel_three: bfloat16 [3, 3, 64, 128], replicated, may hold values from -0.5 to 0.5
- bias_three: float32 [128], replicated, may hold values from -1.5 to 1.5
- kernel_coarse: bfloat16 [3, 3, 128, 256], replicated, may hold values from -0.375 to 0.375
- bias_coarse: float32 [256], replicated, may hold values from -1.5 to 1.5
- decode_three: bfloat16 [3, 3, 384, 128], replicated, may hold values from -0.15625 to 0.15625
- offset_three: float32 [128], replicated, may hold values from -1.5 to 1.5
- decode_two: bfloat16 [3, 3, 192, 64], replicated, may hold values from -0.21875 to 0.21875
- offset_two: float32 [64], replicated, may hold values from -1.5 to 1.5
- decode_one: bfloat16 [3, 3, 96, 32], replicated, may hold values from -0.3125 to 0.3125
- offset_one: float32 [32], replicated, may hold values from -1.5 to 1.5
- head_kernel: bfloat16 [32, 48], replicated, may hold values from -1 to 1
- head_offset: float32 [48], replicated, may hold values from -3 to 3
Outputs:
- corrected: float32 [2, 48, 128, 8192], P(None, None, 'ty', 'tx')
All inputs are finite; a program needn't handle non-finite values.
Results may differ from a plain program's by a relative error of at most 0.009.
Values may be sent and summed in bfloat16 or wider, within the bound.
No kernel may reach another device: no remote copies, remote signals or barrier semaphores. Data moves between devices by JAX's collectives and lax.ppermute only.
A program may use at most 128 MiB of HBM per device.

v0:
```python
import jax
import jax.numpy as jnp
from jax import lax
from jax.sharding import PartitionSpec as P


def extended(value, sides, width):
    for axis, dim in sides:
        size, length = (lax.axis_size(axis), value.shape[dim])
        up = [(i, (i + 1) % size) for i in range(size - 1)]
        down = [(j, i) for i, j in up]
        last = lax.slice_in_dim(value, length - width, length, axis=dim)
        first = lax.slice_in_dim(value, 0, width, axis=dim)
        before = lax.ppermute(last, axis, up)
        after = lax.ppermute(first, axis, down)
        value = jnp.concatenate([before, value, after], axis=dim)
    return value


def convolve_valid(padded, kernel, offset):
    result = lax.conv_general_dilated(
        padded,
        kernel,
        (1, 1),
        "VALID",
        dimension_numbers=("NCHW", "HWIO", "NCHW"),
        preferred_element_type=jnp.float32,
    )
    return jax.nn.silu(result + offset[None, :, None, None]).astype(jnp.bfloat16)


def tile_conv(tensor, kernel, offset):
    padded = extended(tensor, (("ty", 2), ("tx", 3)), 1)
    return convolve_valid(padded, kernel, offset)


def joined_conv(tensor, kernel, offset):
    padded = extended(tensor, (("ty", 2), ("tx", 3)), 1)
    return convolve_valid(padded, kernel, offset)


def average_pool(tensor):
    shape = tensor.shape
    blocks = tensor.astype(jnp.float32).reshape(
        shape[0], shape[1], shape[2] // 2, 2, shape[3] // 2, 2
    )
    return jnp.mean(blocks, axis=(3, 5)).astype(jnp.bfloat16)


def upsample(tensor):
    return jnp.repeat(jnp.repeat(tensor, 2, axis=2), 2, axis=3)


def body(
    fields,
    kernel_one,
    bias_one,
    kernel_two,
    bias_two,
    kernel_three,
    bias_three,
    kernel_coarse,
    bias_coarse,
    decode_three,
    offset_three,
    decode_two,
    offset_two,
    decode_one,
    offset_one,
    head_kernel,
    head_offset,
):
    skip_one = tile_conv(fields, kernel_one, bias_one)
    skip_two = tile_conv(average_pool(skip_one), kernel_two, bias_two)
    skip_three = tile_conv(average_pool(skip_two), kernel_three, bias_three)
    coarse_in = average_pool(skip_three)
    padded = extended(coarse_in, (("ty", 2), ("tx", 3)), 1)
    coarse = convolve_valid(padded, kernel_coarse, bias_coarse)
    back_three = joined_conv(
        jnp.concatenate([upsample(coarse), skip_three], axis=1), decode_three, offset_three
    )
    back_two = joined_conv(
        jnp.concatenate([upsample(back_three), skip_two], axis=1), decode_two, offset_two
    )
    back_one = joined_conv(
        jnp.concatenate([upsample(back_two), skip_one], axis=1), decode_one, offset_one
    )
    projected = jnp.einsum(
        "bchw,cv->bvhw", back_one, head_kernel, preferred_element_type=jnp.float32
    )
    return fields.astype(jnp.float32) + head_offset[None, :, None, None] + projected


def solution(mesh):
    return jax.shard_map(
        body,
        mesh=mesh,
        in_specs=(
            P(None, None, "ty", "tx"),
            P(),
            P(),
            P(),
            P(),
            P(),
            P(),
            P(),
            P(),
            P(),
            P(),
            P(),
            P(),
            P(),
            P(),
            P(),
            P(),
        ),
        out_specs=P(None, None, "ty", "tx"),
        check_vma=False,
    )
```

profile of v0, /device:TPU:97, one launch (start us, length us, event | category | flops | bytes accessed | tf_op | source)
XLA Modules:
  0.0 418.0 jit_solution(6570746729210643769)
XLA Ops:
  10.9 5.7 %collective-permute-done = bf16[2,48,1,1024]{3,1,2,0:T(8,128)(2,1)S(1)} collective-permute-done((bf16[2,48,1,1024]{3,1,2,0:T(8,128)(2,1)S(1)}, bf16[2,48,1,1024]{3,1,2,0:T(8,128)(2,1)S(1)}, u32[]{:S(2)}, u32[]{:S(2)}) %collective-permute-start) | collective-permute-done | bytes 196640 | tf_op jit(solution)/shard_map/ppermute | solution.py:14
  20.9 4.9 %collective-permute-start.2 = (bf16[2,48,10,1]{3,2,1,0:T(8,128)(2,1)S(1)}, bf16[2,48,10,1]{3,2,1,0:T(8,128)(2,1)S(1)}, u32[]{:S(2)}, u32[]{:S(2)}) collective-permute-start(bf16[2,48,10,1]{3,2,1,0:T(8,128)(2,1)S(1)} %get-tuple-element.12), channel_id=1, source_target_pairs={{0,1},{1,2},{2,3},{3,4},{4,5},{5,6},{6,7},{8,9},{9,10},{10,11},{11... | collective-permute-start | bytes 5768 | tf_op jit(solution)/shard_map/ppermute | solution.py:14
  30.5 4.4 %collective-permute-done.3 = bf16[2,48,10,1]{3,2,1,0:T(8,128)(2,1)S(1)} collective-permute-done((bf16[2,48,10,1]{3,2,1,0:T(8,128)(2,1)S(1)}, bf16[2,48,10,1]{3,2,1,0:T(8,128)(2,1)S(1)}, u32[]{:S(2)}, u32[]{:S(2)}) %collective-permute-start.3) | collective-permute-done | bytes 1952 | tf_op jit(solution)/shard_map/ppermute | solution.py:15
  34.9 7.5 %concatenate.52 = bf16[2,48,10,1026]{3,2,1,0:T(8,128)(2,1)} concatenate(bf16[2,48,10,1]{3,2,1,0:T(8,128)(2,1)S(1)} %collective-permute-done.2, bf16[2,48,10,1024]{3,2,1,0:T(8,128)(2,1)} %copy-done.6, bf16[2,48,10,1]{3,2,1,0:T(8,128)(2,1)S(1)} %collective-permute-done.3), dimensions={3} | concatenate | bytes 3939840 | tf_op jit(solution)/shard_map/concatenate | solution.py:16
  45.0 6.0 %reshape.66 = bf16[48,10,2,8,129]{4,3,0,2,1:T(8,128)(2,1)} reshape(bf16[48,10,2,1032]{3,0,2,1:T(8,128)(2,1)S(1)} %pad.clone) | data formatting | bytes 3962880 | tf_op jit(solution)/shard_map/conv_general_dilated | solution.py:21
  56.5 10.9 %copy.168 = bf16[48,10,2,8,131]{0,3,2,4,1:T(8,128)(2,1)} copy(bf16[48,10,2,8,131]{4,3,0,2,1:T(8,128)(2,1)} %fusion.8) | data formatting | bytes 4024320 | tf_op jit(solution)/shard_map/conv_general_dilated | solution.py:21
  67.4 13.2 %fusion.5 = f32[8,16,129,32]{3,1,2,0:T(8,128)} fusion(bf16[3,3,48,32]{2,3,1,0:T(8,128)(2,1)S(1)} %copy-done.23, bf16[48,10,2,8,131]{0,3,2,4,1:T(8,128)(2,1)} %copy.168), kind=kOutput, calls=%fused_computation.9 | convolution fusion | flops 456523776 | bytes 4153344 | tf_op jit(solution)/shard_map/conv_general_dilated | solution.py:21
  80.5 9.1 %copy.169 = f32[8,16,129,32]{2,3,1,0:T(8,128)} copy(f32[8,16,129,32]{3,1,2,0:T(8,128)} %fusion.5) | data formatting | bytes 4227072 | tf_op jit(solution)/shard_map/conv_general_dilated | solution.py:21
  94.7 4.3 %reshape.70 = bf16[8,2,1032,32]{2,1,3,0:T(2,128)(2,1)} reshape(bf16[8,16,129,32]{2,1,3,0:T(8,128)(2,1)S(1)} %copy.170) | data formatting | bytes 2113536 | tf_op jit(solution)/shard_map/convert_element_type | solution.py:29
  102.7 4.7 %copy.172 = f32[2,32,8,1024]{1,3,2,0:T(8,128)} copy(f32[2,32,8,1024]{3,2,1,0:T(8,128)S(1)} %fusion.30) | data formatting | bytes 4194304 | tf_op jit(solution)/shard_map/reshape | solution.py:44
  107.3 9.6 %reduce_sum.34 = f32[2,32,4,512]{1,3,2,0:T(8,128)S(1)} reduce(f32[2,32,4,2,512,2]{1,5,4,3,2,0:T(2,128)} %bitcast.130, f32[]{:T(128)} %constant.19.clone.1), dimensions={3,5}, to_apply=%region_0.1 | reduce | flops 393216 | bytes 2621444 | tf_op jit(solution)/shard_map/reduce_sum | solution.py:47
  131.4 4.8 %collective-permute-start.6 = (bf16[2,32,6,1]{3,1,2,0:T(8,128)(2,1)S(1)}, bf16[2,32,6,1]{3,1,2,0:T(8,128)(2,1)S(1)}, u32[]{:S(2)}, u32[]{:S(2)}) collective-permute-start(bf16[2,32,6,1]{3,1,2,0:T(8,128)(2,1)S(1)} %get-tuple-element.25), channel_id=1, source_target_pairs={{0,1},{1,2},{2,3},{3,4},{4,5},{5,6},{6,7},{8,9},{9,10},{10,11},{11... | collective-permute-start | bytes 2312 | tf_op jit(solution)/shard_map/ppermute | solution.py:14
  171.5 6.4 %collective-permute-start.10 = (bf16[2,64,4,1]{1,3,2,0:T(2,128)(2,1)S(1)}, bf16[2,64,4,1]{1,3,2,0:T(2,128)(2,1)S(1)}, u32[]{:S(2)}, u32[]{:S(2)}) collective-permute-start(bf16[2,64,4,1]{1,3,2,0:T(2,128)(2,1)S(1)} %get-tuple-element.23), channel_id=1, source_target_pairs={{0,1},{1,2},{2,3},{3,4},{4,5},{5,6},{6,7},{8,9},{9,10},{10,11},{11... | collective-permute-start | bytes 3080 | tf_op jit(solution)/shard_map/ppermute | solution.py:14
  192.1 5.3 %collective-permute-start.14 = (bf16[2,128,3,1]{1,3,0,2:T(2,128)(2,1)S(1)}, bf16[2,128,3,1]{1,3,0,2:T(2,128)(2,1)S(1)}, u32[]{:S(2)}, u32[]{:S(2)}) collective-permute-start(bf16[2,128,3,1]{1,3,0,2:T(2,128)(2,1)S(1)} %get-tuple-element.29), channel_id=1, source_target_pairs={{0,1},{1,2},{2,3},{3,4},{4,5},{5,6},{6,7},{8,9},{9,10},{10,11},{11... | collective-permute-start | bytes 4616 | tf_op jit(solution)/shard_map/ppermute | solution.py:14
  207.1 5.3 %collective-permute-done.17 = bf16[2,384,1,256]{1,0,3,2:T(2,128)(2,1)S(1)} collective-permute-done((bf16[2,384,1,256]{1,0,3,2:T(2,128)(2,1)S(1)}, bf16[2,384,1,256]{1,0,3,2:T(2,128)(2,1)S(1)}, u32[]{:S(2)}, u32[]{:S(2)}) %collective-permute-start.17) | collective-permute-done | bytes 393248 | tf_op jit(solution)/shard_map/ppermute | solution.py:15
  218.2 6.6 %collective-permute-start.18 = (bf16[2,384,4,1]{1,0,3,2:T(2,128)(2,1)S(1)}, bf16[2,384,4,1]{1,0,3,2:T(2,128)(2,1)S(1)}, u32[]{:S(2)}, u32[]{:S(2)}) collective-permute-start(bf16[2,384,4,1]{1,0,3,2:T(2,128)(2,1)S(1)} %get-tuple-element.15), channel_id=1, source_target_pairs={{0,1},{1,2},{2,3},{3,4},{4,5},{5,6},{6,7},{8,9},{9,10},{10,11},{11... | collective-permute-start | bytes 18440 | tf_op jit(solution)/shard_map/ppermute | solution.py:14
  225.5 4.6 %maximum_bitcast_fusion.1 = bf16[384,4,2,258]{0,2,3,1:T(2,128)(2,1)S(1)} fusion(bf16[2,384,4,1]{1,0,3,2:T(2,128)(2,1)S(1)} %collective-permute-done.19, bf16[2,384,1,256]{1,0,3,2:T(2,128)(2,1)} %copy-done.11, bf16[2,128,2,256]{1,0,3,2:T(2,128)(2,1)S(1)} %copy.190, bf16[2,256,2,256]{1,0,3,2:T(2,128)(2,1)S(1)} %broadcast_in_dim.30, ...), kind=kLoop, calls=%fused_computation.38 | loop fusion | flops 9510912 | bytes 3170304 | tf_op jit(solution)/shard_map/concatenate | solution.py:16
  241.7 7.0 %collective-permute-done.21 = bf16[2,192,1,512]{1,3,2,0:T(8,128)(2,1)S(1)} collective-permute-done((bf16[2,192,1,512]{1,3,2,0:T(8,128)(2,1)S(1)}, bf16[2,192,1,512]{1,3,2,0:T(8,128)(2,1)S(1)}, u32[]{:S(2)}, u32[]{:S(2)}) %collective-permute-start.21) | collective-permute-done | bytes 393248 | tf_op jit(solution)/shard_map/ppermute | solution.py:15
  254.4 7.6 %collective-permute-start.22 = (bf16[2,192,6,1]{1,3,2,0:T(2,128)(2,1)S(1)}, bf16[2,192,6,1]{1,3,2,0:T(2,128)(2,1)S(1)}, u32[]{:S(2)}, u32[]{:S(2)}) collective-permute-start(bf16[2,192,6,1]{1,3,2,0:T(2,128)(2,1)S(1)} %get-tuple-element.9), channel_id=1, source_target_pairs={{0,1},{1,2},{2,3},{3,4},{4,5},{5,6},{6,7},{8,9},{9,10},{10,11},{11... | collective-permute-start | bytes 13832 | tf_op jit(solution)/shard_map/ppermute | solution.py:14
  262.0 7.2 %copy.221 = bf16[8,2,1024,32]{3,0,2,1:T(8,128)(2,1)} copy(bf16[8,2,1024,32]{2,1,3,0:T(2,128)(2,1)} %copy-done.9) | data formatting | bytes 2097152 | tf_op jit(solution)/shard_map/convert_element_type | solution.py:29
  279.7 6.6 %fusion.10 = f32[4,16,65,64]{3,1,2,0:T(8,128)} fusion(bf16[3,3,192,64]{2,3,1,0:T(8,128)(2,1)S(1)} %copy-done.21, bf16[192,6,2,8,67]{0,2,4,3,1:T(2,128)(2,1)S(1)} %fusion.9), kind=kOutput, calls=%fused_computation.17 | convolution fusion | flops 920125440 | bytes 3756032 | tf_op jit(solution)/shard_map/conv_general_dilated | solution.py:21
  298.8 4.8 %fusion.28 = (bf16[2,96,1,1024]{1,2,3,0:T(2,128)(2,1)S(1)}, bf16[2,96,1,1024]{1,2,3,0:T(2,128)(2,1)S(1)}) fusion(bf16[2,64,8,1024]{1,2,3,0:T(8,128)(2,1)S(1)} %bitcast.128, bf16[2,32,8,1024]{1,2,3,0:T(8,128)(2,1)S(1)} %bitcast.127), kind=kLoop, calls=%fused_computation.47 | loop fusion | flops 1572864 | bytes 3932160 | tf_op jit(solution)/shard_map/concatenate | solution.py:86
  310.3 6.0 %pad_maximum_fusion.1 = bf16[2,96,8,1024]{1,2,3,0:T(8,128)(2,1)} fusion(bf16[2,32,8,1024]{1,2,3,0:T(8,128)(2,1)} %bitcast.126, bf16[2,64,8,1024]{1,2,3,0:T(8,128)(2,1)} %bitcast.129), kind=kLoop, calls=%fused_computation.22 | loop fusion | flops 6291456 | bytes 6291456 | tf_op jit(solution)/shard_map/concatenate | solution.py:86
  316.3 6.4 %copy.203 = bf16[2,96,8,1024]{3,1,2,0:T(8,128)(2,1)} copy(bf16[2,96,8,1024]{1,2,3,0:T(8,128)(2,1)} %pad_maximum_fusion.1) | data formatting | bytes 6291456 | tf_op jit(solution)/shard_map/concatenate | solution.py:86
  335.8 4.4 %collective-permute-done.27 = bf16[2,96,10,1]{3,1,2,0:T(8,128)(2,1)S(1)} collective-permute-done((bf16[2,96,10,1]{3,1,2,0:T(8,128)(2,1)S(1)}, bf16[2,96,10,1]{3,1,2,0:T(8,128)(2,1)S(1)}, u32[]{:S(2)}, u32[]{:S(2)}) %collective-permute-start.27) | collective-permute-done | bytes 3872 | tf_op jit(solution)/shard_map/ppermute | solution.py:15
  340.2 9.1 %concatenate.67 = bf16[2,96,10,1026]{3,1,2,0:T(8,128)(2,1)} concatenate(bf16[2,96,10,1]{3,1,2,0:T(8,128)(2,1)S(1)} %collective-permute-done.26, bf16[2,96,10,1024]{3,1,2,0:T(8,128)(2,1)} %copy-done.5, bf16[2,96,10,1]{3,1,2,0:T(8,128)(2,1)S(1)} %collective-permute-done.27), dimensions={3} | concatenate | bytes 7879680 | tf_op jit(solution)/shard_map/concatenate | solution.py:16
  349.3 8.1 %copy.219 = bf16[96,10,2,1026]{0,3,2,1:T(8,128)(2,1)} copy(bf16[96,10,2,1026]{3,0,1,2:T(8,128)(2,1)} %bitcast.131) | data formatting | bytes 7879680
  357.4 5.9 %pad.12.clone = bf16[96,10,2,1032]{0,3,2,1:T(8,128)(2,1)} pad(bf16[96,10,2,1026]{0,3,2,1:T(8,128)(2,1)} %copy.219, bf16[]{:T(256)} %constant.22), padding=0_0x0_0x0_0x0_6 | pad | bytes 7902722 | tf_op jit(solution)/shard_map/concatenate | solution.py:16
  363.4 8.4 %reshape.108 = bf16[96,10,2,8,129]{0,4,3,2,1:T(8,128)(2,1)} reshape(bf16[96,10,2,1032]{0,3,2,1:T(8,128)(2,1)} %pad.12.clone) | data formatting | bytes 7925760 | tf_op jit(solution)/shard_map/conv_general_dilated | solution.py:21
  377.0 12.2 %fusion.3 = f32[8,16,129,32]{3,1,2,0:T(8,128)} fusion(bf16[3,3,96,32]{2,3,1,0:T(8,128)(2,1)S(1)} %copy-done.25, bf16[96,10,2,8,131]{0,4,3,2,1:T(8,128)(2,1)S(1)} %fusion.2), kind=kOutput, calls=%fused_computation.7 | convolution fusion | flops 913047552 | bytes 6193152 | tf_op jit(solution)/shard_map/conv_general_dilated | solution.py:21
  389.2 9.3 %copy.206 = f32[8,16,129,32]{2,3,1,0:T(8,128)} copy(f32[8,16,129,32]{3,1,2,0:T(8,128)} %fusion.3) | data formatting | bytes 4227072 | tf_op jit(solution)/shard_map/conv_general_dilated | solution.py:21
  404.9 5.7 %reshape.112 = bf16[8,2,1032,32]{2,1,3,0:T(2,128)(2,1)} reshape(bf16[8,16,129,32]{2,1,3,0:T(8,128)(2,1)} %copy.207) | data formatting | bytes 2113536 | tf_op jit(solution)/shard_map/convert_element_type | solution.py:29
  (212 shorter events, 194.3 us)
Async XLA Ops:
  0.0 233.0 %copy-start = (bf16[3,3,384,128]{3,2,1,0:T(8,128)(2,1)S(1)}, bf16[3,3,384,128]{3,2,1,0:T(8,128)(2,1)}, u32[]{:S(2)}) copy-start(bf16[3,3,384,128]{3,2,1,0:T(8,128)(2,1)} %param.26) | copy-start | bytes 2654212
  2.8 7.8 %collective-permute-start.1 = (bf16[2,48,1,1024]{3,1,2,0:T(8,128)(2,1)S(1)}, bf16[2,48,1,1024]{3,1,2,0:T(8,128)(2,1)S(1)}, u32[]{:S(2)}, u32[]{:S(2)}) collective-permute-start(bf16[2,48,1,1024]{3,1,2,0:T(8,128)(2,1)S(1)} %copy.259), channel_id=1, source_target_pairs={{8,0},{16,8},{24,16},{32,24},{40,32},{48,40},{56,48},{64,56},{72,6... | collective-permute-start | bytes 589832 | tf_op jit(solution)/shard_map/ppermute | solution.py:15
  7.1 9.5 %collective-permute-start = (bf16[2,48,1,1024]{3,1,2,0:T(8,128)(2,1)S(1)}, bf16[2,48,1,1024]{3,1,2,0:T(8,128)(2,1)S(1)}, u32[]{:S(2)}, u32[]{:S(2)}) collective-permute-start(bf16[2,48,1,1024]{3,1,2,0:T(8,128)(2,1)S(1)} %copy.260), channel_id=1, source_target_pairs={{0,8},{8,16},{16,24},{24,32},{32,40},{40,48},{48,56},{56,64},{64,7... | collective-permute-start | bytes 589832 | tf_op jit(solution)/shard_map/ppermute | solution.py:14
  20.9 9.6 %collective-permute-start.2 = (bf16[2,48,10,1]{3,2,1,0:T(8,128)(2,1)S(1)}, bf16[2,48,10,1]{3,2,1,0:T(8,128)(2,1)S(1)}, u32[]{:S(2)}, u32[]{:S(2)}) collective-permute-start(bf16[2,48,10,1]{3,2,1,0:T(8,128)(2,1)S(1)} %get-tuple-element.12), channel_id=1, source_target_pairs={{0,1},{1,2},{2,3},{3,4},{4,5},{5,6},{6,7},{8,9},{9,10},{10,11},{11... | collective-permute-start | bytes 5768 | tf_op jit(solution)/shard_map/ppermute | solution.py:14
  25.8 9.1 %collective-permute-start.3 = (bf16[2,48,10,1]{3,2,1,0:T(8,128)(2,1)S(1)}, bf16[2,48,10,1]{3,2,1,0:T(8,128)(2,1)S(1)}, u32[]{:S(2)}, u32[]{:S(2)}) collective-permute-start(bf16[2,48,10,1]{3,2,1,0:T(8,128)(2,1)S(1)} %get-tuple-element.11), channel_id=1, source_target_pairs={{1,0},{2,1},{3,2},{4,3},{5,4},{6,5},{7,6},{9,8},{10,9},{11,10},{12... | collective-permute-start | bytes 5768 | tf_op jit(solution)/shard_map/ppermute | solution.py:15
  118.1 7.1 %collective-permute-start.5 = (bf16[2,32,1,512]{1,3,2,0:T(8,128)(2,1)S(1)}, bf16[2,32,1,512]{1,3,2,0:T(8,128)(2,1)S(1)}, u32[]{:S(2)}, u32[]{:S(2)}) collective-permute-start(bf16[2,32,1,512]{1,3,2,0:T(8,128)(2,1)S(1)} %get-tuple-element.20), channel_id=1, source_target_pairs={{8,0},{16,8},{24,16},{32,24},{40,32},{48,40},{56,48},{64,56},{72,6... | collective-permute-start | bytes 196616 | tf_op jit(solution)/shard_map/ppermute | solution.py:15
  120.1 9.2 %collective-permute-start.4 = (bf16[2,32,1,512]{1,3,2,0:T(8,128)(2,1)S(1)}, bf16[2,32,1,512]{1,3,2,0:T(8,128)(2,1)S(1)}, u32[]{:S(2)}, u32[]{:S(2)}) collective-permute-start(bf16[2,32,1,512]{1,3,2,0:T(8,128)(2,1)S(1)} %get-tuple-element.19), channel_id=1, source_target_pairs={{0,8},{8,16},{16,24},{24,32},{32,40},{40,48},{48,56},{56,64},{64,7... | collective-permute-start | bytes 196616 | tf_op jit(solution)/shard_map/ppermute | solution.py:14
  129.5 7.1 %collective-permute-start.7 = (bf16[2,32,6,1]{3,1,2,0:T(8,128)(2,1)S(1)}, bf16[2,32,6,1]{3,1,2,0:T(8,128)(2,1)S(1)}, u32[]{:S(2)}, u32[]{:S(2)}) collective-permute-start(bf16[2,32,6,1]{3,1,2,0:T(8,128)(2,1)S(1)} %get-tuple-element.26), channel_id=1, source_target_pairs={{1,0},{2,1},{3,2},{4,3},{5,4},{6,5},{7,6},{9,8},{10,9},{11,10},{12... | collective-permute-start | bytes 2312 | tf_op jit(solution)/shard_map/ppermute | solution.py:15
  131.4 6.4 %collective-permute-start.6 = (bf16[2,32,6,1]{3,1,2,0:T(8,128)(2,1)S(1)}, bf16[2,32,6,1]{3,1,2,0:T(8,128)(2,1)S(1)}, u32[]{:S(2)}, u32[]{:S(2)}) collective-permute-start(bf16[2,32,6,1]{3,1,2,0:T(8,128)(2,1)S(1)} %get-tuple-element.25), channel_id=1, source_target_pairs={{0,1},{1,2},{2,3},{3,4},{4,5},{5,6},{6,7},{8,9},{9,10},{10,11},{11... | collective-permute-start | bytes 2312 | tf_op jit(solution)/shard_map/ppermute | solution.py:14
  158.6 21.3 %copy-start.22 = (bf16[3,3,64,128]{3,2,1,0:T(8,128)(2,1)S(1)}, bf16[3,3,64,128]{3,2,1,0:T(8,128)(2,1)}, u32[]{:S(2)}) copy-start(bf16[3,3,64,128]{3,2,1,0:T(8,128)(2,1)} %param.22) | copy-start | bytes 442372
  158.6 21.4 %copy-start.27 = (f32[128]{0:T(128)S(1)}, f32[128]{0:T(128)}, u32[]{:S(2)}) copy-start(f32[128]{0:T(128)} %param.23) | copy-start | bytes 1540
  158.6 21.4 %copy-start.29 = (pred[16,33]{0,1:T(8,128)(4,1)S(1)}, pred[16,33]{0,1:T(8,128)(4,1)}, u32[]{:S(2)}) copy-start(pred[16,33]{0,1:T(8,128)(4,1)} %constant.52) | copy-start | bytes 1588
  159.8 6.0 %collective-permute-start.9 = (bf16[2,64,1,256]{1,3,2,0:T(8,128)(2,1)S(1)}, bf16[2,64,1,256]{1,3,2,0:T(8,128)(2,1)S(1)}, u32[]{:S(2)}, u32[]{:S(2)}) collective-permute-start(bf16[2,64,1,256]{1,3,2,0:T(8,128)(2,1)S(1)} %get-tuple-element.28), channel_id=1, source_target_pairs={{8,0},{16,8},{24,16},{32,24},{40,32},{48,40},{56,48},{64,56},{72,6... | collective-permute-start | bytes 196616 | tf_op jit(solution)/shard_map/ppermute | solution.py:15
  161.7 7.8 %collective-permute-start.8 = (bf16[2,64,1,256]{1,3,2,0:T(8,128)(2,1)S(1)}, bf16[2,64,1,256]{1,3,2,0:T(8,128)(2,1)S(1)}, u32[]{:S(2)}, u32[]{:S(2)}) collective-permute-start(bf16[2,64,1,256]{1,3,2,0:T(8,128)(2,1)S(1)} %get-tuple-element.27), channel_id=1, source_target_pairs={{0,8},{8,16},{16,24},{24,32},{32,40},{40,48},{48,56},{56,64},{64,7... | collective-permute-start | bytes 196616 | tf_op jit(solution)/shard_map/ppermute | solution.py:14
  169.5 8.3 %collective-permute-start.11 = (bf16[2,64,4,1]{1,3,2,0:T(2,128)(2,1)S(1)}, bf16[2,64,4,1]{1,3,2,0:T(2,128)(2,1)S(1)}, u32[]{:S(2)}, u32[]{:S(2)}) collective-permute-start(bf16[2,64,4,1]{1,3,2,0:T(2,128)(2,1)S(1)} %get-tuple-element.24), channel_id=1, source_target_pairs={{1,0},{2,1},{3,2},{4,3},{5,4},{6,5},{7,6},{9,8},{10,9},{11,10},{12... | collective-permute-start | bytes 3080 | tf_op jit(solution)/shard_map/ppermute | solution.py:15
  171.5 6.7 %collective-permute-start.10 = (bf16[2,64,4,1]{1,3,2,0:T(2,128)(2,1)S(1)}, bf16[2,64,4,1]{1,3,2,0:T(2,128)(2,1)S(1)}, u32[]{:S(2)}, u32[]{:S(2)}) collective-permute-start(bf16[2,64,4,1]{1,3,2,0:T(2,128)(2,1)S(1)} %get-tuple-element.23), channel_id=1, source_target_pairs={{0,1},{1,2},{2,3},{3,4},{4,5},{5,6},{6,7},{8,9},{9,10},{10,11},{11... | collective-permute-start | bytes 3080 | tf_op jit(solution)/shard_map/ppermute | solution.py:14
  181.2 5.5 %collective-permute-start.13 = (bf16[2,128,1,128]{1,3,0,2:T(8,128)(2,1)S(1)}, bf16[2,128,1,128]{1,3,0,2:T(8,128)(2,1)S(1)}, u32[]{:S(2)}, u32[]{:S(2)}) collective-permute-start(bf16[2,128,1,128]{1,3,0,2:T(8,128)(2,1)S(1)} %fusion.44), channel_id=1, source_target_pairs={{8,0},{16,8},{24,16},{32,24},{40,32},{48,40},{56,48},{64,56},{72,6... | collective-permute-start | bytes 196616 | tf_op jit(solution)/shard_map/ppermute | solution.py:15
  183.1 7.1 %collective-permute-start.12 = (bf16[2,128,1,128]{1,3,0,2:T(8,128)(2,1)S(1)}, bf16[2,128,1,128]{1,3,0,2:T(8,128)(2,1)S(1)}, u32[]{:S(2)}, u32[]{:S(2)}) collective-permute-start(bf16[2,128,1,128]{1,3,0,2:T(8,128)(2,1)S(1)} %fusion.44), channel_id=1, source_target_pairs={{0,8},{8,16},{16,24},{24,32},{32,40},{40,48},{48,56},{56,64},{64,7... | collective-permute-start | bytes 196616 | tf_op jit(solution)/shard_map/ppermute | solution.py:14
  190.2 7.7 %collective-permute-start.15 = (bf16[2,128,3,1]{1,3,0,2:T(2,128)(2,1)S(1)}, bf16[2,128,3,1]{1,3,0,2:T(2,128)(2,1)S(1)}, u32[]{:S(2)}, u32[]{:S(2)}) collective-permute-start(bf16[2,128,3,1]{1,3,0,2:T(2,128)(2,1)S(1)} %get-tuple-element.30), channel_id=1, source_target_pairs={{1,0},{2,1},{3,2},{4,3},{5,4},{6,5},{7,6},{9,8},{10,9},{11,10},{12... | collective-permute-start | bytes 4616 | tf_op jit(solution)/shard_map/ppermute | solution.py:15
  192.1 6.1 %collective-permute-start.14 = (bf16[2,128,3,1]{1,3,0,2:T(2,128)(2,1)S(1)}, bf16[2,128,3,1]{1,3,0,2:T(2,128)(2,1)S(1)}, u32[]{:S(2)}, u32[]{:S(2)}) collective-permute-start(bf16[2,128,3,1]{1,3,0,2:T(2,128)(2,1)S(1)} %get-tuple-element.29), channel_id=1, source_target_pairs={{0,1},{1,2},{2,3},{3,4},{4,5},{5,6},{6,7},{8,9},{9,10},{10,11},{11... | collective-permute-start | bytes 4616 | tf_op jit(solution)/shard_map/ppermute | solution.py:14
  201.8 10.6 %collective-permute-start.17 = (bf16[2,384,1,256]{1,0,3,2:T(2,128)(2,1)S(1)}, bf16[2,384,1,256]{1,0,3,2:T(2,128)(2,1)S(1)}, u32[]{:S(2)}, u32[]{:S(2)}) collective-permute-start(bf16[2,384,1,256]{1,0,3,2:T(2,128)(2,1)S(1)} %get-tuple-element.22), channel_id=1, source_target_pairs={{8,0},{16,8},{24,16},{32,24},{40,32},{48,40},{56,48},{64,56},{72,6... | collective-permute-start | bytes 1179656 | tf_op jit(solution)/shard_map/ppermute | solution.py:15
  203.8 12.5 %collective-permute-start.16 = (bf16[2,384,1,256]{1,0,3,2:T(2,128)(2,1)S(1)}, bf16[2,384,1,256]{1,0,3,2:T(2,128)(2,1)S(1)}, u32[]{:S(2)}, u32[]{:S(2)}) collective-permute-start(bf16[2,384,1,256]{1,0,3,2:T(2,128)(2,1)S(1)} %get-tuple-element.21), channel_id=1, source_target_pairs={{0,8},{8,16},{16,24},{24,32},{32,40},{40,48},{48,56},{56,64},{64,7... | collective-permute-start | bytes 1179656 | tf_op jit(solution)/shard_map/ppermute | solution.py:14
  216.2 9.2 %collective-permute-start.19 = (bf16[2,384,4,1]{1,0,3,2:T(2,128)(2,1)S(1)}, bf16[2,384,4,1]{1,0,3,2:T(2,128)(2,1)S(1)}, u32[]{:S(2)}, u32[]{:S(2)}) collective-permute-start(bf16[2,384,4,1]{1,0,3,2:T(2,128)(2,1)S(1)} %get-tuple-element.16), channel_id=1, source_target_pairs={{1,0},{2,1},{3,2},{4,3},{5,4},{6,5},{7,6},{9,8},{10,9},{11,10},{12... | collective-permute-start | bytes 18440 | tf_op jit(solution)/shard_map/ppermute | solution.py:15
  218.2 7.3 %collective-permute-start.18 = (bf16[2,384,4,1]{1,0,3,2:T(2,128)(2,1)S(1)}, bf16[2,384,4,1]{1,0,3,2:T(2,128)(2,1)S(1)}, u32[]{:S(2)}, u32[]{:S(2)}) collective-permute-start(bf16[2,384,4,1]{1,0,3,2:T(2,128)(2,1)S(1)} %get-tuple-element.15), channel_id=1, source_target_pairs={{0,1},{1,2},{2,3},{3,4},{4,5},{5,6},{6,7},{8,9},{9,10},{10,11},{11... | collective-permute-start | bytes 18440 | tf_op jit(solution)/shard_map/ppermute | solution.py:14
  236.4 12.3 %collective-permute-start.21 = (bf16[2,192,1,512]{1,3,2,0:T(8,128)(2,1)S(1)}, bf16[2,192,1,512]{1,3,2,0:T(8,128)(2,1)S(1)}, u32[]{:S(2)}, u32[]{:S(2)}) collective-permute-start(bf16[2,192,1,512]{1,3,2,0:T(8,128)(2,1)S(1)} %get-tuple-element.14), channel_id=1, source_target_pairs={{8,0},{16,8},{24,16},{32,24},{40,32},{48,40},{56,48},{64,56},{72,6... | collective-permute-start | bytes 1179656 | tf_op jit(solution)/shard_map/ppermute | solution.py:15
  238.3 14.1 %collective-permute-start.20 = (bf16[2,192,1,512]{1,3,2,0:T(8,128)(2,1)S(1)}, bf16[2,192,1,512]{1,3,2,0:T(8,128)(2,1)S(1)}, u32[]{:S(2)}, u32[]{:S(2)}) collective-permute-start(bf16[2,192,1,512]{1,3,2,0:T(8,128)(2,1)S(1)} %get-tuple-element.13), channel_id=1, source_target_pairs={{0,8},{8,16},{16,24},{24,32},{32,40},{40,48},{48,56},{56,64},{64,7... | collective-permute-start | bytes 1179656 | tf_op jit(solution)/shard_map/ppermute | solution.py:14
  252.5 16.7 %collective-permute-start.23 = (bf16[2,192,6,1]{1,3,2,0:T(2,128)(2,1)S(1)}, bf16[2,192,6,1]{1,3,2,0:T(2,128)(2,1)S(1)}, u32[]{:S(2)}, u32[]{:S(2)}) collective-permute-start(bf16[2,192,6,1]{1,3,2,0:T(2,128)(2,1)S(1)} %get-tuple-element.10), channel_id=1, source_target_pairs={{1,0},{2,1},{3,2},{4,3},{5,4},{6,5},{7,6},{9,8},{10,9},{11,10},{12... | collective-permute-start | bytes 13832 | tf_op jit(solution)/shard_map/ppermute | solution.py:15
  254.4 14.8 %collective-permute-start.22 = (bf16[2,192,6,1]{1,3,2,0:T(2,128)(2,1)S(1)}, bf16[2,192,6,1]{1,3,2,0:T(2,128)(2,1)S(1)}, u32[]{:S(2)}, u32[]{:S(2)}) collective-permute-start(bf16[2,192,6,1]{1,3,2,0:T(2,128)(2,1)S(1)} %get-tuple-element.9), channel_id=1, source_target_pairs={{0,1},{1,2},{2,3},{3,4},{4,5},{5,6},{6,7},{8,9},{9,10},{10,11},{11... | collective-permute-start | bytes 13832 | tf_op jit(solution)/shard_map/ppermute | solution.py:14
  304.3 18.4 %collective-permute-start.25 = (bf16[2,96,1,1024]{3,1,2,0:T(8,128)(2,1)S(1)}, bf16[2,96,1,1024]{3,1,2,0:T(8,128)(2,1)S(1)}, u32[]{:S(2)}, u32[]{:S(2)}) collective-permute-start(bf16[2,96,1,1024]{3,1,2,0:T(8,128)(2,1)S(1)} %copy.202), channel_id=1, source_target_pairs={{8,0},{16,8},{24,16},{32,24},{40,32},{48,40},{56,48},{64,56},{72,6... | collective-permute-start | bytes 1179656 | tf_op jit(solution)/shard_map/ppermute | solution.py:15
  306.9 15.9 %collective-permute-start.24 = (bf16[2,96,1,1024]{3,1,2,0:T(8,128)(2,1)S(1)}, bf16[2,96,1,1024]{3,1,2,0:T(8,128)(2,1)S(1)}, u32[]{:S(2)}, u32[]{:S(2)}) collective-permute-start(bf16[2,96,1,1024]{3,1,2,0:T(8,128)(2,1)S(1)} %copy.201), channel_id=1, source_target_pairs={{0,8},{8,16},{16,24},{24,32},{32,40},{40,48},{48,56},{56,64},{64,7... | collective-permute-start | bytes 1179656 | tf_op jit(solution)/shard_map/ppermute | solution.py:14
  327.1 8.7 %collective-permute-start.26 = (bf16[2,96,10,1]{3,1,2,0:T(8,128)(2,1)S(1)}, bf16[2,96,10,1]{3,1,2,0:T(8,128)(2,1)S(1)}, u32[]{:S(2)}, u32[]{:S(2)}) collective-permute-start(bf16[2,96,10,1]{3,1,2,0:T(8,128)(2,1)S(1)} %get-tuple-element.8), channel_id=1, source_target_pairs={{0,1},{1,2},{2,3},{3,4},{4,5},{5,6},{6,7},{8,9},{9,10},{10,11},{11... | collective-permute-start | bytes 11528 | tf_op jit(solution)/shard_map/ppermute | solution.py:14
  330.1 10.1 %collective-permute-start.27 = (bf16[2,96,10,1]{3,1,2,0:T(8,128)(2,1)S(1)}, bf16[2,96,10,1]{3,1,2,0:T(8,128)(2,1)S(1)}, u32[]{:S(2)}, u32[]{:S(2)}) collective-permute-start(bf16[2,96,10,1]{3,1,2,0:T(8,128)(2,1)S(1)} %get-tuple-element.7), channel_id=1, source_target_pairs={{1,0},{2,1},{3,2},{4,3},{5,4},{6,5},{7,6},{9,8},{10,9},{11,10},{12... | collective-permute-start | bytes 11528 | tf_op jit(solution)/shard_map/ppermute | solution.py:15
  (27 other events, 168.4 us)
where the time goes:
time: 425 us; the launch traced here: 418 us
  local copies, waits for them, and re-layouts  167 us (39%)
  starting transfers between devices  90.1 us (21%)
  other arithmetic  61 us (14%)
  waiting for transfers between devices  56.6 us (13%)
  matrix products  42 us (10%)
    ppermute x14, starting transfers between devices, extended(): before = lax.ppermute(last, axis, up)  60.7 us
    conv_general_dilated x16, local copies, waits for them, and re-layouts, convolve_valid(): lax.conv_general_dilated(padded, kernel, (1, 1), 'VALID', dimension_numbe...  55 us
    conv_general_dilated x7, matrix products, convolve_valid(): lax.conv_general_dilated(padded, kernel, (1, 1), 'VALID', dimension_numbe...  40.5 us
    convert_element_type x25, local copies, waits for them, and re-layouts, convolve_valid(): jax.nn.silu(result + offset[None, :, None, None]).astype(jnp.bfloat16)  34.9 us
    ppermute x14, waiting for transfers between devices, extended(): before = lax.ppermute(last, axis, up)  32.6 us
    ppermute x14, starting transfers between devices, extended(): after = lax.ppermute(first, axis, down)  29.4 us
    concatenate x9, local copies, waits for them, and re-layouts, extended(): value = jnp.concatenate([before, value, after], axis=dim)  27.5 us
    ppermute x14, waiting for transfers between devices, extended(): after = lax.ppermute(first, axis, down)  24 us
  transfers between devices with their start and end apart: 28, of which 19 were waited for; matrix products, arithmetic and copies ran while one was open for 6% of the time, Pallas kernels for 0%

commit v1 on v0

v1 whole, which is shorter than its diff:
```python
import jax
import jax.numpy as jnp
from jax import lax
from jax.experimental import pallas as pl
from jax.experimental.pallas import tpu as pltpu
from jax.sharding import PartitionSpec as P

LANES = 128
WIDE = 384
BF16 = jnp.bfloat16
F32 = jnp.float32


def neighbour(value, axis, step):
    size = lax.axis_size(axis)
    return lax.ppermute(value, axis, [(i, (i + step) % size) for i in range(size)])


def call(body, name, out_shapes, scratch, args, limit=16):
    specs = [pl.BlockSpec(memory_space=pltpu.VMEM)] * len(args)
    return pl.pallas_call(
        body,
        name=name,
        out_shape=[jax.ShapeDtypeStruct(s, d) for s, d in out_shapes],
        in_specs=specs,
        out_specs=[pl.BlockSpec(memory_space=pltpu.VMEM)] * len(out_shapes),
        scratch_shapes=scratch,
        compiler_params=pltpu.CompilerParams(vmem_limit_bytes=limit * 2**20),
    )(*args)


def iota(shape, axis):
    return lax.broadcasted_iota(jnp.int32, shape, axis)


def edges():
    ty, tx = lax.axis_index("ty"), lax.axis_index("tx")
    ny, nx = lax.axis_size("ty"), lax.axis_size("tx")
    inside = (ty > 0, ty < ny - 1, tx > 0, tx < nx - 1)
    return [jnp.where(side, 1.0, 0.0) for side in inside]


def one_hot(cond):
    return jnp.where(cond, 1.0, 0.0).astype(BF16)


def dot(a, b):
    return jnp.dot(a, b, preferred_element_type=F32)


def silu(t):
    return t * (0.5 * jnp.tanh(0.5 * t) + 0.5)


def lane_mask(flags):
    lane = iota((1, WIDE), 1)
    place = lane & 15
    edge = lane >= 256
    left = jnp.where(edge & (place < 4), flags[2], 1.0)
    right = jnp.where(edge & (place >= 12), flags[3], 1.0)
    return left * right


def from_left(slab):
    lane = iota((1, LANES), 1)
    h0, h1, edge = slab[:, :128], slab[:, 128:256], slab[:, 256:]
    h0 = jnp.where(lane == 0, pltpu.roll(edge, 125, 1), pltpu.roll(h0, 1, 1))
    h1 = jnp.where(lane == 0, pltpu.roll(edge, 109, 1), pltpu.roll(h1, 1, 1))
    return jnp.concatenate([h0, h1, pltpu.roll(edge, 1, 1)], axis=1)


def from_right(slab):
    lane = iota((1, LANES), 1)
    h0, h1, edge = slab[:, :128], slab[:, 128:256], slab[:, 256:]
    h0 = jnp.where(lane == 127, pltpu.roll(edge, 115, 1), pltpu.roll(h0, 127, 1))
    h1 = jnp.where(lane == 127, pltpu.roll(edge, 99, 1), pltpu.roll(h1, 127, 1))
    return jnp.concatenate([h0, h1, pltpu.roll(edge, 127, 1)], axis=1)


def put(scratch, row, phases, slab_of, valid=None):
    for p in range(phases):
        slab = slab_of(p)
        if valid is not None:
            slab = jnp.where(valid > 0.5, slab, jnp.zeros_like(slab))
        scratch[row, p + 1] = slab
        if p == 0:
            scratch[row, phases + 1] = from_right(slab)
        if p == phases - 1:
            scratch[row, 0] = from_left(slab)


def window(scratch, row, phase, rows, cols):
    v = scratch[pl.ds(row, rows), phase : phase + cols]
    return v.reshape(rows * cols * v.shape[2], v.shape[3])


def fields_kernel(x, fl, fr, out):
    flags = edges()
    lane = iota((1, LANES), 1)
    rows = x.shape[1]
    i, k = iota((rows, rows), 0), iota((rows, rows), 1)
    turn = one_hot(i == (k & 7) * (rows // 8) + (k >> 3))
    ends = []
    for h in range(2):
        a = jnp.where((lane >= 96) & (flags[2] > 0.5), fl[h], jnp.where(lane < 32, x[h, :, :128], 0))
        b = jnp.where(lane >= 96, x[h, :, 896:], jnp.where((lane < 32) & (flags[3] > 0.5), fr[h], 0))
        ends += [a.astype(BF16), b.astype(BF16)]
    ends = jnp.concatenate(ends, axis=1)
    channels = rows // 8
    for q in range(4):
        c = iota((1, 256), 1)
        split = one_hot(iota((1024, 256), 0) == 8 * (c & 127) + 2 * q + (c >> 7))
        row = 128 * ((c & 127) >> 3) + (((8 * (c & 7) + 2 * q + (c >> 7)) + 96) & 127)
        pick = (iota((512, 256), 0) == row) & ((c & 127) < 32)
        parts = [dot(x[0], split), dot(x[1], split), dot(ends, one_hot(pick))]
        for n, part in enumerate(parts):
            part = dot(turn, part.astype(BF16)).astype(BF16)
            for r in range(8):
                for s in range(2):
                    out[r, 2 * q + s, :, n * 128 : (n + 1) * 128] = part[
                        r * channels : (r + 1) * channels, s * 128 : (s + 1) * 128
                    ]


def one_kernel(x, above, below, w, b, skip, pooled, first, last, xs):
    flags = edges()
    put(xs, 0, 8, lambda p: above[p], flags[0])
    for r in range(8):
        put(xs, r + 1, 8, lambda p: x[r, p])
    put(xs, 9, 8, lambda p: below[p], flags[1])
    mask = lane_mask(flags)
    bias = b[...]

    def pair(k, carry):
        for q in range(4):
            total = None
            for r in range(2):
                rhs = jnp.concatenate(
                    [window(xs, 2 * k + r, 2 * q + s, 3, 3) for s in range(2)], axis=1
                )
                res = dot(w[...], rhs)
                for s in range(2):
                    y = (silu(res[:, s * WIDE : (s + 1) * WIDE] + bias) * mask).astype(BF16)
                    skip[2 * k + r, 2 * q + s] = y
                    total = y.astype(F32) if total is None else total + y.astype(F32)
            pooled[k, q] = (total * 0.25).astype(BF16)
        return carry

    lax.fori_loop(0, 4, pair, 0)
    first[...] = pooled[0:3]
    last[...] = pooled[1:4]


def two_kernel(x, above, below, w2, b2, w3, b3, skip2, skip3, coarse_in, xs, xs3, tmp):
    flags = edges()
    for r in range(3):
        put(xs, r, 4, lambda p: above[r, p], flags[0])
        put(xs, r + 7, 4, lambda p: below[r, p], flags[1])
    for r in range(4):
        put(xs, r + 3, 4, lambda p: x[r, p])
    mask = lane_mask(flags)
    bias = b2[...]

    def pair(k, carry):
        valid = jnp.where(k == 0, flags[0], jnp.where(k == 3, flags[1], 1.0))
        for q in range(2):
            total = None
            for r in range(2):
                rhs = jnp.concatenate(
                    [window(xs, 2 * k + r, 2 * q + s, 3, 3) for s in range(2)], axis=1
                )
                res = dot(w2[...], rhs)
                for s in range(2):
                    y = silu(res[:, s * WIDE : (s + 1) * WIDE] + bias) * (mask * valid)
                    y = y.astype(BF16)
                    skip2[2 * k + r, 2 * q + s] = y
                    total = y.astype(F32) if total is None else total + y.astype(F32)
            tmp[k, q] = (total * 0.25).astype(BF16)
        return carry

    lax.fori_loop(0, 4, pair, 0)
    for r in range(4):
        put(xs3, r, 2, lambda p: tmp[r, p])
    total = None
    for r in range(2):
        for p in range(2):
            y = silu(dot(w3[...], window(xs3, r, p, 3, 3)) + b3[...]) * mask
            y = y.astype(BF16)
            skip3[r, p] = y
            total = y.astype(F32) if total is None else total + y.astype(F32)
    coarse_in[...] = (total * 0.25).astype(BF16)


def coarse_kernel(x, above, below, w, b, out, xs):
    flags = edges()
    put(xs, 0, 1, lambda p: above[...], flags[0])
    put(xs, 1, 1, lambda p: x[...])
    put(xs, 2, 1, lambda p: below[...], flags[1])
    res = dot(w[...], window(xs, 0, 0, 3, 3)) + b[...]
    out[...] = (silu(res) * lane_mask(flags)).astype(BF16)


def back_kernel(
    c, c_up, c_dn, s3, s3_up, s3_dn, s2, wu3, ws3, b3, wu2, ws2, b2, out, xc, x3, xb, x2
):
    flags = edges()
    put(xc, 0, 1, lambda p: c_up[...], flags[0])
    put(xc, 1, 1, lambda p: c[...])
    put(xc, 2, 1, lambda p: c_dn[...], flags[1])
    for r in range(2):
        put(x3, r, 2, lambda p: s3_up[r, p], flags[0])
        put(x3, r + 2, 2, lambda p: s3[r, p])
        put(x3, r + 4, 2, lambda p: s3_dn[r, p], flags[1])
    mask = lane_mask(flags)
    for r in range(-1, 3):
        valid = flags[0] if r < 0 else flags[1] if r > 1 else None
        slabs = []
        for p in range(2):
            res = dot(wu3[r & 1, p], window(xc, (r + 1) // 2, p, 2, 2))
            res = res + dot(ws3[...], window(x3, r + 1, p, 3, 3))
            y = silu(res + b3[...]) * mask
            if valid is not None:
                y = y * valid
            slabs.append(y.astype(BF16))
        put(xb, r + 1, 2, lambda p: slabs[p])
    for r in range(8):
        put(x2, r, 4, lambda p: s2[r, p])

    def pair(k, carry):
        for i in range(2):
            valid = jnp.where(
                (k == 0) & (i == 0), flags[0], jnp.where((k == 2) & (i == 1), flags[1], 1.0)
            )
            for p in range(4):
                res = dot(wu2[1 - i, p & 1], window(xb, k, (p + 1) // 2, 2, 2))
                res = res + dot(ws2[...], window(x2, 2 * k + i, p, 3, 3))
                out[2 * k + i, p] = (silu(res + b2[...]) * (mask * valid)).astype(BF16)
        return carry

    lax.fori_loop(0, 3, pair, 0)


def last_kernel(bt, s1, s1_up, s1_dn, wu, ws, b, out, xb, x1):
    flags = edges()
    for r in range(6):
        put(xb, r, 4, lambda p: bt[r, p])
    put(x1, 0, 8, lambda p: s1_up[p], flags[0])
    for r in range(8):
        put(x1, r + 1, 8, lambda p: s1[r, p])
    put(x1, 9, 8, lambda p: s1_dn[p], flags[1])

    def pair(k, carry):
        for i in range(2):
            for p in range(8):
                up = window(xb, k + i, (p + 1) // 2, 2, 2)[:, :256]
                res = dot(wu[i, p & 1], up)
                res = res + dot(ws[...], window(x1, 2 * k + i, p, 3, 3)[:, :256])
                y = silu(res + b[...]).astype(BF16)
                for h in range(2):
                    out[h, 2 * k + i, :, p * 128 : (p + 1) * 128] = y[:, h * 128 : (h + 1) * 128]
        return carry

    lax.fori_loop(0, 4, pair, 0)


def head_kernel_body(back, fields, w, offset, out):
    col = iota((1, 256), 1) + 256 * pl.program_id(0)
    merge = one_hot(iota((1024, 256), 0) == 128 * (col & 7) + (col >> 3))
    for h in range(2):
        rows = dot(back[h], merge).astype(BF16)
        out[h] = fields[h].astype(F32) + offset[...] + dot(w[...], rows)


def flip(value):
    eye = one_hot(iota((value.shape[1],) * 2, 0) == iota((value.shape[1],) * 2, 1))
    dims = (((1,), (1,)), ((), ()))
    return lax.dot_general(eye, value, dims, preferred_element_type=F32).astype(BF16)


def column(row, width, repeat=1):
    size = row.shape[1]
    i, j = iota((size * repeat, size), 0), iota((size * repeat, size), 1)
    col = jnp.sum(jnp.where(i // repeat == j, row, 0.0), axis=1, keepdims=True)
    return jnp.broadcast_to(col, (size * repeat, width))


def sums(a):
    return ((0,), (1, 2)) if a == 0 else ((0, 1), (2,))


def summed(tap, a, b, i, j):
    total = None
    for dy in sums(a)[i]:
        for dx in sums(b)[j]:
            value = tap(dy, dx).astype(F32)
            total = value if total is None else total + value
    return total.astype(BF16)


def placed(parts, width):
    size = parts[0].shape[1]
    total = None
    for n, part in enumerate(parts):
        spot = one_hot(iota((size, width), 1) == iota((size, width), 0) + n * size)
        value = dot(part, spot)
        total = value if total is None else total + value
    return total.astype(BF16)


NINE = [(dy, dx) for dy in range(3) for dx in range(3)]
FOUR = [(i, j) for i in range(2) for j in range(2)]


def early_kernel(k1, k2, k3, r1, r2, r3, w1, w2, w3, b1, b2, b3):
    w1[...] = placed([k1[n] for n in NINE], w1.shape[1])
    w2[...] = flip(k2[...].reshape(-1, k2.shape[3]))
    w3[...] = flip(k3[...].reshape(-1, k3.shape[3]))
    for r, b in ((r1, b1), (r2, b2), (r3, b3)):
        b[...] = column(r[...], WIDE)


def late_kernel(
    kc, d3, d2, d1, hk, rc, r3, r2, r1, rh, wc, wu3, ws3, wu2, ws2, wu1, ws1, wh, bc, b3, b2, b1, bh
):
    wc[...] = flip(kc[...].reshape(-1, kc.shape[3]))
    for r, b in ((rc, bc), (r3, b3), (r2, b2), (r1, b1)):
        b[...] = column(r[...], b.shape[1])
    bh[...] = column(rh[...], bh.shape[1], 8)
    up3, up2, up1 = wu3.shape[3] // 4, wu2.shape[3] // 4, wu1.shape[3] // 4
    for a in range(2):
        for b in range(2):
            tall = [summed(lambda y, x: d3[y, x, :up3, :], a, b, i, j) for i, j in FOUR]
            wu3[a, b] = flip(jnp.concatenate(tall, axis=0))
            wide = [summed(lambda y, x: d2[y, x, :, :up2], a, b, i, j) for i, j in FOUR]
            wu2[a, b] = jnp.concatenate(wide, axis=1)
            wide = [summed(lambda y, x: d1[y, x, :, :up1], a, b, i, j) for i, j in FOUR]
            wu1[a, b] = placed(wide, wu1.shape[3])
    ws3[...] = flip(jnp.concatenate([d3[y, x, up3:, :] for y, x in NINE], axis=0))
    ws2[...] = placed([d2[y, x, :, up2:] for y, x in NINE], ws2.shape[1])
    ws1[...] = placed([d1[y, x, :, up1:] for y, x in NINE], ws1.shape[1])
    v, c = hk.shape[1], hk.shape[0]
    spread = one_hot(iota((v * 8, v), 0) // 8 == iota((v * 8, v), 1))
    dims = (((1,), (1,)), ((), ()))
    tall = lax.dot_general(spread, hk[...], dims, preferred_element_type=F32).astype(BF16)
    i, k = iota((v * 8, 8 * c), 0), iota((v * 8, 8 * c), 1)
    tiled = dot(tall, one_hot(iota((c, 8 * c), 0) == iota((c, 8 * c), 1) % c))
    wh[...] = jnp.where(i % 8 == k // c, tiled, 0.0).astype(BF16)


def body(
    fields,
    kernel_one,
    bias_one,
    kernel_two,
    bias_two,
    kernel_three,
    bias_three,
    kernel_coarse,
    bias_coarse,
    decode_three,
    offset_three,
    decode_two,
    offset_two,
    decode_one,
    offset_one,
    head_kernel,
    head_offset,
):
    c1, c2, c3, c4 = (k.shape[3] for k in (kernel_one, kernel_two, kernel_three, kernel_coarse))
    v = fields.shape[1]

    x = fields.reshape(2, v * 8, 1024)
    from_l = neighbour(x[:, :, 896:], "tx", 1)
    from_r = neighbour(x[:, :, :128], "tx", -1)

    def up(value):
        return neighbour(value, "ty", -1)

    def down(value):
        return neighbour(value, "ty", 1)

    row = lambda bias: bias[None, :]
    swap = lambda kernel: jnp.transpose(kernel, (0, 1, 3, 2))
    weights = lambda *shape: (shape, BF16)
    biases = lambda size, width=WIDE: ((size, width), F32)
    w1, w2, w3, b1, b2, b3 = call(
        early_kernel,
        "early",
        [weights(c1, 9 * v), weights(c2, 9 * c1), weights(c3, 9 * c2)]
        + [biases(c1), biases(c2), biases(c3)],
        [],
        [swap(kernel_one), kernel_two, kernel_three, row(bias_one), row(bias_two), row(bias_three)],
    )
    wc, wu3, ws3, wu2, ws2, wu1, ws1, wh, bc, ob3, ob2, ob1, bh = call(
        late_kernel,
        "late",
        [weights(c4, 9 * c3), weights(2, 2, c3, 4 * c4), weights(c3, 9 * c3)]
        + [weights(2, 2, c2, 4 * c3), weights(c2, 9 * c2)]
        + [weights(2, 2, c1, 4 * c2), weights(c1, 9 * c1), weights(8 * v, 8 * c1)]
        + [biases(c4), biases(c3), biases(c2), biases(c1, 256), biases(8 * v, 256)],
        [],
        [kernel_coarse, decode_three, swap(decode_two), swap(decode_one), head_kernel]
        + [row(b) for b in (bias_coarse, offset_three, offset_two, offset_one, head_offset)],
    )
    (f,) = call(fields_kernel, "fields", [((8, 8, v, WIDE), BF16)], [], [x, from_l, from_r])
    s1, p1, p1_first, p1_last = call(
        one_kernel,
        "one",
        [((8, 8, c1, WIDE), BF16), ((4, 4, c1, WIDE), BF16)] + [((3, 4, c1, WIDE), BF16)] * 2,
        [pltpu.VMEM((10, 10, v, WIDE), BF16)],
        [f, down(f[7]), up(f[0]), w1, b1],
    )
    s2, s3, coarse_in = call(
        two_kernel,
        "two",
        [((8, 4, c2, WIDE), BF16), ((2, 2, c3, WIDE), BF16), ((c3, WIDE), BF16)],
        [
            pltpu.VMEM((10, 6, c1, WIDE), BF16),
            pltpu.VMEM((4, 4, c2, WIDE), BF16),
            pltpu.VMEM((4, 2, c2, WIDE), BF16),
        ],
        [p1, down(p1_last), up(p1_first), w2, b2]
        + [w3, b3],
    )
    (coarse,) = call(
        coarse_kernel,
        "coarse",
        [((c4, WIDE), BF16)],
        [pltpu.VMEM((3, 3, c3, WIDE), BF16)],
        [coarse_in, down(coarse_in), up(coarse_in), wc, bc],
    )
    (back_two,) = call(
        back_kernel,
        "back",
        [((6, 4, c2, WIDE), BF16)],
        [
            pltpu.VMEM((3, 3, c4, WIDE), BF16),
            pltpu.VMEM((6, 4, c3, WIDE), BF16),
            pltpu.VMEM((4, 4, c3, WIDE), BF16),
            pltpu.VMEM((8, 6, c2, WIDE), BF16),
        ],
        [coarse, down(coarse), up(coarse), s3, down(s3), up(s3), s2]
        + [wu3, ws3, ob3, wu2, ws2, ob2],
    )
    (back_one,) = call(
        last_kernel,
        "last",
        [((2, 8, c1, 1024), BF16)],
        [pltpu.VMEM((6, 6, c2, WIDE), BF16), pltpu.VMEM((10, 10, c1, WIDE), BF16)],
        [back_two, s1, down(s1[7]), up(s1[0])]
        + [wu1, ws1, ob1],
    )
    block = lambda rows, dtype: pl.BlockSpec((2, rows, 256), lambda i: (0, 0, i))
    whole = lambda *shape: pl.BlockSpec(shape, lambda i: (0,) * len(shape))
    out = pl.pallas_call(
        head_kernel_body,
        name="head",
        grid=(4,),
        out_shape=jax.ShapeDtypeStruct((2, v * 8, 1024), F32),
        in_specs=[whole(2, 8 * c1, 1024), block(v * 8, BF16), whole(v * 8, 8 * c1), whole(v * 8, 256)],
        out_specs=block(v * 8, F32),
        compiler_params=pltpu.CompilerParams(vmem_limit_bytes=24 * 2**20),
    )(
        back_one.reshape(2, 8 * c1, 1024),
        x,
        wh,
        bh,
    )
    return out.reshape(2, v, 8, 1024)


def solution(mesh):
    return jax.shard_map(
        body,
        mesh=mesh,
        in_specs=(P(None, None, "ty", "tx"),) + (P(),) * 16,
        out_specs=P(None, None, "ty", "tx"),
        check_vma=False,
    )
```

time: 425 us -> 90.5 us (0.21)
  the two profiles are of different devices: /device:TPU:97 before, /device:TPU:24 now
where the time goes in v1:
time: 90.5 us; the launch traced here: 89.6 us
  Pallas kernels  31 us (34%)
  starting transfers between devices  30.4 us (34%)
  waiting for transfers between devices  25.2 us (28%)
  local copies, waits for them, and re-layouts  2.66 us (3%)
    ppermute x14, starting transfers between devices, neighbour(): lax.ppermute(value, axis, [(i, (i + step) % size) for i in range(size)])  30.4 us
    pallas_call x8, Pallas kernels, call(): pl.pallas_call(body, name=name, out_shape=[jax.ShapeDtypeStruct(s, d) for...  25.3 us
    ppermute x14, waiting for transfers between devices, neighbour(): lax.ppermute(value, axis, [(i, (i + step) % size) for i in range(size)])  25.2 us
    pallas_call x1, Pallas kernels, body(): pl.pallas_call(head_kernel_body, name='head', grid=(4,), out_shape=jax.Sh...  5.69 us
  transfers between devices with their start and end apart: 14, of which 4 were waited for; matrix products, arithmetic and copies ran while one was open for 0% of the time, Pallas kernels for 10%

profile of v1, /device:TPU:24, one launch (start us, length us, event | category | flops | bytes accessed | tf_op | source)
XLA Modules:
  0.0 89.6 jit_solution(1188531527283193782)
XLA Ops:
  0.0 1.1 %fusion = (bf16[2,384,128]{2,1,0:T(8,128)(2,1)S(1)}, bf16[2,384,128]{2,1,0:T(8,128)(2,1)S(1)}) fusion(bf16[2,384,1024]{2,1,0:T(8,128)(2,1)} %bitcast.22), kind=kLoop, calls=%fused_computation.4 | loop fusion | bytes 786432 | tf_op jit(solution)/shard_map/slice | solution.py:374
  1.1 0.0 collective-permute-start
  1.1 0.0 copy-start.11
  1.1 1.7 %collective-permute-start.1 = (bf16[2,384,128]{2,1,0:T(8,128)(2,1)S(1)}, bf16[2,384,128]{2,1,0:T(8,128)(2,1)S(1)}, u32[]{:S(2)}, u32[]{:S(2)}) collective-permute-start(bf16[2,384,128]{2,1,0:T(8,128)(2,1)S(1)} %get-tuple-element.61), channel_id=1, source_target_pairs={{0,7},{1,0},{2,1},{3,2},{4,3},{5,4},{6,5},{7,6},{8,15},{9,8},{10,9... | collective-permute-start | bytes 589832 | tf_op jit(solution)/shard_map/ppermute | solution.py:16
  2.8 3.3 %collective-permute-done.fl = bf16[2,384,128]{2,1,0:T(8,128)(2,1)S(1)} collective-permute-done((bf16[2,384,128]{2,1,0:T(8,128)(2,1)S(1)}, bf16[2,384,128]{2,1,0:T(8,128)(2,1)S(1)}, u32[]{:S(2)}, u32[]{:S(2)}) %collective-permute-start) | collective-permute-done | bytes 196640 | tf_op jit(solution)/shard_map/ppermute | solution.py:16
  6.2 1.4 %copy-done = bf16[2,48,8,1024]{3,2,1,0:T(8,128)(2,1)S(1)} copy-done((bf16[2,48,8,1024]{3,2,1,0:T(8,128)(2,1)S(1)}, bf16[2,48,8,1024]{3,2,1,0:T(8,128)(2,1)}, u32[]{:S(2)}) %copy-start) | copy-done | bytes 1572888
  7.6 3.5 %fields.1.x = bf16[8,8,48,384]{3,2,1,0:T(8,128)(2,1)S(1)} custom-call(bf16[2,384,1024]{2,1,0:T(8,128)(2,1)S(1)} %bitcast.23, bf16[2,384,128]{2,1,0:T(8,128)(2,1)S(1)} %collective-permute-done.fl, bf16[2,384,128]{2,1,0:T(8,128)(2,1)S(1)} %collective-permute-done.1.fr), custom_call_target="tpu_custom_call" | custom-call | tf_op jit(solution)/shard_map/fields/pallas_call | solution.py:21
  11.1 0.1 slice_bitcast_fusion
  11.2 1.6 %collective-permute-start.2 = (bf16[8,48,384]{2,1,0:T(8,128)(2,1)S(1)}, bf16[8,48,384]{2,1,0:T(8,128)(2,1)S(1)}, u32[]{:S(2)}, u32[]{:S(2)}) collective-permute-start(bf16[8,48,384]{2,1,0:T(8,128)(2,1)S(1)} %get-tuple-element.58), channel_id=1, source_target_pairs={{0,8},{8,16},{16,24},{24,32},{32,40},{40,48},{48,56},{56,64},{64,7... | collective-permute-start | bytes 884744 | tf_op jit(solution)/shard_map/ppermute | solution.py:16
  12.8 4.8 %collective-permute-start.3 = (bf16[8,48,384]{2,1,0:T(8,128)(2,1)S(1)}, bf16[8,48,384]{2,1,0:T(8,128)(2,1)S(1)}, u32[]{:S(2)}, u32[]{:S(2)}) collective-permute-start(bf16[8,48,384]{2,1,0:T(8,128)(2,1)S(1)} %get-tuple-element.57), channel_id=1, source_target_pairs={{0,120},{8,0},{16,8},{24,16},{32,24},{40,32},{48,40},{56,48},{64,5... | collective-permute-start | bytes 884744 | tf_op jit(solution)/shard_map/ppermute | solution.py:16
  17.6 0.3 early.1
  17.9 6.6 %collective-permute-done.2.above = bf16[8,48,384]{2,1,0:T(8,128)(2,1)S(1)} collective-permute-done((bf16[8,48,384]{2,1,0:T(8,128)(2,1)S(1)}, bf16[8,48,384]{2,1,0:T(8,128)(2,1)S(1)}, u32[]{:S(2)}, u32[]{:S(2)}) %collective-permute-start.2) | collective-permute-done | bytes 294944 | tf_op jit(solution)/shard_map/ppermute | solution.py:16
  24.5 0.0 copy-start.9
  24.5 0.0 copy-start.10
  24.6 4.9 %one.1 = (bf16[8,8,32,384]{3,2,1,0:T(8,128)(2,1)S(1)}, bf16[4,4,32,384]{3,2,1,0:T(8,128)(2,1)S(1)}, bf16[3,4,32,384]{3,2,1,0:T(8,128)(2,1)S(1)}, bf16[3,4,32,384]{3,2,1,0:T(8,128)(2,1)S(1)}) custom-call(bf16[8,8,48,384]{3,2,1,0:T(8,128)(2,1)S(1)} %fields.1.x, bf16[8,48,384]{2,1,0:T(8,128)(2,1)S(1)} %collective-permute-done.2.above, ...), custom_call_target="tpu_custom_call" | custom-call | tf_op jit(solution)/shard_map/one/pallas_call | solution.py:21
  29.6 0.1 collective-permute-start.4
  29.6 5.8 %collective-permute-start.5 = (bf16[3,4,32,384]{3,2,1,0:T(8,128)(2,1)S(1)}, bf16[3,4,32,384]{3,2,1,0:T(8,128)(2,1)S(1)}, u32[]{:S(2)}, u32[]{:S(2)}) collective-permute-start(bf16[3,4,32,384]{3,2,1,0:T(8,128)(2,1)S(1)} %get-tuple-element.35), channel_id=1, source_target_pairs={{0,120},{8,0},{16,8},{24,16},{32,24},{40,32},{48,40},{56,48},{64,5... | collective-permute-start | bytes 884744 | tf_op jit(solution)/shard_map/ppermute | solution.py:16
  35.4 7.5 %collective-permute-done.4.above = bf16[3,4,32,384]{3,2,1,0:T(8,128)(2,1)S(1)} collective-permute-done((bf16[3,4,32,384]{3,2,1,0:T(8,128)(2,1)S(1)}, bf16[3,4,32,384]{3,2,1,0:T(8,128)(2,1)S(1)}, u32[]{:S(2)}, u32[]{:S(2)}) %collective-permute-start.4) | collective-permute-done | bytes 294944 | tf_op jit(solution)/shard_map/ppermute | solution.py:16
  42.9 3.3 %two.1 = (bf16[8,4,64,384]{3,2,1,0:T(8,128)(2,1)S(1)}, bf16[2,2,128,384]{3,2,1,0:T(8,128)(2,1)S(1)}, bf16[128,384]{1,0:T(8,128)(2,1)S(1)}) custom-call(bf16[4,4,32,384]{3,2,1,0:T(8,128)(2,1)S(1)} %get-tuple-element.33.x, bf16[3,4,32,384]{3,2,1,0:T(8,128)(2,1)S(1)} %collective-permute-done.4.above, bf16[3,4,32,384]{3,2,1,0:T(8,128)(2,1)S(1)} %collective-permute-done.5.below, ...), custom_call_target="tpu_custom_call" | custom-call | tf_op jit(solution)/shard_map/two/pallas_call | solution.py:21
  46.2 0.1 collective-permute-start.6
  46.3 5.3 %collective-permute-start.7 = (bf16[128,384]{1,0:T(8,128)(2,1)S(1)}, bf16[128,384]{1,0:T(8,128)(2,1)S(1)}, u32[]{:S(2)}, u32[]{:S(2)}) collective-permute-start(bf16[128,384]{1,0:T(8,128)(2,1)S(1)} %get-tuple-element.40.x), channel_id=1, source_target_pairs={{0,120},{8,0},{16,8},{24,16},{32,24},{40,32},{48,40},{56,48},{64,5... | collective-permute-start | bytes 294920 | tf_op jit(solution)/shard_map/ppermute | solution.py:16
  51.7 1.4 %late.1 = (bf16[256,1152]{1,0:T(8,128)(2,1)S(1)}, bf16[2,2,128,1024]{3,2,1,0:T(8,128)(2,1)S(1)}, bf16[128,1152]{1,0:T(8,128)(2,1)S(1)}, bf16[2,2,64,512]{3,2,1,0...) custom-call(bf16[3,3,128,256]{3,2,1,0:T(8,128)(2,1)S(1)} %copy-done., ...), custom_call_target="tpu_custom_call" | custom-call | tf_op jit(solution)/shard_map/late/pallas_call | solution.py:21
  53.1 0.1 collective-permute-start.10
  53.2 5.3 %collective-permute-start.11 = (bf16[2,2,128,384]{3,2,1,0:T(8,128)(2,1)S(1)}, bf16[2,2,128,384]{3,2,1,0:T(8,128)(2,1)S(1)}, u32[]{:S(2)}, u32[]{:S(2)}) collective-permute-start(bf16[2,2,128,384]{3,2,1,0:T(8,128)(2,1)S(1)} %get-tuple-element.43.s3), channel_id=1, source_target_pairs={{0,120},{8,0},{16,8},{24,16},{32,24},{40,32},{48,40},{56,48},{64,5... | collective-permute-start | bytes 1179656 | tf_op jit(solution)/shard_map/ppermute | solution.py:16
  58.5 0.7 coarse.1.c
  59.2 0.3 collective-permute-start.8
  59.4 5.3 %collective-permute-start.9 = (bf16[256,384]{1,0:T(8,128)(2,1)S(1)}, bf16[256,384]{1,0:T(8,128)(2,1)S(1)}, u32[]{:S(2)}, u32[]{:S(2)}) collective-permute-start(bf16[256,384]{1,0:T(8,128)(2,1)S(1)} %coarse.1.c), channel_id=1, source_target_pairs={{0,120},{8,0},{16,8},{24,16},{32,24},{40,32},{48,40},{56,48},{64,5... | collective-permute-start | bytes 589832 | tf_op jit(solution)/shard_map/ppermute | solution.py:16
  64.8 0.1 collective-permute-start.12
  64.9 7.8 %collective-permute-done.8.c_up = bf16[256,384]{1,0:T(8,128)(2,1)S(1)} collective-permute-done((bf16[256,384]{1,0:T(8,128)(2,1)S(1)}, bf16[256,384]{1,0:T(8,128)(2,1)S(1)}, u32[]{:S(2)}, u32[]{:S(2)}) %collective-permute-start.8) | collective-permute-done | bytes 196640 | tf_op jit(solution)/shard_map/ppermute | solution.py:16
  72.7 6.8 %back.1.bt = bf16[6,4,64,384]{3,2,1,0:T(8,128)(2,1)S(1)} custom-call(bf16[256,384]{1,0:T(8,128)(2,1)S(1)} %coarse.1.c, bf16[256,384]{1,0:T(8,128)(2,1)S(1)} %collective-permute-done.8.c_up, bf16[256,384]{1,0:T(8,128)(2,1)S(1)} %collective-permute-done.9.c_dn, bf16[2,2,128,384]{3,2,1,0:T(8,128)(2,1)S(1)} %get-tuple-element.43.s3, ...), custom_call_target="tpu_custom_call" | custom-call | tf_op jit(solution)/shard_map/back/pallas_call | solution.py:21
  79.6 4.3 %last.1 = bf16[2,8,32,1024]{3,2,1,0:T(8,128)(2,1)S(1)} custom-call(bf16[6,4,64,384]{3,2,1,0:T(8,128)(2,1)S(1)} %back.1.bt, bf16[8,8,32,384]{3,2,1,0:T(8,128)(2,1)S(1)} %get-tuple-element.51.s1, bf16[8,32,384]{2,1,0:T(8,128)(2,1)S(1)} %collective-permute-done.12.s1_up, bf16[8,32,384]{2,1,0:T(8,128)(2,1)S(1)} %collective-permute-done.13.s1_dn, ...), custom_call_target="tpu_custom_call" | custom-call | tf_op jit(solution)/shard_map/last/pallas_call | solution.py:21
  83.9 5.7 %head.1 = f32[2,384,1024]{2,1,0:T(8,128)} custom-call(bf16[2,256,1024]{2,1,0:T(8,128)(2,1)S(1)} %bitcast.25, bf16[2,384,1024]{2,1,0:T(8,128)(2,1)S(1)} %bitcast.24, bf16[384,256]{1,0:T(8,128)(2,1)S(1)} %get-tuple-element.55.w, f32[384,256]{1,0:T(8,128)S(1)} %get-tuple-element.56.offset), custom_call_target="tpu_custom_call" | custom-call | tf_op jit(solution)/shard_map/head/pallas_call | solution.py:455
  (44 shorter events, 0.1 us)
Async XLA Ops:
  1.1 5.1 %collective-permute-start = (bf16[2,384,128]{2,1,0:T(8,128)(2,1)S(1)}, bf16[2,384,128]{2,1,0:T(8,128)(2,1)S(1)}, u32[]{:S(2)}, u32[]{:S(2)}) collective-permute-start(bf16[2,384,128]{2,1,0:T(8,128)(2,1)S(1)} %get-tuple-element.62), channel_id=1, source_target_pairs={{0,1},{1,2},{2,3},{3,4},{4,5},{5,6},{6,7},{7,0},{8,9},{9,10},{10,1... | collective-permute-start | bytes 589832 | tf_op jit(solution)/shard_map/ppermute | solution.py:16
  1.1 16.5 %copy-start.11 = (f32[32]{0:T(128)S(1)}, f32[32]{0:T(128)}, u32[]{:S(2)}) copy-start(f32[32]{0:T(128)} %param.19) | copy-start | bytes 388
  1.1 16.5 %copy-start.12 = (f32[64]{0:T(128)S(1)}, f32[64]{0:T(128)}, u32[]{:S(2)}) copy-start(f32[64]{0:T(128)} %param.21) | copy-start | bytes 772
  1.1 16.5 %copy-start.13 = (f32[128]{0:T(128)S(1)}, f32[128]{0:T(128)}, u32[]{:S(2)}) copy-start(f32[128]{0:T(128)} %param.23) | copy-start | bytes 1540
  1.1 5.0 %collective-permute-start.1 = (bf16[2,384,128]{2,1,0:T(8,128)(2,1)S(1)}, bf16[2,384,128]{2,1,0:T(8,128)(2,1)S(1)}, u32[]{:S(2)}, u32[]{:S(2)}) collective-permute-start(bf16[2,384,128]{2,1,0:T(8,128)(2,1)S(1)} %get-tuple-element.61), channel_id=1, source_target_pairs={{0,7},{1,0},{2,1},{3,2},{4,3},{5,4},{6,5},{7,6},{8,15},{9,8},{10,9... | collective-permute-start | bytes 589832 | tf_op jit(solution)/shard_map/ppermute | solution.py:16
  6.2 1.4 %copy-start = (bf16[2,48,8,1024]{3,2,1,0:T(8,128)(2,1)S(1)}, bf16[2,48,8,1024]{3,2,1,0:T(8,128)(2,1)}, u32[]{:S(2)}) copy-start(bf16[2,48,8,1024]{3,2,1,0:T(8,128)(2,1)} %param.17) | copy-start | bytes 4718596
  7.6 10.0 %copy-start.5 = (bf16[3,3,64,128]{3,2,1,0:T(8,128)(2,1)S(1)}, bf16[3,3,64,128]{3,2,1,0:T(8,128)(2,1)}, u32[]{:S(2)}) copy-start(bf16[3,3,64,128]{3,2,1,0:T(8,128)(2,1)} %k3.1) | copy-start | bytes 442372
  7.6 10.0 %copy-start.7 = (bf16[3,3,48,32]{2,3,1,0:T(8,128)(2,1)S(1)}, bf16[3,3,48,32]{2,3,1,0:T(8,128)(2,1)}, u32[]{:S(2)}) copy-start(bf16[3,3,48,32]{2,3,1,0:T(8,128)(2,1)} %param.18) | copy-start | bytes 82948
  7.6 10.0 %copy-start.8 = (bf16[3,3,32,64]{3,2,1,0:T(8,128)(2,1)S(1)}, bf16[3,3,32,64]{3,2,1,0:T(8,128)(2,1)}, u32[]{:S(2)}) copy-start(bf16[3,3,32,64]{3,2,1,0:T(8,128)(2,1)} %k2.1) | copy-start | bytes 110596
  11.2 13.3 %collective-permute-start.2 = (bf16[8,48,384]{2,1,0:T(8,128)(2,1)S(1)}, bf16[8,48,384]{2,1,0:T(8,128)(2,1)S(1)}, u32[]{:S(2)}, u32[]{:S(2)}) collective-permute-start(bf16[8,48,384]{2,1,0:T(8,128)(2,1)S(1)} %get-tuple-element.58), channel_id=1, source_target_pairs={{0,8},{8,16},{16,24},{24,32},{32,40},{40,48},{48,56},{56,64},{64,7... | collective-permute-start | bytes 884744 | tf_op jit(solution)/shard_map/ppermute | solution.py:16
  12.8 11.7 %collective-permute-start.3 = (bf16[8,48,384]{2,1,0:T(8,128)(2,1)S(1)}, bf16[8,48,384]{2,1,0:T(8,128)(2,1)S(1)}, u32[]{:S(2)}, u32[]{:S(2)}) collective-permute-start(bf16[8,48,384]{2,1,0:T(8,128)(2,1)S(1)} %get-tuple-element.57), channel_id=1, source_target_pairs={{0,120},{8,0},{16,8},{24,16},{32,24},{40,32},{48,40},{56,48},{64,5... | collective-permute-start | bytes 884744 | tf_op jit(solution)/shard_map/ppermute | solution.py:16
  24.5 27.1 %copy-start.2 = (bf16[3,3,384,128]{3,2,1,0:T(8,128)(2,1)S(1)}, bf16[3,3,384,128]{3,2,1,0:T(8,128)(2,1)}, u32[]{:S(2)}) copy-start(bf16[3,3,384,128]{3,2,1,0:T(8,128)(2,1)} %d3.1) | copy-start | bytes 2654212
  24.5 27.1 %copy-start.3 = (bf16[3,3,128,256]{3,2,1,0:T(8,128)(2,1)S(1)}, bf16[3,3,128,256]{3,2,1,0:T(8,128)(2,1)}, u32[]{:S(2)}) copy-start(bf16[3,3,128,256]{3,2,1,0:T(8,128)(2,1)} %kc.1) | copy-start | bytes 1769476
  24.5 27.1 %copy-start.4 = (bf16[3,3,192,64]{2,3,1,0:T(8,128)(2,1)S(1)}, bf16[3,3,192,64]{2,3,1,0:T(8,128)(2,1)}, u32[]{:S(2)}) copy-start(bf16[3,3,192,64]{2,3,1,0:T(8,128)(2,1)} %param.28) | copy-start | bytes 663556
  24.5 27.1 %copy-start.6 = (bf16[3,3,96,32]{2,3,1,0:T(8,128)(2,1)S(1)}, bf16[3,3,96,32]{2,3,1,0:T(8,128)(2,1)}, u32[]{:S(2)}) copy-start(bf16[3,3,96,32]{2,3,1,0:T(8,128)(2,1)} %param.30) | copy-start | bytes 165892
  24.5 27.1 %copy-start.9 = (bf16[32,48]{1,0:T(8,128)(2,1)S(1)}, bf16[32,48]{1,0:T(8,128)(2,1)}, u32[]{:S(2)}) copy-start(bf16[32,48]{1,0:T(8,128)(2,1)} %hk.1) | copy-start | bytes 9220
  24.5 27.1 %copy-start.10 = (f32[256]{0:T(256)S(1)}, f32[256]{0:T(256)}, u32[]{:S(2)}) copy-start(f32[256]{0:T(256)} %param.25) | copy-start | bytes 3076
  24.6 27.1 %copy-start.14 = (f32[128]{0:T(128)S(1)}, f32[128]{0:T(128)}, u32[]{:S(2)}) copy-start(f32[128]{0:T(128)} %param.27) | copy-start | bytes 1540
  24.6 27.1 %copy-start.15 = (f32[64]{0:T(128)S(1)}, f32[64]{0:T(128)}, u32[]{:S(2)}) copy-start(f32[64]{0:T(128)} %param.29) | copy-start | bytes 772
  24.6 27.1 %copy-start.16 = (f32[32]{0:T(128)S(1)}, f32[32]{0:T(128)}, u32[]{:S(2)}) copy-start(f32[32]{0:T(128)} %param.31) | copy-start | bytes 388
  24.6 27.1 %copy-start.17 = (f32[48]{0:T(128)S(1)}, f32[48]{0:T(128)}, u32[]{:S(2)}) copy-start(f32[48]{0:T(128)} %param.33) | copy-start | bytes 580
  29.6 13.3 %collective-permute-start.4 = (bf16[3,4,32,384]{3,2,1,0:T(8,128)(2,1)S(1)}, bf16[3,4,32,384]{3,2,1,0:T(8,128)(2,1)S(1)}, u32[]{:S(2)}, u32[]{:S(2)}) collective-permute-start(bf16[3,4,32,384]{3,2,1,0:T(8,128)(2,1)S(1)} %get-tuple-element.34), channel_id=1, source_target_pairs={{0,8},{8,16},{16,24},{24,32},{32,40},{40,48},{48,56},{56,64},{64,7... | collective-permute-start | bytes 884744 | tf_op jit(solution)/shard_map/ppermute | solution.py:16
  29.6 13.3 %collective-permute-start.5 = (bf16[3,4,32,384]{3,2,1,0:T(8,128)(2,1)S(1)}, bf16[3,4,32,384]{3,2,1,0:T(8,128)(2,1)S(1)}, u32[]{:S(2)}, u32[]{:S(2)}) collective-permute-start(bf16[3,4,32,384]{3,2,1,0:T(8,128)(2,1)S(1)} %get-tuple-element.35), channel_id=1, source_target_pairs={{0,120},{8,0},{16,8},{24,16},{32,24},{40,32},{48,40},{56,48},{64,5... | collective-permute-start | bytes 884744 | tf_op jit(solution)/shard_map/ppermute | solution.py:16
  46.2 12.3 %collective-permute-start.6 = (bf16[128,384]{1,0:T(8,128)(2,1)S(1)}, bf16[128,384]{1,0:T(8,128)(2,1)S(1)}, u32[]{:S(2)}, u32[]{:S(2)}) collective-permute-start(bf16[128,384]{1,0:T(8,128)(2,1)S(1)} %get-tuple-element.40.x), channel_id=1, source_target_pairs={{0,8},{8,16},{16,24},{24,32},{32,40},{40,48},{48,56},{56,64},{64,7... | collective-permute-start | bytes 294920 | tf_op jit(solution)/shard_map/ppermute | solution.py:16
  46.3 12.2 %collective-permute-start.7 = (bf16[128,384]{1,0:T(8,128)(2,1)S(1)}, bf16[128,384]{1,0:T(8,128)(2,1)S(1)}, u32[]{:S(2)}, u32[]{:S(2)}) collective-permute-start(bf16[128,384]{1,0:T(8,128)(2,1)S(1)} %get-tuple-element.40.x), channel_id=1, source_target_pairs={{0,120},{8,0},{16,8},{24,16},{32,24},{40,32},{48,40},{56,48},{64,5... | collective-permute-start | bytes 294920 | tf_op jit(solution)/shard_map/ppermute | solution.py:16
  53.1 19.6 %collective-permute-start.10 = (bf16[2,2,128,384]{3,2,1,0:T(8,128)(2,1)S(1)}, bf16[2,2,128,384]{3,2,1,0:T(8,128)(2,1)S(1)}, u32[]{:S(2)}, u32[]{:S(2)}) collective-permute-start(bf16[2,2,128,384]{3,2,1,0:T(8,128)(2,1)S(1)} %get-tuple-element.43.s3), channel_id=1, source_target_pairs={{0,8},{8,16},{16,24},{24,32},{32,40},{40,48},{48,56},{56,64},{64,7... | collective-permute-start | bytes 1179656 | tf_op jit(solution)/shard_map/ppermute | solution.py:16
  53.2 19.5 %collective-permute-start.11 = (bf16[2,2,128,384]{3,2,1,0:T(8,128)(2,1)S(1)}, bf16[2,2,128,384]{3,2,1,0:T(8,128)(2,1)S(1)}, u32[]{:S(2)}, u32[]{:S(2)}) collective-permute-start(bf16[2,2,128,384]{3,2,1,0:T(8,128)(2,1)S(1)} %get-tuple-element.43.s3), channel_id=1, source_target_pairs={{0,120},{8,0},{16,8},{24,16},{32,24},{40,32},{48,40},{56,48},{64,5... | collective-permute-start | bytes 1179656 | tf_op jit(solution)/shard_map/ppermute | solution.py:16
  59.2 13.5 %collective-permute-start.8 = (bf16[256,384]{1,0:T(8,128)(2,1)S(1)}, bf16[256,384]{1,0:T(8,128)(2,1)S(1)}, u32[]{:S(2)}, u32[]{:S(2)}) collective-permute-start(bf16[256,384]{1,0:T(8,128)(2,1)S(1)} %coarse.1.c), channel_id=1, source_target_pairs={{0,8},{8,16},{16,24},{24,32},{32,40},{40,48},{48,56},{56,64},{64,7... | collective-permute-start | bytes 589832 | tf_op jit(solution)/shard_map/ppermute | solution.py:16
  59.4 13.2 %collective-permute-start.9 = (bf16[256,384]{1,0:T(8,128)(2,1)S(1)}, bf16[256,384]{1,0:T(8,128)(2,1)S(1)}, u32[]{:S(2)}, u32[]{:S(2)}) collective-permute-start(bf16[256,384]{1,0:T(8,128)(2,1)S(1)} %coarse.1.c), channel_id=1, source_target_pairs={{0,120},{8,0},{16,8},{24,16},{32,24},{40,32},{48,40},{56,48},{64,5... | collective-permute-start | bytes 589832 | tf_op jit(solution)/shard_map/ppermute | solution.py:16
  64.8 14.7 %collective-permute-start.12 = (bf16[8,32,384]{2,1,0:T(8,128)(2,1)S(1)}, bf16[8,32,384]{2,1,0:T(8,128)(2,1)S(1)}, u32[]{:S(2)}, u32[]{:S(2)}) collective-permute-start(bf16[8,32,384]{2,1,0:T(8,128)(2,1)S(1)} %get-tuple-element.60), channel_id=1, source_target_pairs={{0,8},{8,16},{16,24},{24,32},{32,40},{40,48},{48,56},{56,64},{64,7... | collective-permute-start | bytes 589832 | tf_op jit(solution)/shard_map/ppermute | solution.py:16
  72.7 6.9 %collective-permute-start.13 = (bf16[8,32,384]{2,1,0:T(8,128)(2,1)S(1)}, bf16[8,32,384]{2,1,0:T(8,128)(2,1)S(1)}, u32[]{:S(2)}, u32[]{:S(2)}) collective-permute-start(bf16[8,32,384]{2,1,0:T(8,128)(2,1)S(1)} %get-tuple-element.59), channel_id=1, source_target_pairs={{0,120},{8,0},{16,8},{24,16},{32,24},{40,32},{48,40},{56,48},{64,5... | collective-permute-start | bytes 589832 | tf_op jit(solution)/shard_map/ppermute | solution.py:16
  79.5 4.3 %copy-start.1 = (bf16[2,48,8,1024]{3,2,1,0:T(8,128)(2,1)S(1)}, bf16[2,48,8,1024]{3,2,1,0:T(8,128)(2,1)}, u32[]{:S(2)}) copy-start(bf16[2,48,8,1024]{3,2,1,0:T(8,128)(2,1)} %param.17) | copy-start | bytes 4718596

commit v2 on v1

v2 whole, which is shorter than its diff:
```python
import jax
import jax.numpy as jnp
from jax import lax
from jax.experimental import pallas as pl
from jax.experimental.pallas import tpu as pltpu
from jax.sharding import PartitionSpec as P

LANES = 128
WIDE = 384
BF16 = jnp.bfloat16
F32 = jnp.float32


def neighbour(value, axis, step):
    size = lax.axis_size(axis)
    return lax.ppermute(value, axis, [(i, (i + step) % size) for i in range(size)])


def call(body, name, out_shapes, scratch, args, limit=16, flops=0):
    specs = [pl.BlockSpec(memory_space=pltpu.VMEM)] * len(args)
    return pl.pallas_call(
        body,
        name=name,
        out_shape=[jax.ShapeDtypeStruct(s, d) for s, d in out_shapes],
        in_specs=specs,
        out_specs=[pl.BlockSpec(memory_space=pltpu.VMEM)] * len(out_shapes),
        scratch_shapes=scratch,
        cost_estimate=pl.CostEstimate(flops=flops, transcendentals=0, bytes_accessed=0),
        compiler_params=pltpu.CompilerParams(vmem_limit_bytes=limit * 2**20),
    )(*args)


def iota(shape, axis):
    return lax.broadcasted_iota(jnp.int32, shape, axis)


def edges():
    ty, tx = lax.axis_index("ty"), lax.axis_index("tx")
    ny, nx = lax.axis_size("ty"), lax.axis_size("tx")
    inside = (ty > 0, ty < ny - 1, tx > 0, tx < nx - 1)
    return [jnp.where(side, 1.0, 0.0) for side in inside]


def one_hot(cond):
    return jnp.where(cond, 1.0, 0.0).astype(BF16)


def dot(a, b):
    return jnp.dot(a, b, preferred_element_type=F32)


def silu(t):
    return t * (0.5 * jnp.tanh(0.5 * t) + 0.5)


def lane_mask(flags):
    lane = iota((1, WIDE), 1)
    place = lane & 15
    edge = lane >= 256
    left = jnp.where(edge & (place < 4), flags[2], 1.0)
    right = jnp.where(edge & (place >= 12), flags[3], 1.0)
    return left * right


def from_left(slab):
    lane = iota((1, LANES), 1)
    h0, h1, edge = slab[:, :128], slab[:, 128:256], slab[:, 256:]
    h0 = jnp.where(lane == 0, pltpu.roll(edge, 125, 1), pltpu.roll(h0, 1, 1))
    h1 = jnp.where(lane == 0, pltpu.roll(edge, 109, 1), pltpu.roll(h1, 1, 1))
    return jnp.concatenate([h0, h1, pltpu.roll(edge, 1, 1)], axis=1)


def from_right(slab):
    lane = iota((1, LANES), 1)
    h0, h1, edge = slab[:, :128], slab[:, 128:256], slab[:, 256:]
    h0 = jnp.where(lane == 127, pltpu.roll(edge, 115, 1), pltpu.roll(h0, 127, 1))
    h1 = jnp.where(lane == 127, pltpu.roll(edge, 99, 1), pltpu.roll(h1, 127, 1))
    return jnp.concatenate([h0, h1, pltpu.roll(edge, 127, 1)], axis=1)


def fill(scratch, row, slabs, valid=None):
    phases = len(slabs)
    for p, slab in enumerate(slabs):
        if valid is not None:
            slab = jnp.where(valid > 0.5, slab, jnp.zeros_like(slab))
        scratch[row, p + 1] = slab
        if p == 0:
            scratch[row, phases + 1] = from_right(slab)
        if p == phases - 1:
            scratch[row, 0] = from_left(slab)


def window(scratch, row, phase, rows, cols):
    v = scratch[pl.ds(row, rows), phase : phase + cols]
    return v.reshape(rows * cols * v.shape[2], v.shape[3])


def side(*parts):
    return jnp.concatenate(parts, axis=1)


def pack(out, slabs):
    lane = iota((1, LANES), 1)
    count = len(slabs)
    for n, slab in enumerate(slabs):
        out[2 * n] = slab[:, :128]
        out[2 * n + 1] = slab[:, 128:256]
    for g in range(0, count, 4):
        tile = slabs[g][:, 256:]
        for n in range(1, min(4, count - g)):
            tile = jnp.where(lane < 32 * n, tile, pltpu.roll(slabs[g + n][:, 256:], 32 * n, 1))
        out[2 * count + g // 4] = tile


def unpack(packed, n, count):
    tile = packed[2 * count + n // 4]
    if n % 4:
        tile = pltpu.roll(tile, 128 - 32 * (n % 4), 1)
    return side(packed[2 * n], packed[2 * n + 1], tile)


def tiles(count):
    return 2 * count + (count + 3) // 4


def turned(part):
    rows = part.shape[0]
    i, k = iota((rows, rows), 0), iota((rows, rows), 1)
    turn = one_hot(i == (k & 7) * (rows // 8) + (k >> 3))
    return dot(turn, part).astype(BF16)


def main_kernel(x, out):
    channels = x.shape[1] // 8
    lane = iota((1, LANES), 1)
    c = iota((1, 256), 1)
    split = one_hot(iota((256, 256), 0) == 8 * (c & 31) + (c >> 5))
    for h in range(2):
        blocks = [dot(x[h, :, q * 256 : (q + 1) * 256], split).astype(BF16) for q in range(4)]
        phases = []
        for p in range(8):
            half = slice((p // 4) * 128, (p // 4 + 1) * 128)
            tile = rolled(blocks[0][:, half], -32 * (p % 4))
            for q in range(1, 4):
                tile = jnp.where(lane < 32 * q, tile, rolled(blocks[q][:, half], 32 * (q - p % 4)))
            phases.append(tile)
        for q in range(4):
            part = turned(side(phases[2 * q], phases[2 * q + 1]))
            for r in range(8):
                rows = part[r * channels : (r + 1) * channels]
                for s in range(2):
                    out[r, 2 * q + s, :, h * 128 : (h + 1) * 128] = rows[:, s * 128 : (s + 1) * 128]


def rolled(value, shift):
    return pltpu.roll(value, shift % 128, 1) if shift % 128 else value


def ends_kernel(x, main, fl, fr, out, first, last):
    flags = edges()
    lane = iota((1, LANES), 1)
    channels = x.shape[1] // 8
    ends = []
    for h in range(2):
        a = jnp.where((lane >= 96) & (flags[2] > 0.5), fl[h], jnp.where(lane < 32, x[h, :, :128], 0))
        b = jnp.where(lane >= 96, x[h, :, 896:], jnp.where((lane < 32) & (flags[3] > 0.5), fr[h], 0))
        ends += [a.astype(BF16), b.astype(BF16)]
    ends = side(*ends)
    c = iota((1, 256), 1)
    row = 128 * ((c & 31) >> 3) + (((8 * (c & 7) + (c >> 5)) + 96) & 127)
    part = turned(dot(ends, one_hot(iota((512, 256), 0) == row)).astype(BF16))
    for r in range(8):
        rows = part[r * channels : (r + 1) * channels]
        for p in range(8):
            tile = rows[:, (p // 4) * 128 : (p // 4 + 1) * 128]
            out[r, p] = pltpu.roll(tile, 128 - 32 * (p % 4), 1) if p % 4 else tile
        if r in (0, 7):
            ref = first if r == 0 else last
            for p in range(8):
                ref[2 * p] = main[r, p, :, :128]
                ref[2 * p + 1] = main[r, p, :, 128:]
            ref[16] = rows[:, :128]
            ref[17] = rows[:, 128:]


def field_slabs(main, ends, r):
    return [side(main[r, p], ends[r, p]) for p in range(8)]


def conv_rows(xs, w, bias, row, q, group=1):
    rhs = side(*[window(xs, row, 2 * q + s, group + 2, 3) for s in range(2)])
    res = dot(w, rhs)
    size = bias.shape[0]
    return {
        (r, s): silu(res[r * size : (r + 1) * size, s * WIDE : (s + 1) * WIDE] + bias)
        for r in range(group)
        for s in range(2)
    }


def inner_kernel(main, ends, w, b, skip, pooled, xs):
    flags = edges()
    for r in range(8):
        fill(xs, r, field_slabs(main, ends, r))
    mask = lane_mask(flags)
    bias = b[...]

    def one(k, carry):
        for q in range(4):
            for (r, s), y in conv_rows(xs, w[...], bias, 3 * k, q, 3).items():
                skip[3 * k + r, 2 * q + s] = (y * mask).astype(BF16)
        return carry

    lax.fori_loop(0, 2, one, 0)
    for k in range(2):
        for q in range(4):
            pooled[k, q] = mean([skip[2 * k + 1 + r, 2 * q + s] for r in range(2) for s in range(2)])


def mean(slabs):
    total = slabs[0].astype(F32)
    for slab in slabs[1:]:
        total = total + slab.astype(F32)
    return (total * 0.25).astype(BF16)


def outer_kernel(
    main, ends, above, below, skip_in, pooled_in, w, b, skip, pooled, p_first, p_last, xs
):
    flags = edges()
    fill(xs, 0, [unpack(above, p, 8) for p in range(8)], flags[0])
    for n, r in enumerate((0, 1)):
        fill(xs, 1 + n, field_slabs(main, ends, r))
    for n, r in enumerate((6, 7)):
        fill(xs, 3 + n, field_slabs(main, ends, r))
    fill(xs, 5, [unpack(below, p, 8) for p in range(8)], flags[1])
    mask = lane_mask(flags)
    bias = b[...]

    def one(k, carry):
        for q in range(4):
            for (r, s), y in conv_rows(xs, w[...], bias, 3 * k, q).items():
                skip[k, 2 * q + s] = (y * mask).astype(BF16)
        return carry

    lax.fori_loop(0, 2, one, 0)
    for q in range(4):
        pooled[0, q] = mean([src[0, 2 * q + s] for src in (skip, skip_in) for s in range(2)])
        far = [skip_in[5, 2 * q + s] for s in range(2)] + [skip[1, 2 * q + s] for s in range(2)]
        pooled[1, q] = mean(far)
    rows = [[ref[k, q] for q in range(4)] for ref, k in ((pooled, 0), (pooled_in, 0), (pooled_in, 1), (pooled, 1))]
    pack(p_first, rows[0] + rows[1] + rows[2])
    pack(p_last, rows[1] + rows[2] + rows[3])


def two_kernel(pooled_in, pooled, above, below, w2, b2, skip2, pooled2, first, last, xs):
    flags = edges()
    for r in range(3):
        fill(xs, r, [unpack(above, 4 * r + p, 12) for p in range(4)], flags[0])
        fill(xs, r + 7, [unpack(below, 4 * r + p, 12) for p in range(4)], flags[1])
    for n, (ref, r) in enumerate(((pooled, 0), (pooled_in, 0), (pooled_in, 1), (pooled, 1))):
        fill(xs, n + 3, [ref[r, p] for p in range(4)])
    mask = lane_mask(flags)
    bias = b2[...]

    def pair(k, carry):
        valid = jnp.where(k == 0, flags[0], jnp.where(k == 3, flags[1], 1.0))
        inside = mask * valid
        for q in range(2):
            slabs = []
            for (r, s), y in conv_rows(xs, w2[...], bias, 2 * k, q, 2).items():
                y = (y * inside).astype(BF16)
                skip2[2 * k + r, 2 * q + s] = y
                slabs.append(y)
            pooled2[k, q] = mean(slabs)
        return carry

    lax.fori_loop(0, 4, pair, 0)
    pack(first, [pooled2[r, p] for r in (2, 3) for p in range(2)])
    pack(last, [pooled2[r, p] for r in (0, 1) for p in range(2)])


def three_kernel(pooled2, above, below, w3, b3, wc, bc, skip3, coarse, send, xs, xc):
    flags = edges()
    for r in range(2):
        fill(xs, r, [unpack(above, 2 * r + p, 4) for p in range(2)], flags[0])
        fill(xs, r + 6, [unpack(below, 2 * r + p, 4) for p in range(2)], flags[1])
    for r in range(4):
        fill(xs, r + 2, [pooled2[r, p] for p in range(2)])
    mask = lane_mask(flags)
    for k in range(3):
        inside = mask * (flags[0] if k == 0 else flags[1]) if k != 1 else mask
        slabs = []
        for r in range(2):
            for (_, p), y in conv_rows(xs, w3[...], b3[...], 2 * k + r, 0).items():
                y = (y * inside).astype(BF16)
                skip3[2 * k + r, p] = y
                slabs.append(y)
        fill(xc, k, [mean(slabs)])
    res = silu(dot(wc[...], window(xc, 0, 0, 3, 3)) + bc[...])
    res = (res * mask).astype(BF16)
    coarse[...] = res
    size = res.shape[0] // 4
    pack(send, [res[n * size : (n + 1) * size] for n in range(4)])


def skip_three_kernel(s3, w, b, out, xs):
    for r in range(6):
        fill(xs, r, [s3[r, p] for p in range(2)])
    for r in range(4):
        res = dot(w[...], side(*[window(xs, r, p, 3, 3) for p in range(2)]))
        for p in range(2):
            out[r, p] = res[:, p * WIDE : (p + 1) * WIDE] + b[...]


def skip_two_kernel(s2, s_out, w, b, out, first, last, xs):
    for r in range(8):
        fill(xs, r, [s2[r, p] for p in range(4)])
    bias = b[...]

    def pair(k, carry):
        for q in range(2):
            res = dot(w[...], side(*[window(xs, 2 * k, 2 * q + s, 4, 3) for s in range(2)]))
            for r in range(2):
                for s in range(2):
                    part = res[r * bias.shape[0] : (r + 1) * bias.shape[0]]
                    out[2 * k + r, 2 * q + s] = part[:, s * WIDE : (s + 1) * WIDE] + bias
        return carry

    lax.fori_loop(0, 3, pair, 0)
    pack(first, [s_out[0, p] for p in range(8)])
    pack(last, [s_out[1, p] for p in range(8)])


def skip_inner_kernel(s_in, s_out, w, b, out, xs):
    fill(xs, 0, [s_out[0, p] for p in range(8)])
    for r in range(6):
        fill(xs, r + 1, [s_in[r, p] for p in range(8)])
    fill(xs, 7, [s_out[1, p] for p in range(8)])
    size = b.shape[0]
    for k in range(2):
        for p in range(8):
            res = dot(w[...], window(xs, 3 * k, p, 5, 3)[:, :256])
            for r in range(3):
                out[3 * k + r, p] = res[r * size : (r + 1) * size] + b[...]


def skip_outer_kernel(s_in, s_out, above, below, w, b, out, xs):
    flags = edges()
    fill(xs, 0, [unpack(above, p, 8) for p in range(8)], flags[0])
    for n, (ref, r) in enumerate(((s_out, 0), (s_in, 0), (s_in, 5), (s_out, 1))):
        fill(xs, n + 1, [ref[r, p] for p in range(8)])
    fill(xs, 5, [unpack(below, p, 8) for p in range(8)], flags[1])
    for k in range(2):
        for p in range(8):
            out[k, p] = dot(w[...], window(xs, 3 * k, p, 3, 3)[:, :256]) + b[...]


def back_kernel(c, above, below, pre3, pre2, wu3, wu2, out, xc, xb):
    flags = edges()
    halo = lambda packed: [jnp.concatenate([unpack(packed, n, 4) for n in range(4)], axis=0)]
    fill(xc, 0, halo(above), flags[0])
    fill(xc, 1, [c[...]])
    fill(xc, 2, halo(below), flags[1])
    mask = lane_mask(flags)
    slabs = {}
    for a in range(2):
        for p in range(2):
            res = dot(wu3[a, p], side(window(xc, 0, p, 2, 2), window(xc, 1, p, 2, 2)))
            for n in range(2):
                r = 2 * n + 1 - a
                y = silu(res[:, n * WIDE : (n + 1) * WIDE] + pre3[r, p])
                inside = mask * flags[0] if r == 0 else mask * flags[1] if r == 3 else mask
                slabs[r, p] = (y * inside).astype(BF16)
    for r in range(4):
        fill(xb, r, [slabs[r, p] for p in range(2)])

    def pair(k, carry):
        for b in range(2):
            rhs = side(*[window(xb, k, (p + 1) // 2, 2, 2) for p in (b, b + 2)])
            res = dot(wu2[b], rhs)
            size = res.shape[0] // 2
            for i in range(2):
                valid = jnp.where(
                    (k == 0) & (i == 0), flags[0], jnp.where((k == 2) & (i == 1), flags[1], 1.0)
                )
                inside = mask * valid
                rows = res[i * size : (i + 1) * size]
                for n in range(2):
                    y = silu(rows[:, n * WIDE : (n + 1) * WIDE] + pre2[2 * k + i, b + 2 * n])
                    out[2 * k + i, b + 2 * n] = (y * inside).astype(BF16)
        return carry

    lax.fori_loop(0, 3, pair, 0)


def last_kernel(bt, pre_in, pre_out, wu, out, xb):
    for r in range(6):
        fill(xb, r, [bt[r, p] for p in range(4)])
    size = wu.shape[0] // 4
    for k in range(5):
        for m in range(5):
            res = dot(wu[...], window(xb, k, m, 2, 2)[:, :256])
            for i in range(2):
                for j in range(2):
                    r, p = 2 * k - 1 + i, 2 * m - 1 + j
                    if not (0 <= r < 8 and 0 <= p < 8):
                        continue
                    pre = pre_out[0, p] if r == 0 else pre_out[1, p] if r == 7 else pre_in[r - 1, p]
                    n = 2 * (1 - i) + 1 - j
                    y = silu(res[n * size : (n + 1) * size] + pre).astype(BF16)
                    for h in range(2):
                        lanes = slice(h * 128, (h + 1) * 128)
                        out[h, r, :, p * 128 : (p + 1) * 128] = y[:, lanes]


def head_kernel_body(back, fields, w, offset, out, buf, sems):
    lane = iota((1, LANES), 1)
    c = iota((1, 256), 1)
    merge = one_hot(iota((256, 256), 0) == 32 * (c & 7) + (c >> 3))
    copies = []
    for h in range(2):
        for half in range(2):
            blocks = []
            for q in (2 * half, 2 * half + 1):
                pieces = []
                for g in range(2):
                    tile = rolled(back[h, :, g * 512 : g * 512 + 128], -32 * q)
                    for n in range(1, 4):
                        start = g * 512 + n * 128
                        piece = rolled(back[h, :, start : start + 128], 32 * (n - q))
                        tile = jnp.where(lane < 32 * n, tile, piece)
                    pieces.append(tile)
                blocks.append(dot(side(*pieces), merge).astype(BF16))
            cols = slice(half * 512, (half + 1) * 512)
            base = fields[h, :, cols].astype(F32) + side(offset[...], offset[...])
            buf[h, :, cols] = base + dot(w[...], side(*blocks))
            n = 2 * h + half
            copies.append(pltpu.make_async_copy(buf.at[h, :, cols], out.at[h, :, cols], sems.at[n]))
            copies[n].start()
    for copy in copies:
        copy.wait()


def flip(value):
    eye = one_hot(iota((value.shape[1],) * 2, 0) == iota((value.shape[1],) * 2, 1))
    dims = (((1,), (1,)), ((), ()))
    return lax.dot_general(eye, value, dims, preferred_element_type=F32).astype(BF16)


def column(row, width, repeat=1):
    size = row.shape[1]
    i, j = iota((size * repeat, size), 0), iota((size * repeat, size), 1)
    col = jnp.sum(jnp.where(i // repeat == j, row, 0.0), axis=1, keepdims=True)
    return jnp.broadcast_to(col, (size * repeat, width))


def sums(a):
    return ((0,), (1, 2)) if a == 0 else ((0, 1), (2,))


def summed(tap, a, b, i, j):
    total = None
    for dy in sums(a)[i]:
        for dx in sums(b)[j]:
            value = tap(dy, dx).astype(F32)
            total = value if total is None else total + value
    return total.astype(BF16)


def placed(parts, width):
    size = parts[0].shape[1]
    total = None
    for n, part in enumerate(parts):
        spot = one_hot(iota((size, width), 1) == iota((size, width), 0) + n * size)
        value = dot(part, spot)
        total = value if total is None else total + value
    return total.astype(BF16)


def grouped(w, rows):
    size, step = w.shape[1], w.shape[1] // 3
    width = step * (rows + 2)
    i, j = iota((size, width), 0), iota((size, width), 1)
    parts = [dot(w, one_hot(j == i + n * step)).astype(BF16) for n in range(rows)]
    return jnp.concatenate(parts, axis=0)


NINE = [(dy, dx) for dy in range(3) for dx in range(3)]
FOUR = [(i, j) for i in range(2) for j in range(2)]


def early_kernel(k1, k2, k3, r1, r2, r3, w1, g1, w2, w3, b1, b2, b3):
    w1[...] = placed([k1[n] for n in NINE], w1.shape[1])
    g1[...] = grouped(w1[...], 3)
    w2[...] = grouped(flip(k2[...].reshape(-1, k2.shape[3])), 2)
    w3[...] = flip(k3[...].reshape(-1, k3.shape[3]))
    for r, b in ((r1, b1), (r2, b2), (r3, b3)):
        b[...] = column(r[...], WIDE)


def late_kernel(
    kc, d3, d2, d1, hk, rc, r3, r2, r1, rh, wc, wu3, ws3, wu2, gs2, wu1, ws1, gs1, wh, bc, b3, b2, b1, bh
):
    wc[...] = flip(kc[...].reshape(-1, kc.shape[3]))
    for r, b in ((rc, bc), (r3, b3), (r2, b2), (r1, b1)):
        b[...] = column(r[...], b.shape[1])
    bh[...] = column(rh[...], bh.shape[1], 8)
    up3, up2, up1 = wu3.shape[3] // 4, wu2.shape[2] // 4, wu1.shape[1] // 4
    n2, n1 = d2.shape[2], d1.shape[2]
    for a in range(2):
        for b in range(2):
            tall = [summed(lambda y, x: d3[y, x, :up3, :], a, b, i, j) for i, j in FOUR]
            wu3[a, b] = flip(jnp.concatenate(tall, axis=0))
            wide = [summed(lambda y, x: d2[y, x, :, :up2], a, b, i, j) for i, j in FOUR]
            wu2[b, (1 - a) * n2 : (2 - a) * n2] = jnp.concatenate(wide, axis=1)
            wide = [summed(lambda y, x: d1[y, x, :, :up1], a, b, i, j) for i, j in FOUR]
            wu1[(2 * a + b) * n1 : (2 * a + b + 1) * n1] = placed(wide, wu1.shape[1])
    ws3[...] = flip(jnp.concatenate([d3[y, x, up3:, :] for y, x in NINE], axis=0))
    skips = [d2[y, x, :, up2:] for y, x in NINE]
    gs2[...] = grouped(placed(skips, 9 * skips[0].shape[1]), 2)
    ws1[...] = placed([d1[y, x, :, up1:] for y, x in NINE], ws1.shape[1])
    gs1[...] = grouped(ws1[...], 3)
    v, c = hk.shape[1], hk.shape[0]
    spread = one_hot(iota((v * 8, v), 0) // 8 == iota((v * 8, v), 1))
    dims = (((1,), (1,)), ((), ()))
    tall = lax.dot_general(spread, hk[...], dims, preferred_element_type=F32).astype(BF16)
    i, k = iota((v * 8, 8 * c), 0), iota((v * 8, 8 * c), 1)
    tiled = dot(tall, one_hot(iota((c, 8 * c), 0) == iota((c, 8 * c), 1) % c))
    wh[...] = jnp.where(i % 8 == k // c, tiled, 0.0).astype(BF16)


def body(
    fields,
    kernel_one,
    bias_one,
    kernel_two,
    bias_two,
    kernel_three,
    bias_three,
    kernel_coarse,
    bias_coarse,
    decode_three,
    offset_three,
    decode_two,
    offset_two,
    decode_one,
    offset_one,
    head_kernel,
    head_offset,
):
    c1, c2, c3, c4 = (k.shape[3] for k in (kernel_one, kernel_two, kernel_three, kernel_coarse))
    v = fields.shape[1]

    x = fields.reshape(2, v * 8, 1024)
    from_l = neighbour(x[:, :, 896:], "tx", 1)
    from_r = neighbour(x[:, :, :128], "tx", -1)

    def up(value):
        return neighbour(value, "ty", -1)

    def down(value):
        return neighbour(value, "ty", 1)

    row = lambda bias: bias[None, :]
    swap = lambda kernel: jnp.transpose(kernel, (0, 1, 3, 2))
    weights = lambda *shape: (shape, BF16)
    biases = lambda size, width=WIDE: ((size, width), F32)
    w1, g1, w2, w3, b1, b2, b3 = call(
        early_kernel,
        "early",
        [weights(c1, 9 * v), weights(3 * c1, 15 * v), weights(2 * c2, 12 * c1), weights(c3, 9 * c2)]
        + [biases(c1), biases(c2), biases(c3)],
        [],
        [swap(kernel_one), kernel_two, kernel_three, row(bias_one), row(bias_two), row(bias_three)],
    )
    wc, wu3, ws3, wu2, gs2, wu1, ws1, gs1, wh, bc, ob3, ob2, ob1, bh = call(
        late_kernel,
        "late",
        [weights(c4, 9 * c3), weights(2, 2, c3, 4 * c4), weights(c3, 9 * c3)]
        + [weights(2, 2 * c2, 4 * c3), weights(2 * c2, 12 * c2)]
        + [weights(4 * c1, 4 * c2), weights(c1, 9 * c1), weights(3 * c1, 15 * c1)]
        + [weights(8 * v, 8 * c1)]
        + [biases(c4), biases(c3), biases(c2), biases(c1, 256), biases(8 * v, 256)],
        [],
        [kernel_coarse, decode_three, swap(decode_two), swap(decode_one), head_kernel]
        + [row(b) for b in (bias_coarse, offset_three, offset_two, offset_one, head_offset)],
        flops=5 * 10**8,
    )
    (main,) = call(main_kernel, "main", [((8, 8, v, 256), BF16)], [], [x], flops=10**9)
    packed = lambda count, size: ((tiles(count), size, LANES), BF16)
    ends, f_first, f_last = call(
        ends_kernel,
        "ends",
        [((8, 8, v, LANES), BF16), packed(8, v), packed(8, v)],
        [],
        [x, main, from_l, from_r],
    )
    f_above, f_below = down(f_last), up(f_first)
    s_in, p_in = call(
        inner_kernel,
        "inner",
        [((6, 8, c1, WIDE), BF16), ((2, 4, c1, WIDE), BF16)],
        [pltpu.VMEM((8, 10, v, WIDE), BF16)],
        [main, ends, g1, b1],
        flops=10**9,
    )
    s_out, p_out, p_first, p_last = call(
        outer_kernel,
        "outer",
        [((2, 8, c1, WIDE), BF16), ((2, 4, c1, WIDE), BF16)]
        + [packed(12, c1)] * 2,
        [pltpu.VMEM((6, 10, v, WIDE), BF16)],
        [main, ends, f_above, f_below, s_in, p_in, w1, b1],
    )
    p_above, p_below = down(p_last), up(p_first)
    s2, p2, q_first, q_last = call(
        two_kernel,
        "two",
        [((8, 4, c2, WIDE), BF16), ((4, 2, c2, WIDE), BF16), packed(4, c2), packed(4, c2)],
        [pltpu.VMEM((10, 6, c1, WIDE), BF16)],
        [p_in, p_out, p_above, p_below, w2, b2],
    )
    q_above, q_below = down(q_last), up(q_first)
    pre2, s_first, s_last = call(
        skip_two_kernel,
        "skip_two",
        [((6, 4, c2, WIDE), F32), packed(8, c1), packed(8, c1)],
        [pltpu.VMEM((8, 6, c2, WIDE), BF16)],
        [s2, s_out, gs2, ob2],
        flops=10**9,
    )
    s_above, s_below = down(s_last), up(s_first)
    s3, coarse, c_send = call(
        three_kernel,
        "three",
        [((6, 2, c3, WIDE), BF16), ((c4, WIDE), BF16), packed(4, c4 // 4)],
        [pltpu.VMEM((8, 4, c2, WIDE), BF16), pltpu.VMEM((3, 3, c3, WIDE), BF16)],
        [p2, q_above, q_below, w3, b3, wc, bc],
    )
    c_above, c_below = down(c_send), up(c_send)
    (pre_in,) = call(
        skip_inner_kernel,
        "skip_inner",
        [((6, 8, c1, 256), F32)],
        [pltpu.VMEM((8, 10, c1, WIDE), BF16)],
        [s_in, s_out, gs1, ob1],
        flops=10**9,
    )
    (pre_out,) = call(
        skip_outer_kernel,
        "skip_outer",
        [((2, 8, c1, 256), F32)],
        [pltpu.VMEM((6, 10, c1, WIDE), BF16)],
        [s_in, s_out, s_above, s_below, ws1, ob1],
        flops=5 * 10**8,
    )
    (pre3,) = call(
        skip_three_kernel,
        "skip_three",
        [((4, 2, c3, WIDE), F32)],
        [pltpu.VMEM((6, 4, c3, WIDE), BF16)],
        [s3, ws3, ob3],
        flops=10**9,
    )
    (back_two,) = call(
        back_kernel,
        "back",
        [((6, 4, c2, WIDE), BF16)],
        [pltpu.VMEM((3, 3, c4, WIDE), BF16), pltpu.VMEM((4, 4, c3, WIDE), BF16)],
        [coarse, c_above, c_below, pre3, pre2, wu3, wu2],
    )
    (back_one,) = call(
        last_kernel,
        "last",
        [((2, 8, c1, 1024), BF16)],
        [pltpu.VMEM((6, 6, c2, WIDE), BF16)],
        [back_two, pre_in, pre_out, wu1],
    )
    out = pl.pallas_call(
        head_kernel_body,
        name="head",
        out_shape=jax.ShapeDtypeStruct((2, v * 8, 1024), F32),
        in_specs=[pl.BlockSpec(memory_space=pltpu.VMEM)] * 4,
        out_specs=pl.BlockSpec(memory_space=pl.ANY),
        scratch_shapes=[pltpu.VMEM((2, v * 8, 1024), F32), pltpu.SemaphoreType.DMA((4,))],
        compiler_params=pltpu.CompilerParams(vmem_limit_bytes=16 * 2**20),
    )(back_one.reshape(2, 8 * c1, 1024), x, wh, bh)
    return out.reshape(2, v, 8, 1024)


def solution(mesh):
    return jax.shard_map(
        body,
        mesh=mesh,
        in_specs=(P(None, None, "ty", "tx"),) + (P(),) * 16,
        out_specs=P(None, None, "ty", "tx"),
        check_vma=False,
    )
```

time: 90.5 us -> 67.7 us (0.75)
  waiting for transfers between devices: 25.2 us -> 13.2 us
  Pallas kernels: 31 us -> 25 us
  starting transfers between devices: 30.4 us -> 25.6 us
    ppermute x14 -> x12, waiting for transfers between devices: 25.2 us -> 13.2 us  [neighbour(): lax.ppermute(value, axis, [(i, (i + step) % size) for i in range(size)])]
    ppermute x14 -> x12, starting transfers between devices: 30.4 us -> 25.6 us  [neighbour(): lax.ppermute(value, axis, [(i, (i + step) % size) for i in range(size)])]
    pallas_call x1, Pallas kernels: 5.69 us -> 2.55 us  [body(): pl.pallas_call(head_kernel_body, name='head', out_shape=jax.ShapeDtypeStr...]
    pallas_call x8 -> x14, Pallas kernels: 25.3 us -> 22.5 us  [call(): pl.pallas_call(body, name=name, out_shape=[jax.ShapeDtypeStruct(s, d) for...]
  transfers between devices with their start and end apart: 14 -> 12, of which waited for: 4 -> 5; matrix products, arithmetic and copies ran while one was open for 0% -> 0% of each run, Pallas kernels for 10% -> 20%
where the time goes in v2:
time: 67.7 us; the launch traced here: 67.5 us
  starting transfers between devices  25.6 us (38%)
  Pallas kernels  25 us (37%)
  waiting for transfers between devices  13.2 us (19%)
  local copies, waits for them, and re-layouts  3.17 us (5%)
    ppermute x12, starting transfers between devices, neighbour(): lax.ppermute(value, axis, [(i, (i + step) % size) for i in range(size)])  25.6 us
    pallas_call x14, Pallas kernels, call(): pl.pallas_call(body, name=name, out_shape=[jax.ShapeDtypeStruct(s, d) for...  22.5 us
    ppermute x12, waiting for transfers between devices, neighbour(): lax.ppermute(value, axis, [(i, (i + step) % size) for i in range(size)])  13.2 us
    pallas_call x1, Pallas kernels, body(): pl.pallas_call(head_kernel_body, name='head', out_shape=jax.ShapeDtypeStr...  2.55 us
    unnamed x36, local copies, waits for them, and re-layouts  2.11 us
  transfers between devices with their start and end apart: 12, of which 5 were waited for; matrix products, arithmetic and copies ran while one was open for 0% of the time, Pallas kernels for 20%

profile of v2, /device:TPU:24, one launch (start us, length us, event | category | flops | bytes accessed | tf_op | source)
XLA Modules:
  0.0 67.5 jit_solution(16249567814145248193)
XLA Ops:
  0.0 1.1 %fusion = (bf16[2,384,128]{2,1,0:T(8,128)(2,1)S(1)}, bf16[2,384,128]{2,1,0:T(8,128)(2,1)S(1)}) fusion(bf16[2,384,1024]{2,1,0:T(8,128)(2,1)} %bitcast.14), kind=kLoop, calls=%fused_computation | loop fusion | bytes 786432 | tf_op jit(solution)/shard_map/slice | solution.py:557
  1.1 0.2 collective-permute-start.1
  1.3 0.3 collective-permute-start
  1.6 1.4 %copy-done = bf16[2,48,8,1024]{3,2,1,0:T(8,128)(2,1)S(1)} copy-done((bf16[2,48,8,1024]{3,2,1,0:T(8,128)(2,1)S(1)}, bf16[2,48,8,1024]{3,2,1,0:T(8,128)(2,1)}, u32[]{:S(2)}) %copy-start) | copy-done | bytes 1572888
  3.0 2.0 %main.1 = bf16[8,8,48,256]{3,2,1,0:T(8,128)(2,1)S(1)} custom-call(bf16[2,384,1024]{2,1,0:T(8,128)(2,1)S(1)} %bitcast.15), custom_call_target="tpu_custom_call" | custom-call | flops 1000000000 | tf_op jit(solution)/shard_map/main/pallas_call | solution.py:21
  5.1 1.3 %collective-permute-done.fl = bf16[2,384,128]{2,1,0:T(8,128)(2,1)S(1)} collective-permute-done((bf16[2,384,128]{2,1,0:T(8,128)(2,1)S(1)}, bf16[2,384,128]{2,1,0:T(8,128)(2,1)S(1)}, u32[]{:S(2)}, u32[]{:S(2)}) %collective-permute-start) | collective-permute-done | bytes 196640 | tf_op jit(solution)/shard_map/ppermute | solution.py:16
  6.3 0.8 %ends.1 = (bf16[8,8,48,128]{3,2,1,0:T(8,128)(2,1)S(1)}, bf16[18,48,128]{2,1,0:T(8,128)(2,1)S(1)}, bf16[18,48,128]{2,1,0:T(8,128)(2,1)S(1)}) custom-call(bf16[2,384,1024]{2,1,0:T(8,128)(2,1)S(1)} %bitcast.16, bf16[8,8,48,256]{3,2,1,0:T(8,128)(2,1)S(1)} %main.1, bf16[2,384,128]{2,1,0:T(8,128)(2,1)S(1)} %collective-permute-done.fl, ...), custom_call_target="tpu_custom_call" | custom-call | tf_op jit(solution)/shard_map/ends/pallas_call | solution.py:21
  7.1 1.6 %collective-permute-start.2 = (bf16[18,48,128]{2,1,0:T(8,128)(2,1)S(1)}, bf16[18,48,128]{2,1,0:T(8,128)(2,1)S(1)}, u32[]{:S(2)}, u32[]{:S(2)}) collective-permute-start(bf16[18,48,128]{2,1,0:T(8,128)(2,1)S(1)} %get-tuple-element.49), channel_id=1, source_target_pairs={{0,8},{8,16},{16,24},{24,32},{32,40},{40,48},{48,56},{56,64},{64,7... | collective-permute-start | bytes 663560 | tf_op jit(solution)/shard_map/ppermute | solution.py:16
  8.7 4.8 %collective-permute-start.3 = (bf16[18,48,128]{2,1,0:T(8,128)(2,1)S(1)}, bf16[18,48,128]{2,1,0:T(8,128)(2,1)S(1)}, u32[]{:S(2)}, u32[]{:S(2)}) collective-permute-start(bf16[18,48,128]{2,1,0:T(8,128)(2,1)S(1)} %get-tuple-element.50), channel_id=1, source_target_pairs={{0,120},{8,0},{16,8},{24,16},{32,24},{40,32},{48,40},{56,48},{64,5... | collective-permute-start | bytes 663560 | tf_op jit(solution)/shard_map/ppermute | solution.py:16
  13.5 0.8 %early.1 = (bf16[32,432]{1,0:T(8,128)(2,1)S(1)}, bf16[96,720]{1,0:T(8,128)(2,1)S(1)}, bf16[128,384]{1,0:T(8,128)(2,1)S(1)}, bf16[128,576]{1,0:T(8,128)(2,1)S(1)}...) custom-call(bf16[3,3,32,48]{3,2,1,0:T(8,128)(2,1)S(1)} %bitcast.21, ...), custom_call_target="tpu_custom_call" | custom-call | tf_op jit(solution)/shard_map/early/pallas_call | solution.py:21
  14.3 2.3 %inner.1 = (bf16[6,8,32,384]{3,2,1,0:T(8,128)(2,1)S(1)}, bf16[2,4,32,384]{3,2,1,0:T(8,128)(2,1)S(1)}) custom-call(bf16[8,8,48,256]{3,2,1,0:T(8,128)(2,1)S(1)} %main.1, bf16[8,8,48,128]{3,2,1,0:T(8,128)(2,1)S(1)} %get-tuple-element.45.ends, bf16[96,720]{1,0:T(8,128)(2,1)S(1)} %get-tuple-element.46.w, f32[32,384]{1,0:T(8,128)S(1)} %get-tuple-element.47.b), custom_call_target="tpu_custom_call" | custom-call | flops 1000000000 | tf_op jit(solution)/shard_map/inner/pallas_call | solution.py:21
  16.6 2.7 %collective-permute-done.2.above = bf16[18,48,128]{2,1,0:T(8,128)(2,1)S(1)} collective-permute-done((bf16[18,48,128]{2,1,0:T(8,128)(2,1)S(1)}, bf16[18,48,128]{2,1,0:T(8,128)(2,1)S(1)}, u32[]{:S(2)}, u32[]{:S(2)}) %collective-permute-start.2) | collective-permute-done | bytes 221216 | tf_op jit(solution)/shard_map/ppermute | solution.py:16
  19.4 1.8 %outer.1 = (bf16[2,8,32,384]{3,2,1,0:T(8,128)(2,1)S(1)}, bf16[2,4,32,384]{3,2,1,0:T(8,128)(2,1)S(1)}, bf16[27,32,128]{2,1,0:T(8,128)(2,1)S(1)}, bf16[27,32,128]{2,1,0:T(8,128)(2,1)S(1)}) custom-call(bf16[8,8,48,256]{3,2,1,0:T(8,128)(2,1)S(1)} %main.1, bf16[8,8,48,128]{3,2,1,0:T(8,128)(2,1)S(1)} %get-tuple-element.45.ends, ...), custom_call_target="tpu_custom_call" | custom-call | tf_op jit(solution)/shard_map/outer/pallas_call | solution.py:21
  21.2 0.1 collective-permute-start.4
  21.3 5.8 %collective-permute-start.5 = (bf16[27,32,128]{2,1,0:T(8,128)(2,1)S(1)}, bf16[27,32,128]{2,1,0:T(8,128)(2,1)S(1)}, u32[]{:S(2)}, u32[]{:S(2)}) collective-permute-start(bf16[27,32,128]{2,1,0:T(8,128)(2,1)S(1)} %get-tuple-element.55), channel_id=1, source_target_pairs={{0,120},{8,0},{16,8},{24,16},{32,24},{40,32},{48,40},{56,48},{64,5... | collective-permute-start | bytes 663560 | tf_op jit(solution)/shard_map/ppermute | solution.py:16
  27.0 5.6 %collective-permute-done.4.above = bf16[27,32,128]{2,1,0:T(8,128)(2,1)S(1)} collective-permute-done((bf16[27,32,128]{2,1,0:T(8,128)(2,1)S(1)}, bf16[27,32,128]{2,1,0:T(8,128)(2,1)S(1)}, u32[]{:S(2)}, u32[]{:S(2)}) %collective-permute-start.4) | collective-permute-done | bytes 221216 | tf_op jit(solution)/shard_map/ppermute | solution.py:16
  32.7 2.6 %two.1 = (bf16[8,4,64,384]{3,2,1,0:T(8,128)(2,1)S(1)}, bf16[4,2,64,384]{3,2,1,0:T(8,128)(2,1)S(1)}, bf16[9,64,128]{2,1,0:T(8,128)(2,1)S(1)}, bf16[9,64,128]{2,1,0:T(8,128)(2,1)S(1)}) custom-call(bf16[2,4,32,384]{3,2,1,0:T(8,128)(2,1)S(1)} %get-tuple-element.48.pooled_in, bf16[2,4,32,384]{3,2,1,0:T(8,128)(2,1)S(1)} %get-tuple-element.53.pooled, ...), custom_call_target="tpu_custom_call" | custom-call | tf_op jit(solution)/shard_map/two/pallas_call | solution.py:21
  35.3 5.3 %collective-permute-start.7 = (bf16[9,64,128]{2,1,0:T(8,128)(2,1)S(1)}, bf16[9,64,128]{2,1,0:T(8,128)(2,1)S(1)}, u32[]{:S(2)}, u32[]{:S(2)}) collective-permute-start(bf16[9,64,128]{2,1,0:T(8,128)(2,1)S(1)} %get-tuple-element.60), channel_id=1, source_target_pairs={{0,120},{8,0},{16,8},{24,16},{32,24},{40,32},{48,40},{56,48},{64,5... | collective-permute-start | bytes 442376 | tf_op jit(solution)/shard_map/ppermute | solution.py:16
  40.7 1.9 %late.1 = (bf16[256,1152]{1,0:T(8,128)(2,1)S(1)}, bf16[2,2,128,1024]{3,2,1,0:T(8,128)(2,1)S(1)}, bf16[128,1152]{1,0:T(8,128)(2,1)S(1)}, bf16[2,128,512]{2,1,0:T(...) custom-call(bf16[3,3,128,256]{3,2,1,0:T(8,128)(2,1)S(1)} %copy-done., ...), custom_call_target="tpu_custom_call" | custom-call | flops 500000000 | tf_op jit(solution)/shard_map/late/pallas_call | solution.py:21
  42.7 2.0 %skip_two.1 = (f32[6,4,64,384]{3,2,1,0:T(8,128)S(1)}, bf16[18,32,128]{2,1,0:T(8,128)(2,1)S(1)}, bf16[18,32,128]{2,1,0:T(8,128)(2,1)S(1)}) custom-call(bf16[8,4,64,384]{3,2,1,0:T(8,128)(2,1)S(1)} %get-tuple-element.70.s2, bf16[2,8,32,384]{3,2,1,0:T(8,128)(2,1)S(1)} %get-tuple-element.71.s_out, bf16[128,768]{1,0:T(8,128)(2,1)S(1)} %get-tuple-element.72.w, ...), custom_call_target="tpu_custom_call" | custom-call | flops 1000000000 | tf_op jit(solution)/shard_map/skip_two/pallas_call | solution.py:21
  44.8 5.3 %collective-permute-start.11 = (bf16[18,32,128]{2,1,0:T(8,128)(2,1)S(1)}, bf16[18,32,128]{2,1,0:T(8,128)(2,1)S(1)}, u32[]{:S(2)}, u32[]{:S(2)}) collective-permute-start(bf16[18,32,128]{2,1,0:T(8,128)(2,1)S(1)} %get-tuple-element.80), channel_id=1, source_target_pairs={{0,120},{8,0},{16,8},{24,16},{32,24},{40,32},{48,40},{56,48},{64,5... | collective-permute-start | bytes 442376 | tf_op jit(solution)/shard_map/ppermute | solution.py:16
  50.1 1.9 %three.1 = (bf16[6,2,128,384]{3,2,1,0:T(8,128)(2,1)S(1)}, bf16[256,384]{1,0:T(8,128)(2,1)S(1)}, bf16[9,64,128]{2,1,0:T(8,128)(2,1)S(1)}) custom-call(bf16[4,2,64,384]{3,2,1,0:T(8,128)(2,1)S(1)} %get-tuple-element.58.pooled2, bf16[9,64,128]{2,1,0:T(8,128)(2,1)S(1)} %collective-permute-done.6.above, bf16[9,64,128]{2,1,0:T(8,128)(2,1)S(1)} %collective-permute-done.7.below, ...), custom_call_target="tpu_custom_call" | custom-call | tf_op jit(solution)/shard_map/three/pallas_call | solution.py:21
  52.1 2.0 %collective-permute-start.8 = (bf16[9,64,128]{2,1,0:T(8,128)(2,1)S(1)}, bf16[9,64,128]{2,1,0:T(8,128)(2,1)S(1)}, u32[]{:S(2)}, u32[]{:S(2)}) collective-permute-start(bf16[9,64,128]{2,1,0:T(8,128)(2,1)S(1)} %get-tuple-element.66), channel_id=1, source_target_pairs={{0,8},{8,16},{16,24},{24,32},{32,40},{40,48},{48,56},{56,64},{64,7... | collective-permute-start | bytes 442376 | tf_op jit(solution)/shard_map/ppermute | solution.py:16
  54.1 0.8 %skip_inner.1.pre_in = f32[6,8,32,256]{3,2,1,0:T(8,128)S(1)} custom-call(bf16[6,8,32,384]{3,2,1,0:T(8,128)(2,1)S(1)} %get-tuple-element.51.skip_in.s_in, bf16[2,8,32,384]{3,2,1,0:T(8,128)(2,1)S(1)} %get-tuple-element.71.s_out, bf16[96,480]{1,0:T(8,128)(2,1)S(1)} %get-tuple-element.77.w, f32[32,256]{1,0:T(8,128)S(1)} %get-tuple-element.78.b), custom_call_target="tpu_custom_call" | custom-call | flops 1000000000 | tf_op jit(solution)/shard_map/skip_inner/pallas_call | solution.py:21
  54.9 0.7 skip_outer.1.pre_out
  55.6 1.4 %skip_three.1.pre3 = f32[4,2,128,384]{3,2,1,0:T(8,128)S(1)} custom-call(bf16[6,2,128,384]{3,2,1,0:T(8,128)(2,1)S(1)} %get-tuple-element.67.s3, bf16[128,1152]{1,0:T(8,128)(2,1)S(1)} %get-tuple-element.68.w, f32[128,384]{1,0:T(8,128)S(1)} %get-tuple-element.69.b), custom_call_target="tpu_custom_call" | custom-call | flops 1000000000 | tf_op jit(solution)/shard_map/skip_three/pallas_call | solution.py:21
  57.0 0.2 collective-permute-done.9.below
  57.2 3.4 %collective-permute-done.8.above = bf16[9,64,128]{2,1,0:T(8,128)(2,1)S(1)} collective-permute-done((bf16[9,64,128]{2,1,0:T(8,128)(2,1)S(1)}, bf16[9,64,128]{2,1,0:T(8,128)(2,1)S(1)}, u32[]{:S(2)}, u32[]{:S(2)}) %collective-permute-start.8) | collective-permute-done | bytes 147488 | tf_op jit(solution)/shard_map/ppermute | solution.py:16
  60.6 2.8 %back.1.bt = bf16[6,4,64,384]{3,2,1,0:T(8,128)(2,1)S(1)} custom-call(bf16[256,384]{1,0:T(8,128)(2,1)S(1)} %get-tuple-element.65.c, bf16[9,64,128]{2,1,0:T(8,128)(2,1)S(1)} %collective-permute-done.8.above, bf16[9,64,128]{2,1,0:T(8,128)(2,1)S(1)} %collective-permute-done.9.below, f32[4,2,128,384]{3,2,1,0:T(8,128)S(1)} %skip_three.1.pre3, ...), custom_call_target="tpu_custom_call" | custom-call | tf_op jit(solution)/shard_map/back/pallas_call | solution.py:21
  63.4 0.8 %last.1 = bf16[2,8,32,1024]{3,2,1,0:T(8,128)(2,1)S(1)} custom-call(bf16[6,4,64,384]{3,2,1,0:T(8,128)(2,1)S(1)} %back.1.bt, f32[6,8,32,256]{3,2,1,0:T(8,128)S(1)} %skip_inner.1.pre_in, f32[2,8,32,256]{3,2,1,0:T(8,128)S(1)} %skip_outer.1.pre_out, bf16[128,256]{1,0:T(8,128)(2,1)S(1)} %get-tuple-element.82.wu), custom_call_target="tpu_custom_call" | custom-call | tf_op jit(solution)/shard_map/last/pallas_call | solution.py:21
  64.2 0.6 copy-done.1
  64.8 2.6 %head.1 = f32[2,384,1024]{2,1,0:T(8,128)} custom-call(bf16[2,256,1024]{2,1,0:T(8,128)(2,1)S(1)} %bitcast.18, bf16[2,384,1024]{2,1,0:T(8,128)(2,1)S(1)} %bitcast.17, bf16[384,256]{1,0:T(8,128)(2,1)S(1)} %get-tuple-element.83.w, f32[384,256]{1,0:T(8,128)S(1)} %get-tuple-element.84.offset), custom_call_target="tpu_custom_call" | custom-call | tf_op jit(solution)/shard_map/head/pallas_call | solution.py:680
  (44 shorter events, 0.3 us)
Async XLA Ops:
  1.1 4.0 %collective-permute-start.1 = (bf16[2,384,128]{2,1,0:T(8,128)(2,1)S(1)}, bf16[2,384,128]{2,1,0:T(8,128)(2,1)S(1)}, u32[]{:S(2)}, u32[]{:S(2)}) collective-permute-start(bf16[2,384,128]{2,1,0:T(8,128)(2,1)S(1)} %get-tuple-element.85), channel_id=1, source_target_pairs={{0,7},{1,0},{2,1},{3,2},{4,3},{5,4},{6,5},{7,6},{8,15},{9,8},{10,9... | collective-permute-start | bytes 589832 | tf_op jit(solution)/shard_map/ppermute | solution.py:16
  1.3 5.1 %collective-permute-start = (bf16[2,384,128]{2,1,0:T(8,128)(2,1)S(1)}, bf16[2,384,128]{2,1,0:T(8,128)(2,1)S(1)}, u32[]{:S(2)}, u32[]{:S(2)}) collective-permute-start(bf16[2,384,128]{2,1,0:T(8,128)(2,1)S(1)} %get-tuple-element.86), channel_id=1, source_target_pairs={{0,1},{1,2},{2,3},{3,4},{4,5},{5,6},{6,7},{7,0},{8,9},{9,10},{10,1... | collective-permute-start | bytes 589832 | tf_op jit(solution)/shard_map/ppermute | solution.py:16
  1.6 1.4 %copy-start = (bf16[2,48,8,1024]{3,2,1,0:T(8,128)(2,1)S(1)}, bf16[2,48,8,1024]{3,2,1,0:T(8,128)(2,1)}, u32[]{:S(2)}) copy-start(bf16[2,48,8,1024]{3,2,1,0:T(8,128)(2,1)} %param.17) | copy-start | bytes 4718596
  5.0 8.5 %copy-start.5 = (bf16[3,3,64,128]{3,2,1,0:T(8,128)(2,1)S(1)}, bf16[3,3,64,128]{3,2,1,0:T(8,128)(2,1)}, u32[]{:S(2)}) copy-start(bf16[3,3,64,128]{3,2,1,0:T(8,128)(2,1)} %k3.1) | copy-start | bytes 442372
  5.0 8.5 %copy-start.7 = (bf16[3,3,48,32]{2,3,1,0:T(8,128)(2,1)S(1)}, bf16[3,3,48,32]{2,3,1,0:T(8,128)(2,1)}, u32[]{:S(2)}) copy-start(bf16[3,3,48,32]{2,3,1,0:T(8,128)(2,1)} %param.18) | copy-start | bytes 82948
  5.0 8.5 %copy-start.8 = (bf16[3,3,32,64]{3,2,1,0:T(8,128)(2,1)S(1)}, bf16[3,3,32,64]{3,2,1,0:T(8,128)(2,1)}, u32[]{:S(2)}) copy-start(bf16[3,3,32,64]{3,2,1,0:T(8,128)(2,1)} %k2.1) | copy-start | bytes 110596
  5.0 8.5 %copy-start.11 = (f32[32]{0:T(128)S(1)}, f32[32]{0:T(128)}, u32[]{:S(2)}) copy-start(f32[32]{0:T(128)} %param.19) | copy-start | bytes 388
  5.1 8.5 %copy-start.12 = (f32[64]{0:T(128)S(1)}, f32[64]{0:T(128)}, u32[]{:S(2)}) copy-start(f32[64]{0:T(128)} %param.21) | copy-start | bytes 772
  5.1 8.5 %copy-start.13 = (f32[128]{0:T(128)S(1)}, f32[128]{0:T(128)}, u32[]{:S(2)}) copy-start(f32[128]{0:T(128)} %param.23) | copy-start | bytes 1540
  7.1 12.2 %collective-permute-start.2 = (bf16[18,48,128]{2,1,0:T(8,128)(2,1)S(1)}, bf16[18,48,128]{2,1,0:T(8,128)(2,1)S(1)}, u32[]{:S(2)}, u32[]{:S(2)}) collective-permute-start(bf16[18,48,128]{2,1,0:T(8,128)(2,1)S(1)} %get-tuple-element.49), channel_id=1, source_target_pairs={{0,8},{8,16},{16,24},{24,32},{32,40},{40,48},{48,56},{56,64},{64,7... | collective-permute-start | bytes 663560 | tf_op jit(solution)/shard_map/ppermute | solution.py:16
  8.7 10.7 %collective-permute-start.3 = (bf16[18,48,128]{2,1,0:T(8,128)(2,1)S(1)}, bf16[18,48,128]{2,1,0:T(8,128)(2,1)S(1)}, u32[]{:S(2)}, u32[]{:S(2)}) collective-permute-start(bf16[18,48,128]{2,1,0:T(8,128)(2,1)S(1)} %get-tuple-element.50), channel_id=1, source_target_pairs={{0,120},{8,0},{16,8},{24,16},{32,24},{40,32},{48,40},{56,48},{64,5... | collective-permute-start | bytes 663560 | tf_op jit(solution)/shard_map/ppermute | solution.py:16
  19.3 21.3 %copy-start.2 = (bf16[3,3,384,128]{3,2,1,0:T(8,128)(2,1)S(1)}, bf16[3,3,384,128]{3,2,1,0:T(8,128)(2,1)}, u32[]{:S(2)}) copy-start(bf16[3,3,384,128]{3,2,1,0:T(8,128)(2,1)} %d3.1) | copy-start | bytes 2654212
  19.3 21.3 %copy-start.3 = (bf16[3,3,128,256]{3,2,1,0:T(8,128)(2,1)S(1)}, bf16[3,3,128,256]{3,2,1,0:T(8,128)(2,1)}, u32[]{:S(2)}) copy-start(bf16[3,3,128,256]{3,2,1,0:T(8,128)(2,1)} %kc.1) | copy-start | bytes 1769476
  19.3 21.3 %copy-start.4 = (bf16[3,3,192,64]{2,3,1,0:T(8,128)(2,1)S(1)}, bf16[3,3,192,64]{2,3,1,0:T(8,128)(2,1)}, u32[]{:S(2)}) copy-start(bf16[3,3,192,64]{2,3,1,0:T(8,128)(2,1)} %param.28) | copy-start | bytes 663556
  19.4 21.3 %copy-start.6 = (bf16[3,3,96,32]{2,3,1,0:T(8,128)(2,1)S(1)}, bf16[3,3,96,32]{2,3,1,0:T(8,128)(2,1)}, u32[]{:S(2)}) copy-start(bf16[3,3,96,32]{2,3,1,0:T(8,128)(2,1)} %param.30) | copy-start | bytes 165892
  19.4 21.3 %copy-start.9 = (bf16[32,48]{1,0:T(8,128)(2,1)S(1)}, bf16[32,48]{1,0:T(8,128)(2,1)}, u32[]{:S(2)}) copy-start(bf16[32,48]{1,0:T(8,128)(2,1)} %hk.1) | copy-start | bytes 9220
  19.4 21.3 %copy-start.10 = (f32[256]{0:T(256)S(1)}, f32[256]{0:T(256)}, u32[]{:S(2)}) copy-start(f32[256]{0:T(256)} %param.25) | copy-start | bytes 3076
  19.4 21.3 %copy-start.14 = (f32[128]{0:T(128)S(1)}, f32[128]{0:T(128)}, u32[]{:S(2)}) copy-start(f32[128]{0:T(128)} %param.27) | copy-start | bytes 1540
  19.4 21.3 %copy-start.15 = (f32[64]{0:T(128)S(1)}, f32[64]{0:T(128)}, u32[]{:S(2)}) copy-start(f32[64]{0:T(128)} %param.29) | copy-start | bytes 772
  19.4 21.3 %copy-start.16 = (f32[32]{0:T(128)S(1)}, f32[32]{0:T(128)}, u32[]{:S(2)}) copy-start(f32[32]{0:T(128)} %param.31) | copy-start | bytes 388
  19.4 21.3 %copy-start.17 = (f32[48]{0:T(128)S(1)}, f32[48]{0:T(128)}, u32[]{:S(2)}) copy-start(f32[48]{0:T(128)} %param.33) | copy-start | bytes 580
  21.2 11.5 %collective-permute-start.4 = (bf16[27,32,128]{2,1,0:T(8,128)(2,1)S(1)}, bf16[27,32,128]{2,1,0:T(8,128)(2,1)S(1)}, u32[]{:S(2)}, u32[]{:S(2)}) collective-permute-start(bf16[27,32,128]{2,1,0:T(8,128)(2,1)S(1)} %get-tuple-element.54), channel_id=1, source_target_pairs={{0,8},{8,16},{16,24},{24,32},{32,40},{40,48},{48,56},{56,64},{64,7... | collective-permute-start | bytes 663560 | tf_op jit(solution)/shard_map/ppermute | solution.py:16
  21.3 11.4 %collective-permute-start.5 = (bf16[27,32,128]{2,1,0:T(8,128)(2,1)S(1)}, bf16[27,32,128]{2,1,0:T(8,128)(2,1)S(1)}, u32[]{:S(2)}, u32[]{:S(2)}) collective-permute-start(bf16[27,32,128]{2,1,0:T(8,128)(2,1)S(1)} %get-tuple-element.55), channel_id=1, source_target_pairs={{0,120},{8,0},{16,8},{24,16},{32,24},{40,32},{48,40},{56,48},{64,5... | collective-permute-start | bytes 663560 | tf_op jit(solution)/shard_map/ppermute | solution.py:16
  35.3 14.9 %collective-permute-start.6 = (bf16[9,64,128]{2,1,0:T(8,128)(2,1)S(1)}, bf16[9,64,128]{2,1,0:T(8,128)(2,1)S(1)}, u32[]{:S(2)}, u32[]{:S(2)}) collective-permute-start(bf16[9,64,128]{2,1,0:T(8,128)(2,1)S(1)} %get-tuple-element.59), channel_id=1, source_target_pairs={{0,8},{8,16},{16,24},{24,32},{32,40},{40,48},{48,56},{56,64},{64,7... | collective-permute-start | bytes 442376 | tf_op jit(solution)/shard_map/ppermute | solution.py:16
  35.3 14.8 %collective-permute-start.7 = (bf16[9,64,128]{2,1,0:T(8,128)(2,1)S(1)}, bf16[9,64,128]{2,1,0:T(8,128)(2,1)S(1)}, u32[]{:S(2)}, u32[]{:S(2)}) collective-permute-start(bf16[9,64,128]{2,1,0:T(8,128)(2,1)S(1)} %get-tuple-element.60), channel_id=1, source_target_pairs={{0,120},{8,0},{16,8},{24,16},{32,24},{40,32},{48,40},{56,48},{64,5... | collective-permute-start | bytes 442376 | tf_op jit(solution)/shard_map/ppermute | solution.py:16
  44.7 10.2 %collective-permute-start.10 = (bf16[18,32,128]{2,1,0:T(8,128)(2,1)S(1)}, bf16[18,32,128]{2,1,0:T(8,128)(2,1)S(1)}, u32[]{:S(2)}, u32[]{:S(2)}) collective-permute-start(bf16[18,32,128]{2,1,0:T(8,128)(2,1)S(1)} %get-tuple-element.79), channel_id=1, source_target_pairs={{0,8},{8,16},{16,24},{24,32},{32,40},{40,48},{48,56},{56,64},{64,7... | collective-permute-start | bytes 442376 | tf_op jit(solution)/shard_map/ppermute | solution.py:16
  44.8 10.1 %collective-permute-start.11 = (bf16[18,32,128]{2,1,0:T(8,128)(2,1)S(1)}, bf16[18,32,128]{2,1,0:T(8,128)(2,1)S(1)}, u32[]{:S(2)}, u32[]{:S(2)}) collective-permute-start(bf16[18,32,128]{2,1,0:T(8,128)(2,1)S(1)} %get-tuple-element.80), channel_id=1, source_target_pairs={{0,120},{8,0},{16,8},{24,16},{32,24},{40,32},{48,40},{56,48},{64,5... | collective-permute-start | bytes 442376 | tf_op jit(solution)/shard_map/ppermute | solution.py:16
  52.0 5.2 %collective-permute-start.9 = (bf16[9,64,128]{2,1,0:T(8,128)(2,1)S(1)}, bf16[9,64,128]{2,1,0:T(8,128)(2,1)S(1)}, u32[]{:S(2)}, u32[]{:S(2)}) collective-permute-start(bf16[9,64,128]{2,1,0:T(8,128)(2,1)S(1)} %get-tuple-element.66), channel_id=1, source_target_pairs={{0,120},{8,0},{16,8},{24,16},{32,24},{40,32},{48,40},{56,48},{64,5... | collective-permute-start | bytes 442376 | tf_op jit(solution)/shard_map/ppermute | solution.py:16
  52.1 8.5 %collective-permute-start.8 = (bf16[9,64,128]{2,1,0:T(8,128)(2,1)S(1)}, bf16[9,64,128]{2,1,0:T(8,128)(2,1)S(1)}, u32[]{:S(2)}, u32[]{:S(2)}) collective-permute-start(bf16[9,64,128]{2,1,0:T(8,128)(2,1)S(1)} %get-tuple-element.66), channel_id=1, source_target_pairs={{0,8},{8,16},{16,24},{24,32},{32,40},{40,48},{48,56},{56,64},{64,7... | collective-permute-start | bytes 442376 | tf_op jit(solution)/shard_map/ppermute | solution.py:16
  63.4 1.4 %copy-start.1 = (bf16[2,48,8,1024]{3,2,1,0:T(8,128)(2,1)S(1)}, bf16[2,48,8,1024]{3,2,1,0:T(8,128)(2,1)}, u32[]{:S(2)}) copy-start(bf16[2,48,8,1024]{3,2,1,0:T(8,128)(2,1)} %param.17) | copy-start | bytes 4718596

commit v3 on v2

--- a/solution.py
+++ b/solution.py
@@ -11,9 +11,34 @@
 F32 = jnp.float32
 
 
-def neighbour(value, axis, step):
+def swap(near_part, far_part, axis):
     size = lax.axis_size(axis)
-    return lax.ppermute(value, axis, [(i, (i + step) % size) for i in range(size)])
+    near = [(i, i ^ 1) for i in range(size)]
+    far = [(i, (i + 1 if i % 2 else i - 1) % size) for i in range(size)]
+    return lax.ppermute(near_part, axis, near), lax.ppermute(far_part, axis, far)
+
+
+class Either:
+    def __init__(self, cond, one, other):
+        self.cond, self.one, self.other = cond, one, other
+
+    def __getitem__(self, index):
+        return jnp.where(self.cond, self.one[index], self.other[index])
+
+
+def is_even(axis):
+    return lax.axis_index(axis) % 2 == 0
+
+
+def received(near, far, axis):
+    even = is_even(axis)
+    return Either(even, far, near), Either(even, near, far)
+
+
+def pack_both(near, far, before, after):
+    even = is_even("ty")
+    pack(near, [jnp.where(even, b, a) for a, b in zip(before, after)])
+    pack(far, [jnp.where(even, a, b) for a, b in zip(before, after)])
 
 
 def call(body, name, out_shapes, scratch, args, limit=16, flops=0):
@@ -128,6 +153,27 @@
     i, k = iota((rows, rows), 0), iota((rows, rows), 1)
     turn = one_hot(i == (k & 7) * (rows // 8) + (k >> 3))
     return dot(turn, part).astype(BF16)
+
+
+def cols_kernel(x, near, far):
+    lane = iota((1, LANES), 1)
+    size = x.shape[1] // 4
+    even = is_even("tx")
+    for h in range(2):
+        packed = []
+        for start, first in ((0, 0), (896, 96)):
+            tile = None
+            for g in range(4):
+                rows = slice(g * size, (g + 1) * size)
+                piece = rolled(x[h, rows, start : start + 128], 32 * g - first)
+                tile = piece if tile is None else jnp.where(lane < 32 * g, tile, piece)
+            packed.append(tile)
+        near[h] = jnp.where(even, packed[1], packed[0])
+        far[h] = jnp.where(even, packed[0], packed[1])
+
+
+def columns(packed, first):
+    return jnp.concatenate([rolled(packed, first - 32 * g) for g in range(4)], axis=0)
 
 
 def main_kernel(x, out):
@@ -156,14 +202,16 @@
     return pltpu.roll(value, shift % 128, 1) if shift % 128 else value
 
 
-def ends_kernel(x, main, fl, fr, out, first, last):
+def ends_kernel(x, main, cols_near, cols_far, out, near, far):
     flags = edges()
+    fl, fr = received(cols_near, cols_far, "tx")
     lane = iota((1, LANES), 1)
     channels = x.shape[1] // 8
     ends = []
     for h in range(2):
-        a = jnp.where((lane >= 96) & (flags[2] > 0.5), fl[h], jnp.where(lane < 32, x[h, :, :128], 0))
-        b = jnp.where(lane >= 96, x[h, :, 896:], jnp.where((lane < 32) & (flags[3] > 0.5), fr[h], 0))
+        before, after = columns(fl[h], 96), columns(fr[h], 0)
+        a = jnp.where((lane >= 96) & (flags[2] > 0.5), before, jnp.where(lane < 32, x[h, :, :128], 0))
+        b = jnp.where(lane >= 96, x[h, :, 896:], jnp.where((lane < 32) & (flags[3] > 0.5), after, 0))
         ends += [a.astype(BF16), b.astype(BF16)]
     ends = side(*ends)
     c = iota((1, 256), 1)
@@ -174,13 +222,7 @@
         for p in range(8):
             tile = rows[:, (p // 4) * 128 : (p // 4 + 1) * 128]
             out[r, p] = pltpu.roll(tile, 128 - 32 * (p % 4), 1) if p % 4 else tile
-        if r in (0, 7):
-            ref = first if r == 0 else last
-            for p in range(8):
-                ref[2 * p] = main[r, p, :, :128]
-                ref[2 * p + 1] = main[r, p, :, 128:]
-            ref[16] = rows[:, :128]
-            ref[17] = rows[:, 128:]
+    pack_both(near, far, field_slabs(main, out, 0), field_slabs(main, out, 7))
 
 
 def field_slabs(main, ends, r):
@@ -198,7 +240,7 @@
     }
 
 
-def inner_kernel(main, ends, w, b, skip, pooled, xs):
+def inner_kernel(main, ends, w, w_low, w_high, b, skip, pooled, outer, xs):
     flags = edges()
     for r in range(8):
         fill(xs, r, field_slabs(main, ends, r))
@@ -212,6 +254,11 @@
         return carry
 
     lax.fori_loop(0, 2, one, 0)
+    for k, (row, part) in enumerate(((0, w_low), (6, w_high))):
+        for q in range(4):
+            res = dot(part[...], side(*[window(xs, row, 2 * q + s, 2, 3) for s in range(2)]))
+            for s in range(2):
+                outer[k, 2 * q + s] = res[:, s * WIDE : (s + 1) * WIDE] + bias
     for k in range(2):
         for q in range(4):
             pooled[k, q] = mean([skip[2 * k + 1 + r, 2 * q + s] for r in range(2) for s in range(2)])
@@ -225,63 +272,69 @@
 
 
 def outer_kernel(
-    main, ends, above, below, skip_in, pooled_in, w, b, skip, pooled, p_first, p_last, xs
+    f_near, f_far, partial, skip_in, pooled_in, w_top, w_bottom, skip, pooled, near, far, xs
 ):
     flags = edges()
+    above, below = received(f_near, f_far, "ty")
     fill(xs, 0, [unpack(above, p, 8) for p in range(8)], flags[0])
-    for n, r in enumerate((0, 1)):
-        fill(xs, 1 + n, field_slabs(main, ends, r))
-    for n, r in enumerate((6, 7)):
-        fill(xs, 3 + n, field_slabs(main, ends, r))
-    fill(xs, 5, [unpack(below, p, 8) for p in range(8)], flags[1])
+    fill(xs, 1, [unpack(below, p, 8) for p in range(8)], flags[1])
     mask = lane_mask(flags)
-    bias = b[...]
-
-    def one(k, carry):
+    for k, part in enumerate((w_top, w_bottom)):
         for q in range(4):
-            for (r, s), y in conv_rows(xs, w[...], bias, 3 * k, q).items():
+            res = dot(part[...], side(*[window(xs, k, 2 * q + s, 1, 3) for s in range(2)]))
+            for s in range(2):
+                y = silu(res[:, s * WIDE : (s + 1) * WIDE] + partial[k, 2 * q + s])
                 skip[k, 2 * q + s] = (y * mask).astype(BF16)
-        return carry
-
-    lax.fori_loop(0, 2, one, 0)
     for q in range(4):
         pooled[0, q] = mean([src[0, 2 * q + s] for src in (skip, skip_in) for s in range(2)])
-        far = [skip_in[5, 2 * q + s] for s in range(2)] + [skip[1, 2 * q + s] for s in range(2)]
-        pooled[1, q] = mean(far)
+        ends = [skip_in[5, 2 * q + s] for s in range(2)] + [skip[1, 2 * q + s] for s in range(2)]
+        pooled[1, q] = mean(ends)
     rows = [[ref[k, q] for q in range(4)] for ref, k in ((pooled, 0), (pooled_in, 0), (pooled_in, 1), (pooled, 1))]
-    pack(p_first, rows[0] + rows[1] + rows[2])
-    pack(p_last, rows[1] + rows[2] + rows[3])
-
-
-def two_kernel(pooled_in, pooled, above, below, w2, b2, skip2, pooled2, first, last, xs):
+    pack_both(near, far, rows[0] + rows[1] + rows[2], rows[1] + rows[2] + rows[3])
+
+
+def middle_kernel(pooled_in, pooled, w2, b2, skip, xs):
+    for n, (ref, r) in enumerate(((pooled, 0), (pooled_in, 0), (pooled_in, 1), (pooled, 1))):
+        fill(xs, n, [ref[r, p] for p in range(4)])
+    mask = lane_mask(edges())
+    for q in range(2):
+        for (r, s), y in conv_rows(xs, w2[...], b2[...], 0, q, 2).items():
+            skip[r, 2 * q + s] = (y * mask).astype(BF16)
+
+
+def two_kernel(pooled_in, pooled, p_near, p_far, middle, g2, b2, _, skip2, pooled2, near, far, xs):
     flags = edges()
+    above, below = received(p_near, p_far, "ty")
     for r in range(3):
         fill(xs, r, [unpack(above, 4 * r + p, 12) for p in range(4)], flags[0])
-        fill(xs, r + 7, [unpack(below, 4 * r + p, 12) for p in range(4)], flags[1])
-    for n, (ref, r) in enumerate(((pooled, 0), (pooled_in, 0), (pooled_in, 1), (pooled, 1))):
+        fill(xs, r + 5, [unpack(below, 4 * r + p, 12) for p in range(4)], flags[1])
+    for n, (ref, r) in enumerate(((pooled, 0), (pooled_in, 0))):
         fill(xs, n + 3, [ref[r, p] for p in range(4)])
+    for n, (ref, r) in enumerate(((pooled_in, 1), (pooled, 1))):
+        fill(xs, n + 8, [ref[r, p] for p in range(4)])
     mask = lane_mask(flags)
-    bias = b2[...]
-
-    def pair(k, carry):
-        valid = jnp.where(k == 0, flags[0], jnp.where(k == 3, flags[1], 1.0))
-        inside = mask * valid
+    size = b2.shape[0]
+    for k, first in ((0, 0), (1, 3)):
+        rows = ((0, 1, 2, 3, 4), (8, 9, 5, 6, 7))[k]
+        outside = mask * flags[k]
+        for p in range(4):
+            rhs = [window(xs, row, p, 1, 3) for row in rows]
+            res = dot(g2[...], jnp.concatenate(rhs, axis=0))
+            for r in range(3):
+                inside = mask if r == (2, 0)[k] else outside
+                y = silu(res[r * size : (r + 1) * size] + b2[...]) * inside
+                skip2[first + r, p] = y.astype(BF16)
+    order = [(skip2, 0), (skip2, 1), (skip2, 2), (middle, 0), (middle, 1), (skip2, 3), (skip2, 4), (skip2, 5)]
+    for k in range(4):
         for q in range(2):
-            slabs = []
-            for (r, s), y in conv_rows(xs, w2[...], bias, 2 * k, q, 2).items():
-                y = (y * inside).astype(BF16)
-                skip2[2 * k + r, 2 * q + s] = y
-                slabs.append(y)
-            pooled2[k, q] = mean(slabs)
-        return carry
-
-    lax.fori_loop(0, 4, pair, 0)
-    pack(first, [pooled2[r, p] for r in (2, 3) for p in range(2)])
-    pack(last, [pooled2[r, p] for r in (0, 1) for p in range(2)])
-
-
-def three_kernel(pooled2, above, below, w3, b3, wc, bc, skip3, coarse, send, xs, xc):
+            pooled2[k, q] = mean([ref[r, 2 * q + s] for ref, r in order[2 * k : 2 * k + 2] for s in range(2)])
+    before = [pooled2[r, p] for r in (2, 3) for p in range(2)]
+    pack_both(near, far, before, [pooled2[r, p] for r in (0, 1) for p in range(2)])
+
+
+def three_kernel(pooled2, q_near, q_far, w3, b3, wc, bc, skip3, coarse, send, xs, xc):
     flags = edges()
+    above, below = received(q_near, q_far, "ty")
     for r in range(2):
         fill(xs, r, [unpack(above, 2 * r + p, 4) for p in range(2)], flags[0])
         fill(xs, r + 6, [unpack(below, 2 * r + p, 4) for p in range(2)], flags[1])
@@ -313,9 +366,10 @@
             out[r, p] = res[:, p * WIDE : (p + 1) * WIDE] + b[...]
 
 
-def skip_two_kernel(s2, s_out, w, b, out, first, last, xs):
-    for r in range(8):
-        fill(xs, r, [s2[r, p] for p in range(4)])
+def skip_two_kernel(s2, middle, s_out, w, b, out, near, far, xs):
+    order = [(s2, 0), (s2, 1), (s2, 2), (middle, 0), (middle, 1), (s2, 3), (s2, 4), (s2, 5)]
+    for n, (ref, r) in enumerate(order):
+        fill(xs, n, [ref[r, p] for p in range(4)])
     bias = b[...]
 
     def pair(k, carry):
@@ -328,8 +382,7 @@
         return carry
 
     lax.fori_loop(0, 3, pair, 0)
-    pack(first, [s_out[0, p] for p in range(8)])
-    pack(last, [s_out[1, p] for p in range(8)])
+    pack_both(near, far, [s_out[0, p] for p in range(8)], [s_out[1, p] for p in range(8)])
 
 
 def skip_inner_kernel(s_in, s_out, w, b, out, xs):
@@ -345,8 +398,9 @@
                 out[3 * k + r, p] = res[r * size : (r + 1) * size] + b[...]
 
 
-def skip_outer_kernel(s_in, s_out, above, below, w, b, out, xs):
+def skip_outer_kernel(s_in, s_out, s_near, s_far, w, b, out, xs):
     flags = edges()
+    above, below = received(s_near, s_far, "ty")
     fill(xs, 0, [unpack(above, p, 8) for p in range(8)], flags[0])
     for n, (ref, r) in enumerate(((s_out, 0), (s_in, 0), (s_in, 5), (s_out, 1))):
         fill(xs, n + 1, [ref[r, p] for p in range(8)])
@@ -356,8 +410,9 @@
             out[k, p] = dot(w[...], window(xs, 3 * k, p, 3, 3)[:, :256]) + b[...]
 
 
-def back_kernel(c, above, below, pre3, pre2, wu3, wu2, out, xc, xb):
+def back_kernel(c, c_near, c_far, pre3, pre2, wu3, wu2, out, xc, xb):
     flags = edges()
+    above, below = received(c_near, c_far, "ty")
     halo = lambda packed: [jnp.concatenate([unpack(packed, n, 4) for n in range(4)], axis=0)]
     fill(xc, 0, halo(above), flags[0])
     fill(xc, 1, [c[...]])
@@ -414,7 +469,7 @@
                         out[h, r, :, p * 128 : (p + 1) * 128] = y[:, lanes]
 
 
-def head_kernel_body(back, fields, w, offset, out, buf, sems):
+def head_kernel_body(fields, back, w, offset, out, buf, sems):
     lane = iota((1, LANES), 1)
     c = iota((1, 256), 1)
     merge = one_hot(iota((256, 256), 0) == 32 * (c & 7) + (c >> 3))
@@ -490,10 +545,16 @@
 FOUR = [(i, j) for i in range(2) for j in range(2)]
 
 
-def early_kernel(k1, k2, k3, r1, r2, r3, w1, g1, w2, w3, b1, b2, b3):
-    w1[...] = placed([k1[n] for n in NINE], w1.shape[1])
-    g1[...] = grouped(w1[...], 3)
-    w2[...] = grouped(flip(k2[...].reshape(-1, k2.shape[3])), 2)
+def early_kernel(k1, k2, k3, r1, r2, r3, g1, low, high, top, bottom, w2, g2, w3, b1, b2, b3):
+    w1 = placed([k1[n] for n in NINE], 9 * k1.shape[3])
+    step = 3 * k1.shape[3]
+    g1[...] = grouped(w1, 3)
+    for ref, start in ((low, step), (high, 0), (top, 0), (bottom, 2 * step)):
+        i, j = iota((w1.shape[1], ref.shape[1]), 0), iota((w1.shape[1], ref.shape[1]), 1)
+        ref[...] = dot(w1, one_hot(i == j + start)).astype(BF16)
+    flat = flip(k2[...].reshape(-1, k2.shape[3]))
+    w2[...] = grouped(flat, 2)
+    g2[...] = grouped(flat, 3)
     w3[...] = flip(k3[...].reshape(-1, k3.shape[3]))
     for r, b in ((r1, b1), (r2, b2), (r3, b3)):
         b[...] = column(r[...], WIDE)
@@ -553,26 +614,22 @@
     v = fields.shape[1]
 
     x = fields.reshape(2, v * 8, 1024)
-    from_l = neighbour(x[:, :, 896:], "tx", 1)
-    from_r = neighbour(x[:, :, :128], "tx", -1)
-
-    def up(value):
-        return neighbour(value, "ty", -1)
-
-    def down(value):
-        return neighbour(value, "ty", 1)
+    near, far = call(cols_kernel, "cols", [((2, 2 * v, LANES), BF16)] * 2, [], [x])
+    cols = swap(near, far, "tx")
 
     row = lambda bias: bias[None, :]
-    swap = lambda kernel: jnp.transpose(kernel, (0, 1, 3, 2))
+    turn = lambda kernel: jnp.transpose(kernel, (0, 1, 3, 2))
     weights = lambda *shape: (shape, BF16)
     biases = lambda size, width=WIDE: ((size, width), F32)
-    w1, g1, w2, w3, b1, b2, b3 = call(
+    g1, w_low, w_high, w_top, w_bottom, w2, g2, w3, b1, b2, b3 = call(
         early_kernel,
         "early",
-        [weights(c1, 9 * v), weights(3 * c1, 15 * v), weights(2 * c2, 12 * c1), weights(c3, 9 * c2)]
+        [weights(3 * c1, 15 * v)]
+        + [weights(c1, rows * 3 * v) for rows in (2, 2, 1, 1)]
+        + [weights(2 * c2, 12 * c1), weights(3 * c2, 15 * c1), weights(c3, 9 * c2)]
         + [biases(c1), biases(c2), biases(c3)],
         [],
-        [swap(kernel_one), kernel_two, kernel_three, row(bias_one), row(bias_two), row(bias_three)],
+        [turn(kernel_one), kernel_two, kernel_three, row(bias_one), row(bias_two), row(bias_three)],
     )
     wc, wu3, ws3, wu2, gs2, wu1, ws1, gs1, wh, bc, ob3, ob2, ob1, bh = call(
         late_kernel,
@@ -583,62 +640,37 @@
         + [weights(8 * v, 8 * c1)]
         + [biases(c4), biases(c3), biases(c2), biases(c1, 256), biases(8 * v, 256)],
         [],
-        [kernel_coarse, decode_three, swap(decode_two), swap(decode_one), head_kernel]
+        [kernel_coarse, decode_three, turn(decode_two), turn(decode_one), head_kernel]
         + [row(b) for b in (bias_coarse, offset_three, offset_two, offset_one, head_offset)],
         flops=5 * 10**8,
     )
     (main,) = call(main_kernel, "main", [((8, 8, v, 256), BF16)], [], [x], flops=10**9)
     packed = lambda count, size: ((tiles(count), size, LANES), BF16)
-    ends, f_first, f_last = call(
+    ends, near, far = call(
         ends_kernel,
         "ends",
         [((8, 8, v, LANES), BF16), packed(8, v), packed(8, v)],
         [],
-        [x, main, from_l, from_r],
-    )
-    f_above, f_below = down(f_last), up(f_first)
-    s_in, p_in = call(
+        [x, main, *cols],
+    )
+    halo = swap(near, far, "ty")
+    s_in, p_in, partial = call(
         inner_kernel,
         "inner",
-        [((6, 8, c1, WIDE), BF16), ((2, 4, c1, WIDE), BF16)],
+        [((6, 8, c1, WIDE), BF16), ((2, 4, c1, WIDE), BF16), ((2, 8, c1, WIDE), F32)],
         [pltpu.VMEM((8, 10, v, WIDE), BF16)],
-        [main, ends, g1, b1],
+        [main, ends, g1, w_low, w_high, b1],
         flops=10**9,
     )
-    s_out, p_out, p_first, p_last = call(
+    s_out, p_out, near, far = call(
         outer_kernel,
         "outer",
         [((2, 8, c1, WIDE), BF16), ((2, 4, c1, WIDE), BF16)]
         + [packed(12, c1)] * 2,
-        [pltpu.VMEM((6, 10, v, WIDE), BF16)],
-        [main, ends, f_above, f_below, s_in, p_in, w1, b1],
-    )
-    p_above, p_below = down(p_last), up(p_first)
-    s2, p2, q_first, q_last = call(
-        two_kernel,
-        "two",
-        [((8, 4, c2, WIDE), BF16), ((4, 2, c2, WIDE), BF16), packed(4, c2), packed(4, c2)],
-        [pltpu.VMEM((10, 6, c1, WIDE), BF16)],
-        [p_in, p_out, p_above, p_below, w2, b2],
-    )
-    q_above, q_below = down(q_last), up(q_first)
-    pre2, s_first, s_last = call(
-        skip_two_kernel,
-        "skip_two",
-        [((6, 4, c2, WIDE), F32), packed(8, c1), packed(8, c1)],
-        [pltpu.VMEM((8, 6, c2, WIDE), BF16)],
-        [s2, s_out, gs2, ob2],
-        flops=10**9,
-    )
-    s_above, s_below = down(s_last), up(s_first)
-    s3, coarse, c_send = call(
-        three_kernel,
-        "three",
-        [((6, 2, c3, WIDE), BF16), ((c4, WIDE), BF16), packed(4, c4 // 4)],
-        [pltpu.VMEM((8, 4, c2, WIDE), BF16), pltpu.VMEM((3, 3, c3, WIDE), BF16)],
-        [p2, q_above, q_below, w3, b3, wc, bc],
-    )
-    c_above, c_below = down(c_send), up(c_send)
+        [pltpu.VMEM((2, 10, v, WIDE), BF16)],
+        [*halo, partial, s_in, p_in, w_top, w_bottom],
+    )
+    halo = swap(near, far, "ty")
     (pre_in,) = call(
         skip_inner_kernel,
         "skip_inner",
@@ -647,12 +679,45 @@
         [s_in, s_out, gs1, ob1],
         flops=10**9,
     )
+    (middle,) = call(
+        middle_kernel,
+        "middle",
+        [((2, 4, c2, WIDE), BF16)],
+        [pltpu.VMEM((4, 6, c1, WIDE), BF16)],
+        [p_in, p_out, w2, b2],
+        flops=5 * 10**8,
+    )
+    s2, p2, near, far = call(
+        two_kernel,
+        "two",
+        [((6, 4, c2, WIDE), BF16), ((4, 2, c2, WIDE), BF16), packed(4, c2), packed(4, c2)],
+        [pltpu.VMEM((10, 6, c1, WIDE), BF16)],
+        [p_in, p_out, *halo, middle, g2, b2, pre_in],
+    )
+    halo = swap(near, far, "ty")
+    pre2, near, far = call(
+        skip_two_kernel,
+        "skip_two",
+        [((6, 4, c2, WIDE), F32), packed(8, c1), packed(8, c1)],
+        [pltpu.VMEM((8, 6, c2, WIDE), BF16)],
+        [s2, middle, s_out, gs2, ob2],
+        flops=10**9,
+    )
+    skip_halo = swap(near, far, "ty")
+    s3, coarse, c_send = call(
+        three_kernel,
+        "three",
+        [((6, 2, c3, WIDE), BF16), ((c4, WIDE), BF16), packed(4, c4 // 4)],
+        [pltpu.VMEM((8, 4, c2, WIDE), BF16), pltpu.VMEM((3, 3, c3, WIDE), BF16)],
+        [p2, *halo, w3, b3, wc, bc],
+    )
+    halo = swap(c_send, c_send, "ty")
     (pre_out,) = call(
         skip_outer_kernel,
         "skip_outer",
         [((2, 8, c1, 256), F32)],
         [pltpu.VMEM((6, 10, c1, WIDE), BF16)],
-        [s_in, s_out, s_above, s_below, ws1, ob1],
+        [s_in, s_out, *skip_halo, ws1, ob1],
         flops=5 * 10**8,
     )
     (pre3,) = call(
@@ -668,7 +733,7 @@
         "back",
         [((6, 4, c2, WIDE), BF16)],
         [pltpu.VMEM((3, 3, c4, WIDE), BF16), pltpu.VMEM((4, 4, c3, WIDE), BF16)],
-        [coarse, c_above, c_below, pre3, pre2, wu3, wu2],
+        [coarse, *halo, pre3, pre2, wu3, wu2],
     )
     (back_one,) = call(
         last_kernel,
@@ -682,10 +747,13 @@
         name="head",
         out_shape=jax.ShapeDtypeStruct((2, v * 8, 1024), F32),
         in_specs=[pl.BlockSpec(memory_space=pltpu.VMEM)] * 4,
-        out_specs=pl.BlockSpec(memory_space=pl.ANY),
-        scratch_shapes=[pltpu.VMEM((2, v * 8, 1024), F32), pltpu.SemaphoreType.DMA((4,))],
+        out_specs=pl.BlockSpec(memory_space=pltpu.HBM),
+        scratch_shapes=[
+            pltpu.VMEM((2, v * 8, 1024), F32),
+            pltpu.SemaphoreType.DMA((4,)),
+        ],
         compiler_params=pltpu.CompilerParams(vmem_limit_bytes=16 * 2**20),
-    )(back_one.reshape(2, 8 * c1, 1024), x, wh, bh)
+    )(x, back_one.reshape(2, 8 * c1, 1024), wh, bh)
     return out.reshape(2, v, 8, 1024)
 
 

time: 67.7 us -> 61 us (0.901)
  waiting for transfers between devices: 13.2 us -> 7.63 us
  local copies, waits for them, and re-layouts: 3.17 us -> 2.12 us
    ppermute x12, waiting for transfers between devices: 13.2 us -> 7.63 us  [the longest x6 6.3 us: swap(): lax.ppermute(far_part, axis, far)]
    slice x1 -> x0, local copies, waits for them, and re-layouts: 1.05 us -> none  [body(): from_r = neighbour(x[:, :, :128], 'tx', -1)]
    pallas_call x14 -> x16, Pallas kernels: 22.5 us -> 22.2 us  [call(): pl.pallas_call(body, name=name, out_shape=[jax.ShapeDtypeStruct(s, d) for...]
  transfers between devices with their start and end apart: 12 -> 12, of which waited for: 5 -> 6; matrix products, arithmetic and copies ran while one was open for 0% -> 0% of each run, Pallas kernels for 20% -> 25%
where the time goes in v3:
time: 61 us; the launch traced here: 60.8 us
  starting transfers between devices  25.8 us (42%)
  Pallas kernels  24.8 us (41%)
  waiting for transfers between devices  7.63 us (13%)
  local copies, waits for them, and re-layouts  2.12 us (3%)
    ppermute x6, starting transfers between devices, swap(): lax.ppermute(far_part, axis, far)  23.9 us
    pallas_call x16, Pallas kernels, call(): pl.pallas_call(body, name=name, out_shape=[jax.ShapeDtypeStruct(s, d) for...  22.2 us
    ppermute x6, waiting for transfers between devices, swap(): lax.ppermute(far_part, axis, far)  6.3 us
    pallas_call x1, Pallas kernels, body(): pl.pallas_call(head_kernel_body, name='head', out_shape=jax.ShapeDtypeStr...  2.54 us
    unnamed x36, local copies, waits for them, and re-layouts  2.12 us
    ppermute x6, starting transfers between devices, swap(): lax.ppermute(near_part, axis, near)  1.9 us
    ppermute x6, waiting for transfers between devices, swap(): lax.ppermute(near_part, axis, near)  1.34 us
  transfers between devices with their start and end apart: 12, of which 6 were waited for; matrix products, arithmetic and copies ran while one was open for 0% of the time, Pallas kernels for 25%

profile of v3, /device:TPU:24, one launch (start us, length us, event | category | flops | bytes accessed | tf_op | source)
XLA Modules:
  0.0 60.8 jit_solution(11021247106368956454)
XLA Ops:
  0.0 1.4 %copy-done = bf16[2,48,8,1024]{3,2,1,0:T(8,128)(2,1)S(1)} copy-done((bf16[2,48,8,1024]{3,2,1,0:T(8,128)(2,1)S(1)}, bf16[2,48,8,1024]{3,2,1,0:T(8,128)(2,1)}, u32[]{:S(2)}) %copy-start) | copy-done | bytes 1572888
  1.4 0.1 cols.1
  1.7 0.8 %collective-permute-start.1 = (bf16[2,96,128]{2,1,0:T(8,128)(2,1)S(1)}, bf16[2,96,128]{2,1,0:T(8,128)(2,1)S(1)}, u32[]{:S(2)}, u32[]{:S(2)}) collective-permute-start(bf16[2,96,128]{2,1,0:T(8,128)(2,1)S(1)} %get-tuple-element.53), channel_id=1, source_target_pairs={{0,7},{1,2},{2,1},{3,4},{4,3},{5,6},{6,5},{7,0},{8,15},{9,10},{10,... | collective-permute-start | bytes 147464 | tf_op jit(solution)/shard_map/ppermute | solution.py:18
  2.5 2.0 %main.1 = bf16[8,8,48,256]{3,2,1,0:T(8,128)(2,1)S(1)} custom-call(bf16[2,384,1024]{2,1,0:T(8,128)(2,1)S(1)} %bitcast.15), custom_call_target="tpu_custom_call" | custom-call | flops 1000000000 | tf_op jit(solution)/shard_map/main/pallas_call | solution.py:46
  4.6 0.6 %collective-permute-done.1.cols_far = bf16[2,96,128]{2,1,0:T(8,128)(2,1)S(1)} collective-permute-done((bf16[2,96,128]{2,1,0:T(8,128)(2,1)S(1)}, bf16[2,96,128]{2,1,0:T(8,128)(2,1)S(1)}, u32[]{:S(2)}, u32[]{:S(2)}) %collective-permute-start.1) | collective-permute-done | bytes 49184 | tf_op jit(solution)/shard_map/ppermute | solution.py:18
  5.3 0.9 %ends.1 = (bf16[8,8,48,128]{3,2,1,0:T(8,128)(2,1)S(1)}, bf16[18,48,128]{2,1,0:T(8,128)(2,1)S(1)}, bf16[18,48,128]{2,1,0:T(8,128)(2,1)S(1)}) custom-call(bf16[2,384,1024]{2,1,0:T(8,128)(2,1)S(1)} %bitcast.16, bf16[8,8,48,256]{3,2,1,0:T(8,128)(2,1)S(1)} %main.1, bf16[2,96,128]{2,1,0:T(8,128)(2,1)S(1)} %collective-permute-done.cols_near, ...), custom_call_target="tpu_custom_call" | custom-call | tf_op jit(solution)/shard_map/ends/pallas_call | solution.py:46
  6.2 1.6 %collective-permute-start.2 = (bf16[18,48,128]{2,1,0:T(8,128)(2,1)S(1)}, bf16[18,48,128]{2,1,0:T(8,128)(2,1)S(1)}, u32[]{:S(2)}, u32[]{:S(2)}) collective-permute-start(bf16[18,48,128]{2,1,0:T(8,128)(2,1)S(1)} %get-tuple-element.60), channel_id=1, source_target_pairs={{0,8},{8,0},{16,24},{24,16},{32,40},{40,32},{48,56},{56,48},{64,72... | collective-permute-start | bytes 663560 | tf_op jit(solution)/shard_map/ppermute | solution.py:18
  7.7 5.6 %collective-permute-start.3 = (bf16[18,48,128]{2,1,0:T(8,128)(2,1)S(1)}, bf16[18,48,128]{2,1,0:T(8,128)(2,1)S(1)}, u32[]{:S(2)}, u32[]{:S(2)}) collective-permute-start(bf16[18,48,128]{2,1,0:T(8,128)(2,1)S(1)} %get-tuple-element.61), channel_id=1, source_target_pairs={{0,120},{8,16},{16,8},{24,32},{32,24},{40,48},{48,40},{56,64},{64,... | collective-permute-start | bytes 663560 | tf_op jit(solution)/shard_map/ppermute | solution.py:18
  13.3 0.9 %early.1 = (bf16[96,720]{1,0:T(8,128)(2,1)S(1)}, bf16[32,288]{1,0:T(8,128)(2,1)S(1)}, bf16[32,288]{1,0:T(8,128)(2,1)S(1)}, bf16[32,144]{1,0:T(8,128)(2,1)S(1)}, ...) custom-call(bf16[3,3,32,48]{3,2,1,0:T(8,128)(2,1)S(1)} %bitcast.21, ...), custom_call_target="tpu_custom_call" | custom-call | tf_op jit(solution)/shard_map/early/pallas_call | solution.py:46
  14.3 3.0 %inner.1 = (bf16[6,8,32,384]{3,2,1,0:T(8,128)(2,1)S(1)}, bf16[2,4,32,384]{3,2,1,0:T(8,128)(2,1)S(1)}, f32[2,8,32,384]{3,2,1,0:T(8,128)S(1)}) custom-call(bf16[8,8,48,256]{3,2,1,0:T(8,128)(2,1)S(1)} %main.1, bf16[8,8,48,128]{3,2,1,0:T(8,128)(2,1)S(1)} %get-tuple-element.54.ends, bf16[96,720]{1,0:T(8,128)(2,1)S(1)} %get-tuple-element.55.w, ...), custom_call_target="tpu_custom_call" | custom-call | flops 1000000000 | tf_op jit(solution)/shard_map/inner/pallas_call | solution.py:46
  17.5 1.5 %collective-permute-done.3.f_far = bf16[18,48,128]{2,1,0:T(8,128)(2,1)S(1)} collective-permute-done((bf16[18,48,128]{2,1,0:T(8,128)(2,1)S(1)}, bf16[18,48,128]{2,1,0:T(8,128)(2,1)S(1)}, u32[]{:S(2)}, u32[]{:S(2)}) %collective-permute-start.3) | collective-permute-done | bytes 221216 | tf_op jit(solution)/shard_map/ppermute | solution.py:18
  18.9 0.8 %outer.1 = (bf16[2,8,32,384]{3,2,1,0:T(8,128)(2,1)S(1)}, bf16[2,4,32,384]{3,2,1,0:T(8,128)(2,1)S(1)}, bf16[27,32,128]{2,1,0:T(8,128)(2,1)S(1)}, bf16[27,32,128]{2,1,0:T(8,128)(2,1)S(1)}) custom-call(bf16[18,48,128]{2,1,0:T(8,128)(2,1)S(1)} %collective-permute-done.2.f_near, bf16[18,48,128]{2,1,0:T(8,128)(2,1)S(1)} %collective-permute-done.3.f_far, ...), custom_call_target="tpu_custom_call" | custom-call | tf_op jit(solution)/shard_map/outer/pallas_call | solution.py:46
  19.8 5.7 %collective-permute-start.5 = (bf16[27,32,128]{2,1,0:T(8,128)(2,1)S(1)}, bf16[27,32,128]{2,1,0:T(8,128)(2,1)S(1)}, u32[]{:S(2)}, u32[]{:S(2)}) collective-permute-start(bf16[27,32,128]{2,1,0:T(8,128)(2,1)S(1)} %get-tuple-element.68), channel_id=1, source_target_pairs={{0,120},{8,16},{16,8},{24,32},{32,24},{40,48},{48,40},{56,64},{64,... | collective-permute-start | bytes 663560 | tf_op jit(solution)/shard_map/ppermute | solution.py:18
  25.6 1.9 %late.1 = (bf16[256,1152]{1,0:T(8,128)(2,1)S(1)}, bf16[2,2,128,1024]{3,2,1,0:T(8,128)(2,1)S(1)}, bf16[128,1152]{1,0:T(8,128)(2,1)S(1)}, bf16[2,128,512]{2,1,0:T(...) custom-call(bf16[3,3,128,256]{3,2,1,0:T(8,128)(2,1)S(1)} %copy-done., ...), custom_call_target="tpu_custom_call" | custom-call | flops 500000000 | tf_op jit(solution)/shard_map/late/pallas_call | solution.py:46
  27.5 0.5 middle.1
  28.1 0.8 %skip_inner.1._.pre_in = f32[6,8,32,256]{3,2,1,0:T(8,128)S(1)} custom-call(bf16[6,8,32,384]{3,2,1,0:T(8,128)(2,1)S(1)} %get-tuple-element.63.skip_in.s_in, bf16[2,8,32,384]{3,2,1,0:T(8,128)(2,1)S(1)} %get-tuple-element.72.s_out, bf16[96,480]{1,0:T(8,128)(2,1)S(1)} %get-tuple-element.73.w, f32[32,256]{1,0:T(8,128)S(1)} %get-tuple-element.74.b), custom_call_target="tpu_custom_call" | custom-call | flops 1000000000 | tf_op jit(solution)/shard_map/skip_inner/pallas_call | solution.py:46
  28.9 2.5 %collective-permute-done.5.p_far = bf16[27,32,128]{2,1,0:T(8,128)(2,1)S(1)} collective-permute-done((bf16[27,32,128]{2,1,0:T(8,128)(2,1)S(1)}, bf16[27,32,128]{2,1,0:T(8,128)(2,1)S(1)}, u32[]{:S(2)}, u32[]{:S(2)}) %collective-permute-start.5) | collective-permute-done | bytes 221216 | tf_op jit(solution)/shard_map/ppermute | solution.py:18
  31.3 1.6 %two.1 = (bf16[6,4,64,384]{3,2,1,0:T(8,128)(2,1)S(1)}, bf16[4,2,64,384]{3,2,1,0:T(8,128)(2,1)S(1)}, bf16[9,64,128]{2,1,0:T(8,128)(2,1)S(1)}, bf16[9,64,128]{2,1,0:T(8,128)(2,1)S(1)}) custom-call(bf16[2,4,32,384]{3,2,1,0:T(8,128)(2,1)S(1)} %get-tuple-element.59.pooled_in, bf16[2,4,32,384]{3,2,1,0:T(8,128)(2,1)S(1)} %get-tuple-element.66.pooled, ...), custom_call_target="tpu_custom_call" | custom-call | tf_op jit(solution)/shard_map/two/pallas_call | solution.py:46
  33.1 5.3 %collective-permute-start.7 = (bf16[9,64,128]{2,1,0:T(8,128)(2,1)S(1)}, bf16[9,64,128]{2,1,0:T(8,128)(2,1)S(1)}, u32[]{:S(2)}, u32[]{:S(2)}) collective-permute-start(bf16[9,64,128]{2,1,0:T(8,128)(2,1)S(1)} %get-tuple-element.77), channel_id=1, source_target_pairs={{0,120},{8,16},{16,8},{24,32},{32,24},{40,48},{48,40},{56,64},{64,... | collective-permute-start | bytes 442376 | tf_op jit(solution)/shard_map/ppermute | solution.py:18
  38.4 2.0 %skip_two.1 = (f32[6,4,64,384]{3,2,1,0:T(8,128)S(1)}, bf16[18,32,128]{2,1,0:T(8,128)(2,1)S(1)}, bf16[18,32,128]{2,1,0:T(8,128)(2,1)S(1)}) custom-call(bf16[6,4,64,384]{3,2,1,0:T(8,128)(2,1)S(1)} %get-tuple-element.87.s2, bf16[2,4,64,384]{3,2,1,0:T(8,128)(2,1)S(1)} %middle.1, bf16[2,8,32,384]{3,2,1,0:T(8,128)(2,1)S(1)} %get-tuple-element.72.s_out, ...), custom_call_target="tpu_custom_call" | custom-call | flops 1000000000 | tf_op jit(solution)/shard_map/skip_two/pallas_call | solution.py:46
  40.5 1.7 %collective-permute-start.11 = (bf16[18,32,128]{2,1,0:T(8,128)(2,1)S(1)}, bf16[18,32,128]{2,1,0:T(8,128)(2,1)S(1)}, u32[]{:S(2)}, u32[]{:S(2)}) collective-permute-start(bf16[18,32,128]{2,1,0:T(8,128)(2,1)S(1)} %get-tuple-element.94), channel_id=1, source_target_pairs={{0,120},{8,16},{16,8},{24,32},{32,24},{40,48},{48,40},{56,64},{64,... | collective-permute-start | bytes 442376 | tf_op jit(solution)/shard_map/ppermute | solution.py:18
  42.2 1.8 %three.1 = (bf16[6,2,128,384]{3,2,1,0:T(8,128)(2,1)S(1)}, bf16[256,384]{1,0:T(8,128)(2,1)S(1)}, bf16[9,64,128]{2,1,0:T(8,128)(2,1)S(1)}) custom-call(bf16[4,2,64,384]{3,2,1,0:T(8,128)(2,1)S(1)} %get-tuple-element.75.pooled2, bf16[9,64,128]{2,1,0:T(8,128)(2,1)S(1)} %collective-permute-done.6.q_near, bf16[9,64,128]{2,1,0:T(8,128)(2,1)S(1)} %collective-permute-done.7.q_far, ...), custom_call_target="tpu_custom_call" | custom-call | tf_op jit(solution)/shard_map/three/pallas_call | solution.py:46
  44.1 4.7 %collective-permute-start.9 = (bf16[9,64,128]{2,1,0:T(8,128)(2,1)S(1)}, bf16[9,64,128]{2,1,0:T(8,128)(2,1)S(1)}, u32[]{:S(2)}, u32[]{:S(2)}) collective-permute-start(bf16[9,64,128]{2,1,0:T(8,128)(2,1)S(1)} %get-tuple-element.83), channel_id=1, source_target_pairs={{0,120},{8,16},{16,8},{24,32},{32,24},{40,48},{48,40},{56,64},{64,... | collective-permute-start | bytes 442376 | tf_op jit(solution)/shard_map/ppermute | solution.py:18
  48.8 0.7 %collective-permute-done.11.s_far = bf16[18,32,128]{2,1,0:T(8,128)(2,1)S(1)} collective-permute-done((bf16[18,32,128]{2,1,0:T(8,128)(2,1)S(1)}, bf16[18,32,128]{2,1,0:T(8,128)(2,1)S(1)}, u32[]{:S(2)}, u32[]{:S(2)}) %collective-permute-start.11) | collective-permute-done | bytes 147488 | tf_op jit(solution)/shard_map/ppermute | solution.py:18
  49.5 0.7 %skip_outer.1.pre_out = f32[2,8,32,256]{3,2,1,0:T(8,128)S(1)} custom-call(bf16[6,8,32,384]{3,2,1,0:T(8,128)(2,1)S(1)} %get-tuple-element.63.skip_in.s_in, bf16[2,8,32,384]{3,2,1,0:T(8,128)(2,1)S(1)} %get-tuple-element.72.s_out, bf16[18,32,128]{2,1,0:T(8,128)(2,1)S(1)} %collective-permute-done.10.s_near, ...), custom_call_target="tpu_custom_call" | custom-call | flops 500000000 | tf_op jit(solution)/shard_map/skip_outer/pallas_call | solution.py:46
  50.2 1.4 %skip_three.1.pre3 = f32[4,2,128,384]{3,2,1,0:T(8,128)S(1)} custom-call(bf16[6,2,128,384]{3,2,1,0:T(8,128)(2,1)S(1)} %get-tuple-element.84.s3, bf16[128,1152]{1,0:T(8,128)(2,1)S(1)} %get-tuple-element.85.w, f32[128,384]{1,0:T(8,128)S(1)} %get-tuple-element.86.b), custom_call_target="tpu_custom_call" | custom-call | flops 1000000000 | tf_op jit(solution)/shard_map/skip_three/pallas_call | solution.py:46
  51.6 1.0 %collective-permute-done.9.c_far = bf16[9,64,128]{2,1,0:T(8,128)(2,1)S(1)} collective-permute-done((bf16[9,64,128]{2,1,0:T(8,128)(2,1)S(1)}, bf16[9,64,128]{2,1,0:T(8,128)(2,1)S(1)}, u32[]{:S(2)}, u32[]{:S(2)}) %collective-permute-start.9) | collective-permute-done | bytes 147488 | tf_op jit(solution)/shard_map/ppermute | solution.py:18
  52.6 1.3 %collective-permute-done.8.c_near = bf16[9,64,128]{2,1,0:T(8,128)(2,1)S(1)} collective-permute-done((bf16[9,64,128]{2,1,0:T(8,128)(2,1)S(1)}, bf16[9,64,128]{2,1,0:T(8,128)(2,1)S(1)}, u32[]{:S(2)}, u32[]{:S(2)}) %collective-permute-start.8) | collective-permute-done | bytes 147488 | tf_op jit(solution)/shard_map/ppermute | solution.py:18
  53.9 2.8 %back.1.bt = bf16[6,4,64,384]{3,2,1,0:T(8,128)(2,1)S(1)} custom-call(bf16[256,384]{1,0:T(8,128)(2,1)S(1)} %get-tuple-element.82.c, bf16[9,64,128]{2,1,0:T(8,128)(2,1)S(1)} %collective-permute-done.8.c_near, bf16[9,64,128]{2,1,0:T(8,128)(2,1)S(1)} %collective-permute-done.9.c_far, f32[4,2,128,384]{3,2,1,0:T(8,128)S(1)} %skip_three.1.pre3, ...), custom_call_target="tpu_custom_call" | custom-call | tf_op jit(solution)/shard_map/back/pallas_call | solution.py:46
  56.7 0.8 %last.1 = bf16[2,8,32,1024]{3,2,1,0:T(8,128)(2,1)S(1)} custom-call(bf16[6,4,64,384]{3,2,1,0:T(8,128)(2,1)S(1)} %back.1.bt, f32[6,8,32,256]{3,2,1,0:T(8,128)S(1)} %skip_inner.1._.pre_in, f32[2,8,32,256]{3,2,1,0:T(8,128)S(1)} %skip_outer.1.pre_out, bf16[128,256]{1,0:T(8,128)(2,1)S(1)} %get-tuple-element.96.wu), custom_call_target="tpu_custom_call" | custom-call | tf_op jit(solution)/shard_map/last/pallas_call | solution.py:46
  57.5 0.6 %copy-done.1 = bf16[2,48,8,1024]{3,2,1,0:T(8,128)(2,1)S(1)} copy-done((bf16[2,48,8,1024]{3,2,1,0:T(8,128)(2,1)S(1)}, bf16[2,48,8,1024]{3,2,1,0:T(8,128)(2,1)}, u32[]{:S(2)}) %copy-start.1) | copy-done | bytes 1572888
  58.1 2.5 %head.1 = f32[2,384,1024]{2,1,0:T(8,128)} custom-call(bf16[2,384,1024]{2,1,0:T(8,128)(2,1)S(1)} %bitcast.17, bf16[2,256,1024]{2,1,0:T(8,128)(2,1)S(1)} %bitcast.18, bf16[384,256]{1,0:T(8,128)(2,1)S(1)} %get-tuple-element.97.w, f32[384,256]{1,0:T(8,128)S(1)} %get-tuple-element.98.offset), custom_call_target="tpu_custom_call" | custom-call | tf_op jit(solution)/shard_map/head/pallas_call | solution.py:745
  (45 shorter events, 0.5 us)
Async XLA Ops:
  0.0 1.4 %copy-start = (bf16[2,48,8,1024]{3,2,1,0:T(8,128)(2,1)S(1)}, bf16[2,48,8,1024]{3,2,1,0:T(8,128)(2,1)}, u32[]{:S(2)}) copy-start(bf16[2,48,8,1024]{3,2,1,0:T(8,128)(2,1)} %param.17) | copy-start | bytes 4718596
  1.6 3.0 %collective-permute-start = (bf16[2,96,128]{2,1,0:T(8,128)(2,1)S(1)}, bf16[2,96,128]{2,1,0:T(8,128)(2,1)S(1)}, u32[]{:S(2)}, u32[]{:S(2)}) collective-permute-start(bf16[2,96,128]{2,1,0:T(8,128)(2,1)S(1)} %get-tuple-element.52), channel_id=1, source_target_pairs={{0,1},{1,0},{2,3},{3,2},{4,5},{5,4},{6,7},{7,6},{8,9},{9,8},{10,11... | collective-permute-start | bytes 147464 | tf_op jit(solution)/shard_map/ppermute | solution.py:18
  1.7 3.6 %collective-permute-start.1 = (bf16[2,96,128]{2,1,0:T(8,128)(2,1)S(1)}, bf16[2,96,128]{2,1,0:T(8,128)(2,1)S(1)}, u32[]{:S(2)}, u32[]{:S(2)}) collective-permute-start(bf16[2,96,128]{2,1,0:T(8,128)(2,1)S(1)} %get-tuple-element.53), channel_id=1, source_target_pairs={{0,7},{1,2},{2,1},{3,4},{4,3},{5,6},{6,5},{7,0},{8,15},{9,10},{10,... | collective-permute-start | bytes 147464 | tf_op jit(solution)/shard_map/ppermute | solution.py:18
  4.5 8.8 %copy-start.5 = (bf16[3,3,64,128]{3,2,1,0:T(8,128)(2,1)S(1)}, bf16[3,3,64,128]{3,2,1,0:T(8,128)(2,1)}, u32[]{:S(2)}) copy-start(bf16[3,3,64,128]{3,2,1,0:T(8,128)(2,1)} %k3.1) | copy-start | bytes 442372
  4.5 8.8 %copy-start.7 = (bf16[3,3,48,32]{2,3,1,0:T(8,128)(2,1)S(1)}, bf16[3,3,48,32]{2,3,1,0:T(8,128)(2,1)}, u32[]{:S(2)}) copy-start(bf16[3,3,48,32]{2,3,1,0:T(8,128)(2,1)} %param.18) | copy-start | bytes 82948
  4.6 8.8 %copy-start.8 = (bf16[3,3,32,64]{3,2,1,0:T(8,128)(2,1)S(1)}, bf16[3,3,32,64]{3,2,1,0:T(8,128)(2,1)}, u32[]{:S(2)}) copy-start(bf16[3,3,32,64]{3,2,1,0:T(8,128)(2,1)} %k2.1) | copy-start | bytes 110596
  4.6 8.8 %copy-start.11 = (f32[32]{0:T(128)S(1)}, f32[32]{0:T(128)}, u32[]{:S(2)}) copy-start(f32[32]{0:T(128)} %param.19) | copy-start | bytes 388
  4.6 8.7 %copy-start.12 = (f32[64]{0:T(128)S(1)}, f32[64]{0:T(128)}, u32[]{:S(2)}) copy-start(f32[64]{0:T(128)} %param.21) | copy-start | bytes 772
  4.6 8.7 %copy-start.13 = (f32[128]{0:T(128)S(1)}, f32[128]{0:T(128)}, u32[]{:S(2)}) copy-start(f32[128]{0:T(128)} %param.23) | copy-start | bytes 1540
  6.2 11.3 %collective-permute-start.2 = (bf16[18,48,128]{2,1,0:T(8,128)(2,1)S(1)}, bf16[18,48,128]{2,1,0:T(8,128)(2,1)S(1)}, u32[]{:S(2)}, u32[]{:S(2)}) collective-permute-start(bf16[18,48,128]{2,1,0:T(8,128)(2,1)S(1)} %get-tuple-element.60), channel_id=1, source_target_pairs={{0,8},{8,0},{16,24},{24,16},{32,40},{40,32},{48,56},{56,48},{64,72... | collective-permute-start | bytes 663560 | tf_op jit(solution)/shard_map/ppermute | solution.py:18
  7.7 11.2 %collective-permute-start.3 = (bf16[18,48,128]{2,1,0:T(8,128)(2,1)S(1)}, bf16[18,48,128]{2,1,0:T(8,128)(2,1)S(1)}, u32[]{:S(2)}, u32[]{:S(2)}) collective-permute-start(bf16[18,48,128]{2,1,0:T(8,128)(2,1)S(1)} %get-tuple-element.61), channel_id=1, source_target_pairs={{0,120},{8,16},{16,8},{24,32},{32,24},{40,48},{48,40},{56,64},{64,... | collective-permute-start | bytes 663560 | tf_op jit(solution)/shard_map/ppermute | solution.py:18
  17.3 8.2 %copy-start.2 = (bf16[3,3,384,128]{3,2,1,0:T(8,128)(2,1)S(1)}, bf16[3,3,384,128]{3,2,1,0:T(8,128)(2,1)}, u32[]{:S(2)}) copy-start(bf16[3,3,384,128]{3,2,1,0:T(8,128)(2,1)} %d3.1) | copy-start | bytes 2654212
  17.3 8.2 %copy-start.3 = (bf16[3,3,128,256]{3,2,1,0:T(8,128)(2,1)S(1)}, bf16[3,3,128,256]{3,2,1,0:T(8,128)(2,1)}, u32[]{:S(2)}) copy-start(bf16[3,3,128,256]{3,2,1,0:T(8,128)(2,1)} %kc.1) | copy-start | bytes 1769476
  17.3 8.2 %copy-start.4 = (bf16[3,3,192,64]{2,3,1,0:T(8,128)(2,1)S(1)}, bf16[3,3,192,64]{2,3,1,0:T(8,128)(2,1)}, u32[]{:S(2)}) copy-start(bf16[3,3,192,64]{2,3,1,0:T(8,128)(2,1)} %param.28) | copy-start | bytes 663556
  17.4 8.2 %copy-start.6 = (bf16[3,3,96,32]{2,3,1,0:T(8,128)(2,1)S(1)}, bf16[3,3,96,32]{2,3,1,0:T(8,128)(2,1)}, u32[]{:S(2)}) copy-start(bf16[3,3,96,32]{2,3,1,0:T(8,128)(2,1)} %param.30) | copy-start | bytes 165892
  17.4 8.2 %copy-start.9 = (bf16[32,48]{1,0:T(8,128)(2,1)S(1)}, bf16[32,48]{1,0:T(8,128)(2,1)}, u32[]{:S(2)}) copy-start(bf16[32,48]{1,0:T(8,128)(2,1)} %hk.1) | copy-start | bytes 9220
  17.4 8.2 %copy-start.10 = (f32[256]{0:T(256)S(1)}, f32[256]{0:T(256)}, u32[]{:S(2)}) copy-start(f32[256]{0:T(256)} %param.25) | copy-start | bytes 3076
  17.4 8.2 %copy-start.14 = (f32[128]{0:T(128)S(1)}, f32[128]{0:T(128)}, u32[]{:S(2)}) copy-start(f32[128]{0:T(128)} %param.27) | copy-start | bytes 1540
  17.4 8.2 %copy-start.15 = (f32[64]{0:T(128)S(1)}, f32[64]{0:T(128)}, u32[]{:S(2)}) copy-start(f32[64]{0:T(128)} %param.29) | copy-start | bytes 772
  17.4 8.2 %copy-start.16 = (f32[32]{0:T(128)S(1)}, f32[32]{0:T(128)}, u32[]{:S(2)}) copy-start(f32[32]{0:T(128)} %param.31) | copy-start | bytes 388
  17.4 8.2 %copy-start.17 = (f32[48]{0:T(128)S(1)}, f32[48]{0:T(128)}, u32[]{:S(2)}) copy-start(f32[48]{0:T(128)} %param.33) | copy-start | bytes 580
  19.8 9.1 %collective-permute-start.4 = (bf16[27,32,128]{2,1,0:T(8,128)(2,1)S(1)}, bf16[27,32,128]{2,1,0:T(8,128)(2,1)S(1)}, u32[]{:S(2)}, u32[]{:S(2)}) collective-permute-start(bf16[27,32,128]{2,1,0:T(8,128)(2,1)S(1)} %get-tuple-element.67), channel_id=1, source_target_pairs={{0,8},{8,0},{16,24},{24,16},{32,40},{40,32},{48,56},{56,48},{64,72... | collective-permute-start | bytes 663560 | tf_op jit(solution)/shard_map/ppermute | solution.py:18
  19.8 11.5 %collective-permute-start.5 = (bf16[27,32,128]{2,1,0:T(8,128)(2,1)S(1)}, bf16[27,32,128]{2,1,0:T(8,128)(2,1)S(1)}, u32[]{:S(2)}, u32[]{:S(2)}) collective-permute-start(bf16[27,32,128]{2,1,0:T(8,128)(2,1)S(1)} %get-tuple-element.68), channel_id=1, source_target_pairs={{0,120},{8,16},{16,8},{24,32},{32,24},{40,48},{48,40},{56,64},{64,... | collective-permute-start | bytes 663560 | tf_op jit(solution)/shard_map/ppermute | solution.py:18
  33.0 9.2 %collective-permute-start.6 = (bf16[9,64,128]{2,1,0:T(8,128)(2,1)S(1)}, bf16[9,64,128]{2,1,0:T(8,128)(2,1)S(1)}, u32[]{:S(2)}, u32[]{:S(2)}) collective-permute-start(bf16[9,64,128]{2,1,0:T(8,128)(2,1)S(1)} %get-tuple-element.76), channel_id=1, source_target_pairs={{0,8},{8,0},{16,24},{24,16},{32,40},{40,32},{48,56},{56,48},{64,72... | collective-permute-start | bytes 442376 | tf_op jit(solution)/shard_map/ppermute | solution.py:18
  33.1 9.1 %collective-permute-start.7 = (bf16[9,64,128]{2,1,0:T(8,128)(2,1)S(1)}, bf16[9,64,128]{2,1,0:T(8,128)(2,1)S(1)}, u32[]{:S(2)}, u32[]{:S(2)}) collective-permute-start(bf16[9,64,128]{2,1,0:T(8,128)(2,1)S(1)} %get-tuple-element.77), channel_id=1, source_target_pairs={{0,120},{8,16},{16,8},{24,32},{32,24},{40,48},{48,40},{56,64},{64,... | collective-permute-start | bytes 442376 | tf_op jit(solution)/shard_map/ppermute | solution.py:18
  40.4 8.4 %collective-permute-start.10 = (bf16[18,32,128]{2,1,0:T(8,128)(2,1)S(1)}, bf16[18,32,128]{2,1,0:T(8,128)(2,1)S(1)}, u32[]{:S(2)}, u32[]{:S(2)}) collective-permute-start(bf16[18,32,128]{2,1,0:T(8,128)(2,1)S(1)} %get-tuple-element.93), channel_id=1, source_target_pairs={{0,8},{8,0},{16,24},{24,16},{32,40},{40,32},{48,56},{56,48},{64,72... | collective-permute-start | bytes 442376 | tf_op jit(solution)/shard_map/ppermute | solution.py:18
  40.5 9.0 %collective-permute-start.11 = (bf16[18,32,128]{2,1,0:T(8,128)(2,1)S(1)}, bf16[18,32,128]{2,1,0:T(8,128)(2,1)S(1)}, u32[]{:S(2)}, u32[]{:S(2)}) collective-permute-start(bf16[18,32,128]{2,1,0:T(8,128)(2,1)S(1)} %get-tuple-element.94), channel_id=1, source_target_pairs={{0,120},{8,16},{16,8},{24,32},{32,24},{40,48},{48,40},{56,64},{64,... | collective-permute-start | bytes 442376 | tf_op jit(solution)/shard_map/ppermute | solution.py:18
  44.1 8.5 %collective-permute-start.9 = (bf16[9,64,128]{2,1,0:T(8,128)(2,1)S(1)}, bf16[9,64,128]{2,1,0:T(8,128)(2,1)S(1)}, u32[]{:S(2)}, u32[]{:S(2)}) collective-permute-start(bf16[9,64,128]{2,1,0:T(8,128)(2,1)S(1)} %get-tuple-element.83), channel_id=1, source_target_pairs={{0,120},{8,16},{16,8},{24,32},{32,24},{40,48},{48,40},{56,64},{64,... | collective-permute-start | bytes 442376 | tf_op jit(solution)/shard_map/ppermute | solution.py:18
  48.8 5.1 %collective-permute-start.8 = (bf16[9,64,128]{2,1,0:T(8,128)(2,1)S(1)}, bf16[9,64,128]{2,1,0:T(8,128)(2,1)S(1)}, u32[]{:S(2)}, u32[]{:S(2)}) collective-permute-start(bf16[9,64,128]{2,1,0:T(8,128)(2,1)S(1)} %get-tuple-element.83), channel_id=1, source_target_pairs={{0,8},{8,0},{16,24},{24,16},{32,40},{40,32},{48,56},{56,48},{64,72... | collective-permute-start | bytes 442376 | tf_op jit(solution)/shard_map/ppermute | solution.py:18
  56.7 1.4 %copy-start.1 = (bf16[2,48,8,1024]{3,2,1,0:T(8,128)(2,1)S(1)}, bf16[2,48,8,1024]{3,2,1,0:T(8,128)(2,1)}, u32[]{:S(2)}) copy-start(bf16[2,48,8,1024]{3,2,1,0:T(8,128)(2,1)} %param.17) | copy-start | bytes 4718596

commit v4 on v3

--- a/solution.py
+++ b/solution.py
@@ -41,7 +41,7 @@
     pack(far, [jnp.where(even, a, b) for a, b in zip(before, after)])
 
 
-def call(body, name, out_shapes, scratch, args, limit=16, flops=0):
+def call(body, name, out_shapes, scratch, args, limit=16, flops=0, aliases=None):
     specs = [pl.BlockSpec(memory_space=pltpu.VMEM)] * len(args)
     return pl.pallas_call(
         body,
@@ -50,6 +50,7 @@
         in_specs=specs,
         out_specs=[pl.BlockSpec(memory_space=pltpu.VMEM)] * len(out_shapes),
         scratch_shapes=scratch,
+        input_output_aliases=aliases or {},
         cost_estimate=pl.CostEstimate(flops=flops, transcendentals=0, bytes_accessed=0),
         compiler_params=pltpu.CompilerParams(vmem_limit_bytes=limit * 2**20),
     )(*args)
@@ -74,8 +75,12 @@
     return jnp.dot(a, b, preferred_element_type=F32)
 
 
-def silu(t):
-    return t * (0.5 * jnp.tanh(0.5 * t) + 0.5)
+def silu(half):
+    return half * (jnp.tanh(half) + 1.0)
+
+
+def halved(weights):
+    return (weights.astype(F32) * 0.5).astype(BF16)
 
 
 def lane_mask(flags):
@@ -155,7 +160,7 @@
     return dot(turn, part).astype(BF16)
 
 
-def cols_kernel(x, near, far):
+def cols_kernel(x, near, far, _):
     lane = iota((1, LANES), 1)
     size = x.shape[1] // 4
     even = is_even("tx")
@@ -357,13 +362,17 @@
     pack(send, [res[n * size : (n + 1) * size] for n in range(4)])
 
 
-def skip_three_kernel(s3, w, b, out, xs):
+def skip_three_kernel(s3, c, w, wu, b, out, xs, xc):
+    fill(xc, 0, [c[...]])
+    half = wu.shape[3] // 2
     for r in range(6):
         fill(xs, r, [s3[r, p] for p in range(2)])
     for r in range(4):
         res = dot(w[...], side(*[window(xs, r, p, 3, 3) for p in range(2)]))
         for p in range(2):
-            out[r, p] = res[:, p * WIDE : (p + 1) * WIDE] + b[...]
+            start = half if r < 2 else 0
+            own = dot(wu[1 - r % 2, p, :, start : start + half], window(xc, 0, p, 1, 2))
+            out[r, p] = res[:, p * WIDE : (p + 1) * WIDE] + own + b[...]
 
 
 def skip_two_kernel(s2, middle, s_out, w, b, out, near, far, xs):
@@ -410,23 +419,21 @@
             out[k, p] = dot(w[...], window(xs, 3 * k, p, 3, 3)[:, :256]) + b[...]
 
 
-def back_kernel(c, c_near, c_far, pre3, pre2, wu3, wu2, out, xc, xb):
+def back_kernel(c_near, c_far, pre3, pre2, wu3, wu2, out, xc, xb):
     flags = edges()
     above, below = received(c_near, c_far, "ty")
     halo = lambda packed: [jnp.concatenate([unpack(packed, n, 4) for n in range(4)], axis=0)]
     fill(xc, 0, halo(above), flags[0])
-    fill(xc, 1, [c[...]])
-    fill(xc, 2, halo(below), flags[1])
+    fill(xc, 1, halo(below), flags[1])
     mask = lane_mask(flags)
+    half = wu3.shape[3] // 2
     slabs = {}
-    for a in range(2):
+    for r in range(4):
+        start = 0 if r < 2 else half
         for p in range(2):
-            res = dot(wu3[a, p], side(window(xc, 0, p, 2, 2), window(xc, 1, p, 2, 2)))
-            for n in range(2):
-                r = 2 * n + 1 - a
-                y = silu(res[:, n * WIDE : (n + 1) * WIDE] + pre3[r, p])
-                inside = mask * flags[0] if r == 0 else mask * flags[1] if r == 3 else mask
-                slabs[r, p] = (y * inside).astype(BF16)
+            res = dot(wu3[1 - r % 2, p, :, start : start + half], window(xc, r // 2, p, 1, 2))
+            inside = mask * flags[0] if r == 0 else mask * flags[1] if r == 3 else mask
+            slabs[r, p] = (silu(res + pre3[r, p]) * inside).astype(BF16)
     for r in range(4):
         fill(xb, r, [slabs[r, p] for p in range(2)])
 
@@ -520,7 +527,7 @@
         for dx in sums(b)[j]:
             value = tap(dy, dx).astype(F32)
             total = value if total is None else total + value
-    return total.astype(BF16)
+    return (total * 0.5).astype(BF16)
 
 
 def placed(parts, width):
@@ -546,26 +553,26 @@
 
 
 def early_kernel(k1, k2, k3, r1, r2, r3, g1, low, high, top, bottom, w2, g2, w3, b1, b2, b3):
-    w1 = placed([k1[n] for n in NINE], 9 * k1.shape[3])
+    w1 = halved(placed([k1[n] for n in NINE], 9 * k1.shape[3]))
     step = 3 * k1.shape[3]
     g1[...] = grouped(w1, 3)
     for ref, start in ((low, step), (high, 0), (top, 0), (bottom, 2 * step)):
         i, j = iota((w1.shape[1], ref.shape[1]), 0), iota((w1.shape[1], ref.shape[1]), 1)
         ref[...] = dot(w1, one_hot(i == j + start)).astype(BF16)
-    flat = flip(k2[...].reshape(-1, k2.shape[3]))
+    flat = halved(flip(k2[...].reshape(-1, k2.shape[3])))
     w2[...] = grouped(flat, 2)
     g2[...] = grouped(flat, 3)
-    w3[...] = flip(k3[...].reshape(-1, k3.shape[3]))
+    w3[...] = halved(flip(k3[...].reshape(-1, k3.shape[3])))
     for r, b in ((r1, b1), (r2, b2), (r3, b3)):
-        b[...] = column(r[...], WIDE)
+        b[...] = column(r[...] * 0.5, WIDE)
 
 
 def late_kernel(
     kc, d3, d2, d1, hk, rc, r3, r2, r1, rh, wc, wu3, ws3, wu2, gs2, wu1, ws1, gs1, wh, bc, b3, b2, b1, bh
 ):
-    wc[...] = flip(kc[...].reshape(-1, kc.shape[3]))
+    wc[...] = halved(flip(kc[...].reshape(-1, kc.shape[3])))
     for r, b in ((rc, bc), (r3, b3), (r2, b2), (r1, b1)):
-        b[...] = column(r[...], b.shape[1])
+        b[...] = column(r[...] * 0.5, b.shape[1])
     bh[...] = column(rh[...], bh.shape[1], 8)
     up3, up2, up1 = wu3.shape[3] // 4, wu2.shape[2] // 4, wu1.shape[1] // 4
     n2, n1 = d2.shape[2], d1.shape[2]
@@ -577,10 +584,10 @@
             wu2[b, (1 - a) * n2 : (2 - a) * n2] = jnp.concatenate(wide, axis=1)
             wide = [summed(lambda y, x: d1[y, x, :, :up1], a, b, i, j) for i, j in FOUR]
             wu1[(2 * a + b) * n1 : (2 * a + b + 1) * n1] = placed(wide, wu1.shape[1])
-    ws3[...] = flip(jnp.concatenate([d3[y, x, up3:, :] for y, x in NINE], axis=0))
-    skips = [d2[y, x, :, up2:] for y, x in NINE]
+    ws3[...] = halved(flip(jnp.concatenate([d3[y, x, up3:, :] for y, x in NINE], axis=0)))
+    skips = [halved(d2[y, x, :, up2:]) for y, x in NINE]
     gs2[...] = grouped(placed(skips, 9 * skips[0].shape[1]), 2)
-    ws1[...] = placed([d1[y, x, :, up1:] for y, x in NINE], ws1.shape[1])
+    ws1[...] = halved(placed([d1[y, x, :, up1:] for y, x in NINE], ws1.shape[1]))
     gs1[...] = grouped(ws1[...], 3)
     v, c = hk.shape[1], hk.shape[0]
     spread = one_hot(iota((v * 8, v), 0) // 8 == iota((v * 8, v), 1))
@@ -614,7 +621,14 @@
     v = fields.shape[1]
 
     x = fields.reshape(2, v * 8, 1024)
-    near, far = call(cols_kernel, "cols", [((2, 2 * v, LANES), BF16)] * 2, [], [x])
+    near, far, x = call(
+        cols_kernel,
+        "cols",
+        [((2, 2 * v, LANES), BF16)] * 2 + [(x.shape, BF16)],
+        [],
+        [x],
+        aliases={0: 2},
+    )
     cols = swap(near, far, "tx")
 
     row = lambda bias: bias[None, :]
@@ -724,16 +738,16 @@
         skip_three_kernel,
         "skip_three",
         [((4, 2, c3, WIDE), F32)],
-        [pltpu.VMEM((6, 4, c3, WIDE), BF16)],
-        [s3, ws3, ob3],
+        [pltpu.VMEM((6, 4, c3, WIDE), BF16), pltpu.VMEM((1, 3, c4, WIDE), BF16)],
+        [s3, coarse, ws3, wu3, ob3],
         flops=10**9,
     )
     (back_two,) = call(
         back_kernel,
         "back",
         [((6, 4, c2, WIDE), BF16)],
-        [pltpu.VMEM((3, 3, c4, WIDE), BF16), pltpu.VMEM((4, 4, c3, WIDE), BF16)],
-        [coarse, *halo, pre3, pre2, wu3, wu2],
+        [pltpu.VMEM((2, 3, c4, WIDE), BF16), pltpu.VMEM((4, 4, c3, WIDE), BF16)],
+        [*halo, pre3, pre2, wu3, wu2],
     )
     (back_one,) = call(
         last_kernel,

time: 61 us -> 59.5 us (0.975)
  waiting for transfers between devices: 7.63 us -> 7.01 us
  local copies, waits for them, and re-layouts: 2.12 us -> 1.51 us
    ppermute x6, waiting for transfers between devices: 6.3 us -> 5.67 us  [swap(): lax.ppermute(far_part, axis, far)]
    unnamed x36 -> x33, local copies, waits for them, and re-layouts: 2.12 us -> 1.51 us
  transfers between devices with their start and end apart: 12 -> 12, of which waited for: 6 -> 6; matrix products, arithmetic and copies ran while one was open for 0% -> 0% of each run, Pallas kernels for 25% -> 27%
where the time goes in v4:
time: 59.5 us; the launch traced here: 59.3 us
  starting transfers between devices  25.8 us (43%)
  Pallas kernels  24.5 us (41%)
  waiting for transfers between devices  7.01 us (12%)
  local copies, waits for them, and re-layouts  1.51 us (3%)
    ppermute x6, starting transfers between devices, swap(): lax.ppermute(far_part, axis, far)  23.9 us
    pallas_call x16, Pallas kernels, call(): pl.pallas_call(body, name=name, out_shape=[jax.ShapeDtypeStruct(s, d) for...  21.9 us
    ppermute x6, waiting for transfers between devices, swap(): lax.ppermute(far_part, axis, far)  5.67 us
    pallas_call x1, Pallas kernels, body(): pl.pallas_call(head_kernel_body, name='head', out_shape=jax.ShapeDtypeStr...  2.54 us
    ppermute x6, starting transfers between devices, swap(): lax.ppermute(near_part, axis, near)  1.9 us
    unnamed x33, local copies, waits for them, and re-layouts  1.51 us
    ppermute x6, waiting for transfers between devices, swap(): lax.ppermute(near_part, axis, near)  1.34 us
  transfers between devices with their start and end apart: 12, of which 6 were waited for; matrix products, arithmetic and copies ran while one was open for 0% of the time, Pallas kernels for 27%

profile of v4, /device:TPU:24, one launch (start us, length us, event | category | flops | bytes accessed | tf_op | source)
XLA Modules:
  0.0 59.3 jit_solution(4099871052836776010)
XLA Ops:
  0.0 1.4 %copy.21 = bf16[2,48,8,1024]{3,2,1,0:T(8,128)(2,1)S(1)} copy(bf16[2,48,8,1024]{3,2,1,0:T(8,128)(2,1)} %param.17) | data formatting | bytes 3145728
  1.4 0.1 cols.1
  1.6 0.1 collective-permute-start
  1.7 0.8 %collective-permute-start.1 = (bf16[2,96,128]{2,1,0:T(8,128)(2,1)S(1)}, bf16[2,96,128]{2,1,0:T(8,128)(2,1)S(1)}, u32[]{:S(2)}, u32[]{:S(2)}) collective-permute-start(bf16[2,96,128]{2,1,0:T(8,128)(2,1)S(1)} %get-tuple-element.55), channel_id=1, source_target_pairs={{0,7},{1,2},{2,1},{3,4},{4,3},{5,6},{6,5},{7,0},{8,15},{9,10},{10,... | collective-permute-start | bytes 147464 | tf_op jit(solution)/shard_map/ppermute | solution.py:18
  2.5 2.0 %main.1 = bf16[8,8,48,256]{3,2,1,0:T(8,128)(2,1)S(1)} custom-call(bf16[2,384,1024]{2,1,0:T(8,128)(2,1)S(1)} %get-tuple-element.53.x.fields), custom_call_target="tpu_custom_call" | custom-call | flops 1000000000 | tf_op jit(solution)/shard_map/main/pallas_call | solution.py:46
  4.6 0.6 %collective-permute-done.1.cols_far = bf16[2,96,128]{2,1,0:T(8,128)(2,1)S(1)} collective-permute-done((bf16[2,96,128]{2,1,0:T(8,128)(2,1)S(1)}, bf16[2,96,128]{2,1,0:T(8,128)(2,1)S(1)}, u32[]{:S(2)}, u32[]{:S(2)}) %collective-permute-start.1) | collective-permute-done | bytes 49184 | tf_op jit(solution)/shard_map/ppermute | solution.py:18
  5.3 0.9 %ends.1 = (bf16[8,8,48,128]{3,2,1,0:T(8,128)(2,1)S(1)}, bf16[18,48,128]{2,1,0:T(8,128)(2,1)S(1)}, bf16[18,48,128]{2,1,0:T(8,128)(2,1)S(1)}) custom-call(bf16[2,384,1024]{2,1,0:T(8,128)(2,1)S(1)} %get-tuple-element.53.x.fields, bf16[8,8,48,256]{3,2,1,0:T(8,128)(2,1)S(1)} %main.1, bf16[2,96,128]{2,1,0:T(8,128)(2,1)S(1)} %collective-permute-done.cols_near, ...), custom_call_target="tpu_custom_call" | custom-call | tf_op jit(solution)/shard_map/ends/pallas_call | solution.py:46
  6.2 1.6 %collective-permute-start.2 = (bf16[18,48,128]{2,1,0:T(8,128)(2,1)S(1)}, bf16[18,48,128]{2,1,0:T(8,128)(2,1)S(1)}, u32[]{:S(2)}, u32[]{:S(2)}) collective-permute-start(bf16[18,48,128]{2,1,0:T(8,128)(2,1)S(1)} %get-tuple-element.62), channel_id=1, source_target_pairs={{0,8},{8,0},{16,24},{24,16},{32,40},{40,32},{48,56},{56,48},{64,72... | collective-permute-start | bytes 663560 | tf_op jit(solution)/shard_map/ppermute | solution.py:18
  7.7 5.6 %collective-permute-start.3 = (bf16[18,48,128]{2,1,0:T(8,128)(2,1)S(1)}, bf16[18,48,128]{2,1,0:T(8,128)(2,1)S(1)}, u32[]{:S(2)}, u32[]{:S(2)}) collective-permute-start(bf16[18,48,128]{2,1,0:T(8,128)(2,1)S(1)} %get-tuple-element.63), channel_id=1, source_target_pairs={{0,120},{8,16},{16,8},{24,32},{32,24},{40,48},{48,40},{56,64},{64,... | collective-permute-start | bytes 663560 | tf_op jit(solution)/shard_map/ppermute | solution.py:18
  13.3 0.9 %early.1 = (bf16[96,720]{1,0:T(8,128)(2,1)S(1)}, bf16[32,288]{1,0:T(8,128)(2,1)S(1)}, bf16[32,288]{1,0:T(8,128)(2,1)S(1)}, bf16[32,144]{1,0:T(8,128)(2,1)S(1)}, ...) custom-call(bf16[3,3,32,48]{3,2,1,0:T(8,128)(2,1)S(1)} %bitcast.18, ...), custom_call_target="tpu_custom_call" | custom-call | tf_op jit(solution)/shard_map/early/pallas_call | solution.py:46
  14.3 3.0 %inner.1 = (bf16[6,8,32,384]{3,2,1,0:T(8,128)(2,1)S(1)}, bf16[2,4,32,384]{3,2,1,0:T(8,128)(2,1)S(1)}, f32[2,8,32,384]{3,2,1,0:T(8,128)S(1)}) custom-call(bf16[8,8,48,256]{3,2,1,0:T(8,128)(2,1)S(1)} %main.1, bf16[8,8,48,128]{3,2,1,0:T(8,128)(2,1)S(1)} %get-tuple-element.56.ends, bf16[96,720]{1,0:T(8,128)(2,1)S(1)} %get-tuple-element.57.w, ...), custom_call_target="tpu_custom_call" | custom-call | flops 1000000000 | tf_op jit(solution)/shard_map/inner/pallas_call | solution.py:46
  17.4 1.5 %collective-permute-done.3.f_far = bf16[18,48,128]{2,1,0:T(8,128)(2,1)S(1)} collective-permute-done((bf16[18,48,128]{2,1,0:T(8,128)(2,1)S(1)}, bf16[18,48,128]{2,1,0:T(8,128)(2,1)S(1)}, u32[]{:S(2)}, u32[]{:S(2)}) %collective-permute-start.3) | collective-permute-done | bytes 221216 | tf_op jit(solution)/shard_map/ppermute | solution.py:18
  18.9 0.8 %outer.1 = (bf16[2,8,32,384]{3,2,1,0:T(8,128)(2,1)S(1)}, bf16[2,4,32,384]{3,2,1,0:T(8,128)(2,1)S(1)}, bf16[27,32,128]{2,1,0:T(8,128)(2,1)S(1)}, bf16[27,32,128]{2,1,0:T(8,128)(2,1)S(1)}) custom-call(bf16[18,48,128]{2,1,0:T(8,128)(2,1)S(1)} %collective-permute-done.2.f_near, bf16[18,48,128]{2,1,0:T(8,128)(2,1)S(1)} %collective-permute-done.3.f_far, ...), custom_call_target="tpu_custom_call" | custom-call | tf_op jit(solution)/shard_map/outer/pallas_call | solution.py:46
  19.8 5.7 %collective-permute-start.5 = (bf16[27,32,128]{2,1,0:T(8,128)(2,1)S(1)}, bf16[27,32,128]{2,1,0:T(8,128)(2,1)S(1)}, u32[]{:S(2)}, u32[]{:S(2)}) collective-permute-start(bf16[27,32,128]{2,1,0:T(8,128)(2,1)S(1)} %get-tuple-element.70), channel_id=1, source_target_pairs={{0,120},{8,16},{16,8},{24,32},{32,24},{40,48},{48,40},{56,64},{64,... | collective-permute-start | bytes 663560 | tf_op jit(solution)/shard_map/ppermute | solution.py:18
  25.6 2.0 %late.1 = (bf16[256,1152]{1,0:T(8,128)(2,1)S(1)}, bf16[2,2,128,1024]{3,2,1,0:T(8,128)(2,1)S(1)}, bf16[128,1152]{1,0:T(8,128)(2,1)S(1)}, bf16[2,128,512]{2,1,0:T(...) custom-call(bf16[3,3,128,256]{3,2,1,0:T(8,128)(2,1)S(1)} %copy-done., ...), custom_call_target="tpu_custom_call" | custom-call | flops 500000000 | tf_op jit(solution)/shard_map/late/pallas_call | solution.py:46
  27.6 0.5 middle.1
  28.1 0.8 %skip_inner.1._.pre_in = f32[6,8,32,256]{3,2,1,0:T(8,128)S(1)} custom-call(bf16[6,8,32,384]{3,2,1,0:T(8,128)(2,1)S(1)} %get-tuple-element.65.skip_in.s_in, bf16[2,8,32,384]{3,2,1,0:T(8,128)(2,1)S(1)} %get-tuple-element.74.s_out, bf16[96,480]{1,0:T(8,128)(2,1)S(1)} %get-tuple-element.75.w, f32[32,256]{1,0:T(8,128)S(1)} %get-tuple-element.76.b), custom_call_target="tpu_custom_call" | custom-call | flops 1000000000 | tf_op jit(solution)/shard_map/skip_inner/pallas_call | solution.py:46
  28.9 2.4 %collective-permute-done.5.p_far = bf16[27,32,128]{2,1,0:T(8,128)(2,1)S(1)} collective-permute-done((bf16[27,32,128]{2,1,0:T(8,128)(2,1)S(1)}, bf16[27,32,128]{2,1,0:T(8,128)(2,1)S(1)}, u32[]{:S(2)}, u32[]{:S(2)}) %collective-permute-start.5) | collective-permute-done | bytes 221216 | tf_op jit(solution)/shard_map/ppermute | solution.py:18
  31.3 1.5 %two.1 = (bf16[6,4,64,384]{3,2,1,0:T(8,128)(2,1)S(1)}, bf16[4,2,64,384]{3,2,1,0:T(8,128)(2,1)S(1)}, bf16[9,64,128]{2,1,0:T(8,128)(2,1)S(1)}, bf16[9,64,128]{2,1,0:T(8,128)(2,1)S(1)}) custom-call(bf16[2,4,32,384]{3,2,1,0:T(8,128)(2,1)S(1)} %get-tuple-element.61.pooled_in, bf16[2,4,32,384]{3,2,1,0:T(8,128)(2,1)S(1)} %get-tuple-element.68.pooled, ...), custom_call_target="tpu_custom_call" | custom-call | tf_op jit(solution)/shard_map/two/pallas_call | solution.py:46
  32.8 5.3 %collective-permute-start.7 = (bf16[9,64,128]{2,1,0:T(8,128)(2,1)S(1)}, bf16[9,64,128]{2,1,0:T(8,128)(2,1)S(1)}, u32[]{:S(2)}, u32[]{:S(2)}) collective-permute-start(bf16[9,64,128]{2,1,0:T(8,128)(2,1)S(1)} %get-tuple-element.79), channel_id=1, source_target_pairs={{0,120},{8,16},{16,8},{24,32},{32,24},{40,48},{48,40},{56,64},{64,... | collective-permute-start | bytes 442376 | tf_op jit(solution)/shard_map/ppermute | solution.py:18
  38.2 2.0 %skip_two.1 = (f32[6,4,64,384]{3,2,1,0:T(8,128)S(1)}, bf16[18,32,128]{2,1,0:T(8,128)(2,1)S(1)}, bf16[18,32,128]{2,1,0:T(8,128)(2,1)S(1)}) custom-call(bf16[6,4,64,384]{3,2,1,0:T(8,128)(2,1)S(1)} %get-tuple-element.90.s2, bf16[2,4,64,384]{3,2,1,0:T(8,128)(2,1)S(1)} %middle.1, bf16[2,8,32,384]{3,2,1,0:T(8,128)(2,1)S(1)} %get-tuple-element.74.s_out, ...), custom_call_target="tpu_custom_call" | custom-call | flops 1000000000 | tf_op jit(solution)/shard_map/skip_two/pallas_call | solution.py:46
  40.2 1.7 %collective-permute-start.11 = (bf16[18,32,128]{2,1,0:T(8,128)(2,1)S(1)}, bf16[18,32,128]{2,1,0:T(8,128)(2,1)S(1)}, u32[]{:S(2)}, u32[]{:S(2)}) collective-permute-start(bf16[18,32,128]{2,1,0:T(8,128)(2,1)S(1)} %get-tuple-element.96), channel_id=1, source_target_pairs={{0,120},{8,16},{16,8},{24,32},{32,24},{40,48},{48,40},{56,64},{64,... | collective-permute-start | bytes 442376 | tf_op jit(solution)/shard_map/ppermute | solution.py:18
  42.0 1.8 %three.1 = (bf16[6,2,128,384]{3,2,1,0:T(8,128)(2,1)S(1)}, bf16[256,384]{1,0:T(8,128)(2,1)S(1)}, bf16[9,64,128]{2,1,0:T(8,128)(2,1)S(1)}) custom-call(bf16[4,2,64,384]{3,2,1,0:T(8,128)(2,1)S(1)} %get-tuple-element.77.pooled2, bf16[9,64,128]{2,1,0:T(8,128)(2,1)S(1)} %collective-permute-done.6.q_near, bf16[9,64,128]{2,1,0:T(8,128)(2,1)S(1)} %collective-permute-done.7.q_far, ...), custom_call_target="tpu_custom_call" | custom-call | tf_op jit(solution)/shard_map/three/pallas_call | solution.py:46
  43.8 4.7 %collective-permute-start.9 = (bf16[9,64,128]{2,1,0:T(8,128)(2,1)S(1)}, bf16[9,64,128]{2,1,0:T(8,128)(2,1)S(1)}, u32[]{:S(2)}, u32[]{:S(2)}) collective-permute-start(bf16[9,64,128]{2,1,0:T(8,128)(2,1)S(1)} %get-tuple-element.84), channel_id=1, source_target_pairs={{0,120},{8,16},{16,8},{24,32},{32,24},{40,48},{48,40},{56,64},{64,... | collective-permute-start | bytes 442376 | tf_op jit(solution)/shard_map/ppermute | solution.py:18
  48.6 0.6 %collective-permute-done.11.s_far = bf16[18,32,128]{2,1,0:T(8,128)(2,1)S(1)} collective-permute-done((bf16[18,32,128]{2,1,0:T(8,128)(2,1)S(1)}, bf16[18,32,128]{2,1,0:T(8,128)(2,1)S(1)}, u32[]{:S(2)}, u32[]{:S(2)}) %collective-permute-start.11) | collective-permute-done | bytes 147488 | tf_op jit(solution)/shard_map/ppermute | solution.py:18
  49.1 0.7 %skip_outer.1.pre_out = f32[2,8,32,256]{3,2,1,0:T(8,128)S(1)} custom-call(bf16[6,8,32,384]{3,2,1,0:T(8,128)(2,1)S(1)} %get-tuple-element.65.skip_in.s_in, bf16[2,8,32,384]{3,2,1,0:T(8,128)(2,1)S(1)} %get-tuple-element.74.s_out, bf16[18,32,128]{2,1,0:T(8,128)(2,1)S(1)} %collective-permute-done.10.s_near, ...), custom_call_target="tpu_custom_call" | custom-call | flops 500000000 | tf_op jit(solution)/shard_map/skip_outer/pallas_call | solution.py:46
  49.8 2.0 %skip_three.1.pre3 = f32[4,2,128,384]{3,2,1,0:T(8,128)S(1)} custom-call(bf16[6,2,128,384]{3,2,1,0:T(8,128)(2,1)S(1)} %get-tuple-element.85.s3, bf16[256,384]{1,0:T(8,128)(2,1)S(1)} %get-tuple-element.86.c, bf16[128,1152]{1,0:T(8,128)(2,1)S(1)} %get-tuple-element.87.w, bf16[2,2,128,1024]{3,2,1,0:T(8,128)(2,1)S(1)} %get-tuple-element.88.wu.wu3, ...), custom_call_target="tpu_custom_call" | custom-call | flops 1000000000 | tf_op jit(solution)/shard_map/skip_three/pallas_call | solution.py:46
  51.8 0.6 collective-permute-done.9.c_far
  52.4 1.3 %collective-permute-done.8.c_near = bf16[9,64,128]{2,1,0:T(8,128)(2,1)S(1)} collective-permute-done((bf16[9,64,128]{2,1,0:T(8,128)(2,1)S(1)}, bf16[9,64,128]{2,1,0:T(8,128)(2,1)S(1)}, u32[]{:S(2)}, u32[]{:S(2)}) %collective-permute-start.8) | collective-permute-done | bytes 147488 | tf_op jit(solution)/shard_map/ppermute | solution.py:18
  53.7 2.2 %back.1.bt = bf16[6,4,64,384]{3,2,1,0:T(8,128)(2,1)S(1)} custom-call(bf16[9,64,128]{2,1,0:T(8,128)(2,1)S(1)} %collective-permute-done.8.c_near, bf16[9,64,128]{2,1,0:T(8,128)(2,1)S(1)} %collective-permute-done.9.c_far, f32[4,2,128,384]{3,2,1,0:T(8,128)S(1)} %skip_three.1.pre3, f32[6,4,64,384]{3,2,1,0:T(8,128)S(1)} %get-tuple-element.93.pre2, ...), custom_call_target="tpu_custom_call" | custom-call | tf_op jit(solution)/shard_map/back/pallas_call | solution.py:46
  55.9 0.7 %last.1 = bf16[2,8,32,1024]{3,2,1,0:T(8,128)(2,1)S(1)} custom-call(bf16[6,4,64,384]{3,2,1,0:T(8,128)(2,1)S(1)} %back.1.bt, f32[6,8,32,256]{3,2,1,0:T(8,128)S(1)} %skip_inner.1._.pre_in, f32[2,8,32,256]{3,2,1,0:T(8,128)S(1)} %skip_outer.1.pre_out, bf16[128,256]{1,0:T(8,128)(2,1)S(1)} %get-tuple-element.98.wu), custom_call_target="tpu_custom_call" | custom-call | tf_op jit(solution)/shard_map/last/pallas_call | solution.py:46
  56.6 2.5 %head.1 = f32[2,384,1024]{2,1,0:T(8,128)} custom-call(bf16[2,384,1024]{2,1,0:T(8,128)(2,1)S(1)} %get-tuple-element.53.x.fields, bf16[2,256,1024]{2,1,0:T(8,128)(2,1)S(1)} %bitcast.15, bf16[384,256]{1,0:T(8,128)(2,1)S(1)} %get-tuple-element.99.w, f32[384,256]{1,0:T(8,128)S(1)} %get-tuple-element.100.offset), custom_call_target="tpu_custom_call" | custom-call | tf_op jit(solution)/shard_map/head/pallas_call | solution.py:759
  (42 shorter events, 0.4 us)
Async XLA Ops:
  1.6 3.0 %collective-permute-start = (bf16[2,96,128]{2,1,0:T(8,128)(2,1)S(1)}, bf16[2,96,128]{2,1,0:T(8,128)(2,1)S(1)}, u32[]{:S(2)}, u32[]{:S(2)}) collective-permute-start(bf16[2,96,128]{2,1,0:T(8,128)(2,1)S(1)} %get-tuple-element.54), channel_id=1, source_target_pairs={{0,1},{1,0},{2,3},{3,2},{4,5},{5,4},{6,7},{7,6},{8,9},{9,8},{10,11... | collective-permute-start | bytes 147464 | tf_op jit(solution)/shard_map/ppermute | solution.py:18
  1.7 3.6 %collective-permute-start.1 = (bf16[2,96,128]{2,1,0:T(8,128)(2,1)S(1)}, bf16[2,96,128]{2,1,0:T(8,128)(2,1)S(1)}, u32[]{:S(2)}, u32[]{:S(2)}) collective-permute-start(bf16[2,96,128]{2,1,0:T(8,128)(2,1)S(1)} %get-tuple-element.55), channel_id=1, source_target_pairs={{0,7},{1,2},{2,1},{3,4},{4,3},{5,6},{6,5},{7,0},{8,15},{9,10},{10,... | collective-permute-start | bytes 147464 | tf_op jit(solution)/shard_map/ppermute | solution.py:18
  4.5 8.8 %copy-start.3 = (bf16[3,3,64,128]{3,2,1,0:T(8,128)(2,1)S(1)}, bf16[3,3,64,128]{3,2,1,0:T(8,128)(2,1)}, u32[]{:S(2)}) copy-start(bf16[3,3,64,128]{3,2,1,0:T(8,128)(2,1)} %k3.1) | copy-start | bytes 442372
  4.5 8.8 %copy-start.5 = (bf16[3,3,48,32]{2,3,1,0:T(8,128)(2,1)S(1)}, bf16[3,3,48,32]{2,3,1,0:T(8,128)(2,1)}, u32[]{:S(2)}) copy-start(bf16[3,3,48,32]{2,3,1,0:T(8,128)(2,1)} %param.18) | copy-start | bytes 82948
  4.6 8.8 %copy-start.6 = (bf16[3,3,32,64]{3,2,1,0:T(8,128)(2,1)S(1)}, bf16[3,3,32,64]{3,2,1,0:T(8,128)(2,1)}, u32[]{:S(2)}) copy-start(bf16[3,3,32,64]{3,2,1,0:T(8,128)(2,1)} %k2.1) | copy-start | bytes 110596
  4.6 8.8 %copy-start.9 = (f32[32]{0:T(128)S(1)}, f32[32]{0:T(128)}, u32[]{:S(2)}) copy-start(f32[32]{0:T(128)} %param.19) | copy-start | bytes 388
  4.6 8.7 %copy-start.10 = (f32[64]{0:T(128)S(1)}, f32[64]{0:T(128)}, u32[]{:S(2)}) copy-start(f32[64]{0:T(128)} %param.21) | copy-start | bytes 772
  4.6 8.7 %copy-start.11 = (f32[128]{0:T(128)S(1)}, f32[128]{0:T(128)}, u32[]{:S(2)}) copy-start(f32[128]{0:T(128)} %param.23) | copy-start | bytes 1540
  6.2 11.2 %collective-permute-start.2 = (bf16[18,48,128]{2,1,0:T(8,128)(2,1)S(1)}, bf16[18,48,128]{2,1,0:T(8,128)(2,1)S(1)}, u32[]{:S(2)}, u32[]{:S(2)}) collective-permute-start(bf16[18,48,128]{2,1,0:T(8,128)(2,1)S(1)} %get-tuple-element.62), channel_id=1, source_target_pairs={{0,8},{8,0},{16,24},{24,16},{32,40},{40,32},{48,56},{56,48},{64,72... | collective-permute-start | bytes 663560 | tf_op jit(solution)/shard_map/ppermute | solution.py:18
  7.7 11.2 %collective-permute-start.3 = (bf16[18,48,128]{2,1,0:T(8,128)(2,1)S(1)}, bf16[18,48,128]{2,1,0:T(8,128)(2,1)S(1)}, u32[]{:S(2)}, u32[]{:S(2)}) collective-permute-start(bf16[18,48,128]{2,1,0:T(8,128)(2,1)S(1)} %get-tuple-element.63), channel_id=1, source_target_pairs={{0,120},{8,16},{16,8},{24,32},{32,24},{40,48},{48,40},{56,64},{64,... | collective-permute-start | bytes 663560 | tf_op jit(solution)/shard_map/ppermute | solution.py:18
  17.3 8.2 %copy-start = (bf16[3,3,384,128]{3,2,1,0:T(8,128)(2,1)S(1)}, bf16[3,3,384,128]{3,2,1,0:T(8,128)(2,1)}, u32[]{:S(2)}) copy-start(bf16[3,3,384,128]{3,2,1,0:T(8,128)(2,1)} %d3.1) | copy-start | bytes 2654212
  17.3 8.2 %copy-start.1 = (bf16[3,3,128,256]{3,2,1,0:T(8,128)(2,1)S(1)}, bf16[3,3,128,256]{3,2,1,0:T(8,128)(2,1)}, u32[]{:S(2)}) copy-start(bf16[3,3,128,256]{3,2,1,0:T(8,128)(2,1)} %kc.1) | copy-start | bytes 1769476
  17.3 8.2 %copy-start.2 = (bf16[3,3,192,64]{2,3,1,0:T(8,128)(2,1)S(1)}, bf16[3,3,192,64]{2,3,1,0:T(8,128)(2,1)}, u32[]{:S(2)}) copy-start(bf16[3,3,192,64]{2,3,1,0:T(8,128)(2,1)} %param.28) | copy-start | bytes 663556
  17.3 8.2 %copy-start.4 = (bf16[3,3,96,32]{2,3,1,0:T(8,128)(2,1)S(1)}, bf16[3,3,96,32]{2,3,1,0:T(8,128)(2,1)}, u32[]{:S(2)}) copy-start(bf16[3,3,96,32]{2,3,1,0:T(8,128)(2,1)} %param.30) | copy-start | bytes 165892
  17.3 8.2 %copy-start.7 = (bf16[32,48]{1,0:T(8,128)(2,1)S(1)}, bf16[32,48]{1,0:T(8,128)(2,1)}, u32[]{:S(2)}) copy-start(bf16[32,48]{1,0:T(8,128)(2,1)} %hk.1) | copy-start | bytes 9220
  17.4 8.2 %copy-start.8 = (f32[256]{0:T(256)S(1)}, f32[256]{0:T(256)}, u32[]{:S(2)}) copy-start(f32[256]{0:T(256)} %param.25) | copy-start | bytes 3076
  17.4 8.2 %copy-start.12 = (f32[128]{0:T(128)S(1)}, f32[128]{0:T(128)}, u32[]{:S(2)}) copy-start(f32[128]{0:T(128)} %param.27) | copy-start | bytes 1540
  17.4 8.2 %copy-start.13 = (f32[64]{0:T(128)S(1)}, f32[64]{0:T(128)}, u32[]{:S(2)}) copy-start(f32[64]{0:T(128)} %param.29) | copy-start | bytes 772
  17.4 8.2 %copy-start.14 = (f32[32]{0:T(128)S(1)}, f32[32]{0:T(128)}, u32[]{:S(2)}) copy-start(f32[32]{0:T(128)} %param.31) | copy-start | bytes 388
  17.4 8.2 %copy-start.15 = (f32[48]{0:T(128)S(1)}, f32[48]{0:T(128)}, u32[]{:S(2)}) copy-start(f32[48]{0:T(128)} %param.33) | copy-start | bytes 580
  19.7 9.2 %collective-permute-start.4 = (bf16[27,32,128]{2,1,0:T(8,128)(2,1)S(1)}, bf16[27,32,128]{2,1,0:T(8,128)(2,1)S(1)}, u32[]{:S(2)}, u32[]{:S(2)}) collective-permute-start(bf16[27,32,128]{2,1,0:T(8,128)(2,1)S(1)} %get-tuple-element.69), channel_id=1, source_target_pairs={{0,8},{8,0},{16,24},{24,16},{32,40},{40,32},{48,56},{56,48},{64,72... | collective-permute-start | bytes 663560 | tf_op jit(solution)/shard_map/ppermute | solution.py:18
  19.8 11.5 %collective-permute-start.5 = (bf16[27,32,128]{2,1,0:T(8,128)(2,1)S(1)}, bf16[27,32,128]{2,1,0:T(8,128)(2,1)S(1)}, u32[]{:S(2)}, u32[]{:S(2)}) collective-permute-start(bf16[27,32,128]{2,1,0:T(8,128)(2,1)S(1)} %get-tuple-element.70), channel_id=1, source_target_pairs={{0,120},{8,16},{16,8},{24,32},{32,24},{40,48},{48,40},{56,64},{64,... | collective-permute-start | bytes 663560 | tf_op jit(solution)/shard_map/ppermute | solution.py:18
  32.8 9.2 %collective-permute-start.6 = (bf16[9,64,128]{2,1,0:T(8,128)(2,1)S(1)}, bf16[9,64,128]{2,1,0:T(8,128)(2,1)S(1)}, u32[]{:S(2)}, u32[]{:S(2)}) collective-permute-start(bf16[9,64,128]{2,1,0:T(8,128)(2,1)S(1)} %get-tuple-element.78), channel_id=1, source_target_pairs={{0,8},{8,0},{16,24},{24,16},{32,40},{40,32},{48,56},{56,48},{64,72... | collective-permute-start | bytes 442376 | tf_op jit(solution)/shard_map/ppermute | solution.py:18
  32.8 9.1 %collective-permute-start.7 = (bf16[9,64,128]{2,1,0:T(8,128)(2,1)S(1)}, bf16[9,64,128]{2,1,0:T(8,128)(2,1)S(1)}, u32[]{:S(2)}, u32[]{:S(2)}) collective-permute-start(bf16[9,64,128]{2,1,0:T(8,128)(2,1)S(1)} %get-tuple-element.79), channel_id=1, source_target_pairs={{0,120},{8,16},{16,8},{24,32},{32,24},{40,48},{48,40},{56,64},{64,... | collective-permute-start | bytes 442376 | tf_op jit(solution)/shard_map/ppermute | solution.py:18
  40.1 8.4 %collective-permute-start.10 = (bf16[18,32,128]{2,1,0:T(8,128)(2,1)S(1)}, bf16[18,32,128]{2,1,0:T(8,128)(2,1)S(1)}, u32[]{:S(2)}, u32[]{:S(2)}) collective-permute-start(bf16[18,32,128]{2,1,0:T(8,128)(2,1)S(1)} %get-tuple-element.95), channel_id=1, source_target_pairs={{0,8},{8,0},{16,24},{24,16},{32,40},{40,32},{48,56},{56,48},{64,72... | collective-permute-start | bytes 442376 | tf_op jit(solution)/shard_map/ppermute | solution.py:18
  40.2 8.9 %collective-permute-start.11 = (bf16[18,32,128]{2,1,0:T(8,128)(2,1)S(1)}, bf16[18,32,128]{2,1,0:T(8,128)(2,1)S(1)}, u32[]{:S(2)}, u32[]{:S(2)}) collective-permute-start(bf16[18,32,128]{2,1,0:T(8,128)(2,1)S(1)} %get-tuple-element.96), channel_id=1, source_target_pairs={{0,120},{8,16},{16,8},{24,32},{32,24},{40,48},{48,40},{56,64},{64,... | collective-permute-start | bytes 442376 | tf_op jit(solution)/shard_map/ppermute | solution.py:18
  43.8 8.5 %collective-permute-start.9 = (bf16[9,64,128]{2,1,0:T(8,128)(2,1)S(1)}, bf16[9,64,128]{2,1,0:T(8,128)(2,1)S(1)}, u32[]{:S(2)}, u32[]{:S(2)}) collective-permute-start(bf16[9,64,128]{2,1,0:T(8,128)(2,1)S(1)} %get-tuple-element.84), channel_id=1, source_target_pairs={{0,120},{8,16},{16,8},{24,32},{32,24},{40,48},{48,40},{56,64},{64,... | collective-permute-start | bytes 442376 | tf_op jit(solution)/shard_map/ppermute | solution.py:18
  48.5 5.1 %collective-permute-start.8 = (bf16[9,64,128]{2,1,0:T(8,128)(2,1)S(1)}, bf16[9,64,128]{2,1,0:T(8,128)(2,1)S(1)}, u32[]{:S(2)}, u32[]{:S(2)}) collective-permute-start(bf16[9,64,128]{2,1,0:T(8,128)(2,1)S(1)} %get-tuple-element.84), channel_id=1, source_target_pairs={{0,8},{8,0},{16,24},{24,16},{32,40},{40,32},{48,56},{56,48},{64,72... | collective-permute-start | bytes 442376 | tf_op jit(solution)/shard_map/ppermute | solution.py:18
